TPU v7x, 512 devices: a 4x2x32 block of a 4x8x32 slice. The times are simulated.
512 devices in a mesh: img: 2 (over y), row: 128 (over x, z), col: 2 (over core).
Axes of the slice: x: 4, y: 2, z: 32, core: 2. Of those that a mesh axis runs over, the one named last changes fastest.
The devices are a block of a 4x8x32 slice.
Arguments:
- features: bfloat16 [256, 128, 512], P(('img', 'row'), 'col'), parts along dimension 0, may hold values from -60 to 60
- first_gain: float32 [512], replicated, may hold values from 0.1 to 1.9
- first_shift: float32 [512], replicated, may hold values from -2.5 to 2.5
- first_weight: bfloat16 [3, 3, 512, 512], P(None, None, 'row'), may hold values from -0.09375 to 0.09375
- first_bias: float32 [512], replicated, may hold values from -2.5 to 2.5
- second_gain: float32 [512], replicated, may hold values from 0.1 to 1.9
- second_shift: float32 [512], replicated, may hold values from -2.5 to 2.5
- second_weight: bfloat16 [3, 3, 512, 512], P(None, None, 'row'), may hold values from -0.09375 to 0.09375
- second_bias: float32 [512], replicated, may hold values from -2.5 to 2.5
- upsample_weight: bfloat16 [3, 3, 512, 512], P(None, None, 'row'), may hold values from -0.09375 to 0.09375
- upsample_bias: float32 [512], replicated, may hold values from -2.5 to 2.5
Outputs:
- upsampled: bfloat16 [512, 256, 512], P(('img', 'row'), 'col'), parts along dimension 0
There are 2 independent parts, one for each index of `img`. A program takes and returns all parts, laid end to end along the dimension named above; an argument that names none is the same for every part. Nothing has to cross between parts.
All inputs are finite; a program needn't handle non-finite values.
Results may differ from a plain program's by a relative error of at most 0.0075.
Values may be sent and summed in bfloat16 or wider, within the bound.
No kernel may reach another device: no remote copies, remote signals or barrier semaphores. Data moves between devices by JAX's collectives and lax.ppermute only.
A program may use at most 128 MiB of HBM per device.

v0:
```python
import functools

import jax
import jax.numpy as jnp
from jax import lax
from jax.sharding import Mesh
from jax.sharding import PartitionSpec as P

G = 32
ROW_COL = ("row_0", "row_1", "col")
ROW = ("row_0", "row_1")
IMG_ROW = ("img", "row_0", "row_1")


EPS = 1e-06


def over_axes(x, axes):
    return functools.reduce(lax.psum, axes, x)


def extended(cells, sides, width):
    for axis, dim in sides:
        count = lax.axis_size(axis)
        ends = count - 1
        head = lax.slice_in_dim(cells, 0, width, axis=dim)
        tail = lax.slice_in_dim(cells, cells.shape[dim] - width, cells.shape[dim], axis=dim)
        cells = jnp.concatenate(
            [
                lax.ppermute(tail, axis, [(i, (i + 1) % count) for i in range(ends)]),
                cells,
                lax.ppermute(head, axis, [((i + 1) % count, i) for i in range(ends)]),
            ],
            axis=dim,
        )
    return cells


def joined_along(parts, dim):
    parts = jnp.moveaxis(parts, 0, dim)
    dims = parts.shape
    return parts.reshape(*dims[:dim], dims[dim] * dims[dim + 1], *dims[dim + 2 :])


def gather_in_order(x, axes, turns):
    parts = x
    for k in turns:
        parts = lax.all_gather(parts, axes[k])
    done = turns[::-1]
    back = [done.index(k) for k in range(len(axes))]
    parts = parts.transpose(*back, *range(len(axes), parts.ndim))
    return parts.reshape(-1, *x.shape)


def gathered_by_axis(x, axes, turns, dim):
    return joined_along(gather_in_order(x, axes, turns), dim)


def norm_silu(values, gain, shift):
    height, breadth, channels = values.shape
    grouped = values.reshape(height * breadth, G, channels // G)
    total = jnp.sum(grouped, axis=(0, 2))
    squares = jnp.sum(grouped * grouped, axis=(0, 2))
    total, squares = (over_axes(total, ROW_COL), over_axes(squares, ROW_COL))
    count = height * breadth * lax.axis_size(ROW) * lax.axis_size("col") * (channels // G)
    mean = total / count
    var = squares / count - mean * mean
    factor = lax.rsqrt(var + EPS)
    normed = (grouped - mean[None, :, None]) * factor[None, :, None]
    normed = normed.reshape(height, breadth, channels) * gain + shift
    return jax.nn.silu(normed).astype(jnp.bfloat16)


def extend(values):
    return extended(values, ((ROW, 0), ("col", 1)), 1)


def convolve(padded, weight, bias, height, breadth):
    outputs = weight.shape[3]
    empty = jnp.zeros((height, breadth, outputs), jnp.float32)
    share = weight.shape[2] // lax.axis_size("col")
    own = lax.dynamic_slice_in_dim(weight, lax.axis_index("col") * share, share, 2)
    total = empty
    piece = gathered_by_axis(own, ROW_COL, (0, 1, 2), 2)
    depth = piece.shape[2]
    offset = jnp.asarray(jnp.int32(0), jnp.int32)
    for offset_y in range(3):
        for offset_x in range(3):
            window = lax.dynamic_slice(
                padded, (jnp.int32(offset_y), jnp.int32(offset_x), offset), (height, breadth, depth)
            )
            total = total + jnp.einsum(
                "hwk,kc->hwc", window, piece[offset_y, offset_x], preferred_element_type=jnp.float32
            )
    return total + bias


def on_device(
    features,
    first_gain,
    first_shift,
    first_weight,
    first_bias,
    second_gain,
    second_shift,
    second_weight,
    second_bias,
    upsample_weight,
    upsample_bias,
):
    height, breadth, channels = features.shape
    normed_one = norm_silu(features.astype(jnp.float32), first_gain, first_shift)
    hidden = convolve(extend(normed_one), first_weight, first_bias, height, breadth).astype(
        jnp.bfloat16
    )
    normed_two = norm_silu(hidden.astype(jnp.float32), second_gain, second_shift)
    block_out = (
        convolve(extend(normed_two), second_weight, second_bias, height, breadth)
        + features.astype(jnp.float32)
    ).astype(jnp.bfloat16)
    doubled = jnp.repeat(jnp.repeat(block_out, 2, axis=0), 2, axis=1)
    padded = extend(doubled)
    return convolve(padded, upsample_weight, upsample_bias, 2 * height, 2 * breadth).astype(
        jnp.bfloat16
    )


def solution(mesh):
    finer = Mesh(
        mesh.devices.reshape(mesh.shape["img"], 4, 32, mesh.shape["col"]),
        ("img", "row_0", "row_1", "col"),
    )
    in_specs = (
        P(IMG_ROW, "col", None),
        P(),
        P(),
        P(None, None, ROW, None),
        P(),
        P(),
        P(),
        P(None, None, ROW, None),
        P(),
        P(None, None, ROW, None),
        P(),
    )
    out_specs = P(IMG_ROW, "col", None)
    return jax.shard_map(
        on_device, mesh=finer, in_specs=in_specs, out_specs=out_specs, check_vma=False
    )
```

profile of v0, /device:TPU:33, one launch (start us, length us, event | category | flops | bytes accessed | tf_op | source)
XLA Modules:
  0.0 729.3 jit_solution(16499633768120713842)
XLA Ops:
  7.3 11.2 %all-gather = bf16[12,3,2,512]{3,2,1,0:T(2,128)(2,1)} all-gather(bf16[3,3,2,512]{3,2,1,0:T(2,128)(2,1)S(1)} %constant_dynamic-slice_fusion.2), channel_id=2, replica_groups=mesh['img'=2,'row_0'=4,'row_1'=32,'col'=2] {'row_0'}, dimensions={0}, use_global_device_ids=true | all-gather | bytes 92160 | tf_op jit(solution)/shard_map/all_gather | solution.py:48
  19.5 9.8 %all-gather.3 = bf16[12,3,2,512]{3,2,1,0:T(2,128)(2,1)} all-gather(bf16[3,3,2,512]{3,2,1,0:T(2,128)(2,1)S(1)} %constant_dynamic-slice_fusion.1), channel_id=5, replica_groups=mesh['img'=2,'row_0'=4,'row_1'=32,'col'=2] {'row_0'}, dimensions={0}, use_global_device_ids=true | all-gather | bytes 92160 | tf_op jit(solution)/shard_map/all_gather | solution.py:48
  30.2 9.8 %all-gather.6 = bf16[12,3,2,512]{3,2,1,0:T(2,128)(2,1)} all-gather(bf16[3,3,2,512]{3,2,1,0:T(2,128)(2,1)S(1)} %constant_dynamic-slice_fusion), channel_id=8, replica_groups=mesh['img'=2,'row_0'=4,'row_1'=32,'col'=2] {'row_0'}, dimensions={0}, use_global_device_ids=true | all-gather | bytes 92160 | tf_op jit(solution)/shard_map/all_gather | solution.py:48
  40.2 122.1 %all-gather.16.cloned.1.call-done = bf16[128,3,3,2,512]{4,3,2,1,0:T(2,128)(2,1)} async-done(((bf16[4,3,3,2,512]{4,3,2,1,0:T(2,128)(2,1)}), bf16[128,3,3,2,512]{4,3,2,1,0:T(2,128)(2,1)}) %all-gather.16.cloned.1.call-update) | async-done | bytes 2359312 | tf_op jit(solution)/shard_map/all_gather | solution.py:48
  166.7 126.1 %all-gather.20.cloned.1.call-done = bf16[128,3,3,2,512]{4,3,2,1,0:T(2,128)(2,1)} async-done(((bf16[4,3,3,2,512]{4,3,2,1,0:T(2,128)(2,1)}), bf16[128,3,3,2,512]{4,3,2,1,0:T(2,128)(2,1)}) %all-gather.20.cloned.1.call-update) | async-done | bytes 2359312 | tf_op jit(solution)/shard_map/all_gather | solution.py:48
  292.8 4.3 copy.34
  297.2 126.0 %all-gather.24.cloned.1.call-done = bf16[128,3,3,2,512]{4,3,2,1,0:T(2,128)(2,1)} async-done(((bf16[4,3,3,2,512]{4,3,2,1,0:T(2,128)(2,1)}), bf16[128,3,3,2,512]{4,3,2,1,0:T(2,128)(2,1)}) %all-gather.24.cloned.1.call-update) | async-done | bytes 2359312 | tf_op jit(solution)/shard_map/all_gather | solution.py:48
  428.0 8.8 %all-reduce.3 = (f32[32]{0:T(128)S(1)}, f32[32]{0:T(128)S(1)}) all-reduce(f32[32]{0:T(128)S(1)} %reduce_sum.54, f32[32]{0:T(128)S(1)} %reduce_sum.51), channel_id=1, replica_groups=mesh['img'=2,'row_0'=4,'row_1'=32,'col'=2] {'row_0'}, use_global_device_ids=true, to_apply=%region_7.0 | all-reduce | flops 64 | bytes 512 | tf_op jit(solution)/shard_map/psum | solution.py:19
  436.9 39.8 %all-reduce.1 = (f32[32]{0:T(128)S(1)}, f32[32]{0:T(128)S(1)}) all-reduce(f32[32]{0:T(128)S(1)} %get-tuple-element.15, f32[32]{0:T(128)S(1)} %get-tuple-element.16), channel_id=1, replica_groups=mesh['img'=2,'row_0'=4,'row_1'=32,'col'=2] {'row_1'}, use_global_device_ids=true, to_apply=%region_8.9 | all-reduce | flops 64 | bytes 512 | tf_op jit(solution)/shard_map/psum | solution.py:19
  476.7 39.6 %all-reduce.5 = (f32[32]{0:T(128)S(1)}, f32[32]{0:T(128)S(1)}) all-reduce(f32[32]{0:T(128)S(1)} %get-tuple-element.11, f32[32]{0:T(128)S(1)} %get-tuple-element.12), channel_id=1, replica_groups=mesh['img'=2,'row_0'=4,'row_1'=32,'col'=2] {'col'}, use_global_device_ids=true, to_apply=%region_9.10 | all-reduce | flops 64 | bytes 512 | tf_op jit(solution)/shard_map/psum | solution.py:19
  528.9 6.1 copy.31
  535.0 10.1 %copy.42 = bf16[4,32,2,3,3,2,512]{6,5,2,1,0,4,3:T(2,128)(2,1)} copy(bf16[4,32,2,3,3,2,512]{6,1,2,5,4,3,0:T(8,128)(2,1)} %bitcast.191) | data formatting | bytes 9437184 | tf_op jit(solution)/shard_map/transpose | solution.py:40
  545.1 8.1 %reshape.252 = bf16[3,3,512,512]{3,2,1,0:T(8,128)(2,1)} reshape(bf16[3,3,256,2,512]{4,3,2,1,0:T(2,128)(2,1)} %bitcast.192) | data formatting | bytes 9437184 | tf_op jit(solution)/shard_map/reshape | solution.py:42
  565.0 6.6 all-reduce.2
  571.6 42.8 %all-reduce = (f32[32]{0:T(128)S(1)}, f32[32]{0:T(128)S(1)}) all-reduce(f32[32]{0:T(128)S(1)} %get-tuple-element.13, f32[32]{0:T(128)S(1)} %get-tuple-element.14), channel_id=1, replica_groups=mesh['img'=2,'row_0'=4,'row_1'=32,'col'=2] {'row_1'}, use_global_device_ids=true, to_apply=%region_18.19 | all-reduce | flops 64 | bytes 512 | tf_op jit(solution)/shard_map/psum | solution.py:19
  614.4 19.4 %all-reduce.4 = (f32[32]{0:T(128)S(1)}, f32[32]{0:T(128)S(1)}) all-reduce(f32[32]{0:T(128)S(1)} %get-tuple-element.9, f32[32]{0:T(128)S(1)} %get-tuple-element.10), channel_id=1, replica_groups=mesh['img'=2,'row_0'=4,'row_1'=32,'col'=2] {'col'}, use_global_device_ids=true, to_apply=%region_19.20 | all-reduce | flops 64 | bytes 512 | tf_op jit(solution)/shard_map/psum | solution.py:19
  637.0 6.2 copy.35
  643.2 9.4 %copy.43 = bf16[4,32,2,3,3,2,512]{6,5,2,1,0,4,3:T(2,128)(2,1)} copy(bf16[4,32,2,3,3,2,512]{6,1,2,5,4,3,0:T(8,128)(2,1)} %bitcast.193) | data formatting | bytes 9437184 | tf_op jit(solution)/shard_map/transpose | solution.py:40
  652.6 8.1 %reshape.263 = bf16[3,3,512,512]{3,2,1,0:T(8,128)(2,1)} reshape(bf16[3,3,256,2,512]{4,3,2,1,0:T(2,128)(2,1)} %bitcast.194) | data formatting | bytes 9437184 | tf_op jit(solution)/shard_map/reshape | solution.py:42
  661.9 6.2 copy.39
  668.1 9.4 %copy.44 = bf16[4,32,2,3,3,2,512]{6,5,2,1,0,4,3:T(2,128)(2,1)} copy(bf16[4,32,2,3,3,2,512]{6,1,2,5,4,3,0:T(8,128)(2,1)} %bitcast.195) | data formatting | bytes 9437184 | tf_op jit(solution)/shard_map/transpose | solution.py:40
  677.5 8.1 %reshape.272 = bf16[3,3,512,512]{3,2,1,0:T(8,128)(2,1)} reshape(bf16[3,3,256,2,512]{4,3,2,1,0:T(2,128)(2,1)} %bitcast.196) | data formatting | bytes 9437184 | tf_op jit(solution)/shard_map/reshape | solution.py:42
  699.6 4.6 collective-permute-start.8
  711.3 4.5 collective-permute-start.11
  (123 shorter events, 68.3 us)
Async XLA Ops:
  6.6 155.7 %all-gather.16.cloned.1.call-start = ((), (), s32[]{:S(2)}) async-start(), calls=%async_computation | async-start | bytes 2433024 | tf_op jit(solution)/shard_map/all_gather | solution.py:48
  18.6 274.1 %all-gather.20.cloned.1.call-start = ((), (), s32[]{:S(2)}) async-start(), calls=%async_computation.2 | async-start | bytes 2433024 | tf_op jit(solution)/shard_map/all_gather | solution.py:48
  29.4 393.9 %all-gather.24.cloned.1.call-start = ((), (), s32[]{:S(2)}) async-start(), calls=%async_computation.4 | async-start | bytes 2433024 | tf_op jit(solution)/shard_map/all_gather | solution.py:48
  40.1 488.9 %all-gather.18.cloned.1.call-start = ((), (), s32[]{:S(2)}) async-start(), calls=%async_computation.1 | async-start | bytes 7077888 | tf_op jit(solution)/shard_map/all_gather | solution.py:48
  166.6 470.4 %all-gather.22.cloned.1.call-start = ((), (), s32[]{:S(2)}) async-start(), calls=%async_computation.3 | async-start | bytes 7077888 | tf_op jit(solution)/shard_map/all_gather | solution.py:48
  297.1 130.5 %copy-start.2 = (bf16[1,64,512]{2,1,0:T(8,128)(2,1)S(1)}, bf16[1,64,512]{2,1,0:T(8,128)(2,1)}, u32[]{:S(2)}) copy-start(bf16[1,64,512]{2,1,0:T(8,128)(2,1)} %param.11) | copy-start | bytes 196612
  297.1 219.5 %copy-start.3 = (f32[512]{0:T(512)S(1)}, f32[512]{0:T(512)}, u32[]{:S(2)}) copy-start(f32[512]{0:T(512)} %param.13) | copy-start | bytes 6148
  297.1 219.5 %copy-start.4 = (f32[512]{0:T(512)S(1)}, f32[512]{0:T(512)}, u32[]{:S(2)}) copy-start(f32[512]{0:T(512)} %param.12) | copy-start | bytes 6148
  297.1 364.8 %all-gather.26.cloned.1.call-start = ((), (), s32[]{:S(2)}) async-start(), calls=%async_computation.5 | async-start | bytes 7077888 | tf_op jit(solution)/shard_map/all_gather | solution.py:48
  516.6 3.3 collective-permute-start
  518.6 5.0 collective-permute-start.1
  523.7 29.5 %collective-permute-start.3 = (bf16[3,1,512]{2,1,0:T(2,128)(2,1)S(1)}, bf16[3,1,512]{2,1,0:T(2,128)(2,1)S(1)}, u32[]{:S(2)}, u32[]{:S(2)}) collective-permute-start(bf16[3,1,512]{2,1,0:T(2,128)(2,1)S(1)} %get-tuple-element.28), channel_id=1, source_target_pairs={{1,0},{3,2},{5,4},{7,6},{9,8},{11,10},{13,12},{15,14},{17,16},{19,... | collective-permute-start | bytes 9224 | tf_op jit(solution)/shard_map/ppermute | solution.py:32
  527.4 28.3 %collective-permute-start.2 = (bf16[3,1,512]{2,1,0:T(2,128)(2,1)S(1)}, bf16[3,1,512]{2,1,0:T(2,128)(2,1)S(1)}, u32[]{:S(2)}, u32[]{:S(2)}) collective-permute-start(bf16[3,1,512]{2,1,0:T(2,128)(2,1)S(1)} %get-tuple-element.27), channel_id=1, source_target_pairs={{0,1},{2,3},{4,5},{6,7},{8,9},{10,11},{12,13},{14,15},{16,17},{18,... | collective-permute-start | bytes 9224 | tf_op jit(solution)/shard_map/ppermute | solution.py:30
  553.2 80.9 %copy-start.6 = (f32[512]{0:T(512)S(1)}, f32[512]{0:T(512)}, u32[]{:S(2)}) copy-start(f32[512]{0:T(512)} %param.17) | copy-start | bytes 6148
  553.2 80.9 %copy-start.7 = (f32[512]{0:T(512)S(1)}, f32[512]{0:T(512)}, u32[]{:S(2)}) copy-start(f32[512]{0:T(512)} %param.16) | copy-start | bytes 6148
  634.2 51.4 %collective-permute-start.4 = (bf16[1,64,512]{2,1,0:T(8,128)(2,1)S(1)}, bf16[1,64,512]{2,1,0:T(8,128)(2,1)S(1)}, u32[]{:S(2)}, u32[]{:S(2)}) collective-permute-start(bf16[1,64,512]{2,1,0:T(8,128)(2,1)S(1)} %fusion.153), channel_id=1, source_target_pairs={{0,2},{2,4},{4,6},{6,8},{8,10},{10,12},{12,14},{14,16},{16,18},{18... | collective-permute-start | bytes 196616 | tf_op jit(solution)/shard_map/ppermute | solution.py:30
  635.5 50.1 %collective-permute-start.5 = (bf16[1,64,512]{2,1,0:T(8,128)(2,1)S(1)}, bf16[1,64,512]{2,1,0:T(8,128)(2,1)S(1)}, u32[]{:S(2)}, u32[]{:S(2)}) collective-permute-start(bf16[1,64,512]{2,1,0:T(8,128)(2,1)S(1)} %fusion.153), channel_id=1, source_target_pairs={{2,0},{4,2},{6,4},{8,6},{10,8},{12,10},{14,12},{16,14},{18,16},{20... | collective-permute-start | bytes 196616 | tf_op jit(solution)/shard_map/ppermute | solution.py:32
  685.6 8.7 %collective-permute-start.7 = (bf16[3,1,512]{2,1,0:T(2,128)(2,1)S(1)}, bf16[3,1,512]{2,1,0:T(2,128)(2,1)S(1)}, u32[]{:S(2)}, u32[]{:S(2)}) collective-permute-start(bf16[3,1,512]{2,1,0:T(2,128)(2,1)S(1)} %get-tuple-element.26), channel_id=1, source_target_pairs={{1,0},{3,2},{5,4},{7,6},{9,8},{11,10},{13,12},{15,14},{17,16},{19,... | collective-permute-start | bytes 9224 | tf_op jit(solution)/shard_map/ppermute | solution.py:32
  687.9 3.8 collective-permute-start.6
  693.0 27.1 %slice-start = ((s8[4718592]{0:T(1024)(128)(4,1)}), s8[524288]{0:T(1024)(128)(4,1)S(1)}, s32[]{:S(2)}) async-start(s8[4718592]{0:T(1024)(128)(4,1)} %bitcast.197), calls=%async_computation.6 | async-start | bytes 1048576
  699.6 7.2 collective-permute-start.8
  704.2 5.7 collective-permute-start.9
  710.0 8.5 %collective-permute-start.10 = (bf16[4,1,512]{2,1,0:T(2,128)(2,1)S(1)}, bf16[4,1,512]{2,1,0:T(2,128)(2,1)S(1)}, u32[]{:S(2)}, u32[]{:S(2)}) collective-permute-start(bf16[4,1,512]{2,1,0:T(2,128)(2,1)S(1)} %get-tuple-element.23), channel_id=1, source_target_pairs={{0,1},{2,3},{4,5},{6,7},{8,9},{10,11},{12,13},{14,15},{16,17},{18,... | collective-permute-start | bytes 12296 | tf_op jit(solution)/shard_map/ppermute | solution.py:30
  711.3 7.2 collective-permute-start.11
  (6 other events, 48.9 us)
Sparse Core Ops, SparseCore 0:
  18.7 143.4 all-gather.15
  164.3 128.3 all-gather.19
  294.9 128.3 all-gather.23
  425.2 47.7 all-gather.17
  474.9 34.9 all-gather.21
  511.9 34.9 all-gather.25
where the time goes:
time: 735 us; the launch traced here: 729 us
  waiting for transfers between devices  381 us (52%)
  blocking collectives  188 us (26%)
  local copies, waits for them, and re-layouts  87.9 us (12%)
  matrix products  30.2 us (4%)
  starting transfers between devices  27 us (4%)
  between operations  14.1 us (2%)
    all_gather x6, waiting for transfers between devices, gather_in_order(): parts = lax.all_gather(parts, axes[k])  374 us
    psum x6, blocking collectives, over_axes(): return functools.reduce(lax.psum, axes, x)  157 us
    all_gather x6, local copies, waits for them, and re-layouts, gather_in_order(): parts = lax.all_gather(parts, axes[k])  31.3 us
    all_gather x3, blocking collectives, gather_in_order(): parts = lax.all_gather(parts, axes[k])  30.8 us
    dot_general x27, matrix products, convolve(): jnp.einsum('hwk,kc->hwc', window, piece[offset_y, offset_x], preferred_el...  30.2 us
    transpose x3, local copies, waits for them, and re-layouts, joined_along(): parts = jnp.moveaxis(parts, 0, dim)  28.9 us
    reshape x3, local copies, waits for them, and re-layouts, joined_along(): parts.reshape(*dims[:dim], dims[dim] * dims[dim + 1], *dims[dim + 2:])  24.2 us
  transfers between devices with their start and end apart: 18, of which 5 were waited for; matrix products, arithmetic and copies ran while one was open for 15% of the time, Pallas kernels for 0%

commit v1 on v0

v1 whole, which is shorter than its diff:
```python
import functools

import jax
import jax.numpy as jnp
from jax import lax
from jax.experimental import pallas as pl
from jax.experimental.pallas import tpu as pltpu
from jax.sharding import Mesh
from jax.sharding import PartitionSpec as P

G = 32
EPS = 1e-06
F32, BF16 = jnp.float32, jnp.bfloat16
HIGHEST = lax.Precision.HIGHEST
ROW = ("x", "z")
IMG_ROW = ("img", "x", "z")


def sum_over(vector, axes):
    count = lax.axis_size(axes)
    sent = jnp.broadcast_to(vector, (count, vector.shape[1]))
    return lax.all_to_all(sent, axes, 0, 0, tiled=True)


def shifted_rows(values, axis, by):
    count = lax.axis_size(axis)
    pairs = [(i, i - by) for i in range(count) if 0 <= i - by < count]
    return lax.ppermute(values, axis, pairs)


def put_shifted(S, row, cols, y, lanes):
    at = pl.ds(row * cols, cols)
    column = lax.broadcasted_iota(jnp.int32, y.shape, 0)
    S[1, at, lanes] = y.astype(BF16)
    S[0, at, lanes] = jnp.where(column == 0, 0.0, pltpu.roll(y, 1, 0)).astype(BF16)
    S[2, at, lanes] = jnp.where(column == cols - 1, 0.0, pltpu.roll(y, cols - 1, 0)).astype(BF16)


def silu(u):
    return u / (1.0 + jnp.exp(-u))


def conv_one_kernel(cols, rows, image_rows, at_ref, x_ref, a_ref, b_ref, bias_ref, pick_ref, w_ref, out_ref, sums_ref, S, acc):
    t = pl.program_id(0)
    first = at_ref[0] - 3
    outs = acc.shape[1]

    @pl.when(t == 0)
    def _():
        for i in range(rows + 2):
            x = x_ref[pl.ds(i * cols, cols), :].astype(F32)
            y = silu(x * a_ref[...] + b_ref[...])
            inside = jnp.logical_and(first + i >= 0, first + i < image_rows)
            y = jnp.where(inside, y, 0.0)
            put_shifted(S, i, cols, y, slice(None))
        acc[...] = jnp.broadcast_to(bias_ref[...], acc.shape)

    start = pl.multiple_of((t // 3) * cols, cols)
    piece = w_ref[...].reshape(-1, outs)
    acc[...] += jnp.dot(S[t % 3, pl.ds(start, rows * cols), :], piece, preferred_element_type=F32)

    @pl.when(t == 8)
    def _():
        hidden = acc[...].astype(BF16)
        out_ref[...] = hidden
        mid = rows // 2
        own = hidden[mid * cols : (mid + 1) * cols].astype(F32)
        both = jnp.concatenate(
            [jnp.sum(own, axis=0, keepdims=True), jnp.sum(own * own, axis=0, keepdims=True)], axis=1
        )
        both = jnp.broadcast_to(both, (8, 2 * outs))
        sums_ref[...] = jnp.dot(both, pick_ref[...], precision=HIGHEST, preferred_element_type=F32)


def norm_kernel(cols, rows, image_rows, count, groups, at_ref, x_ref, stats_ref, gain_ref, shift_ref, pick_ref, out_ref):
    totals = jnp.sum(stats_ref[...], axis=0, keepdims=True)
    totals = jnp.broadcast_to(totals, (8, totals.shape[1]))
    spread = lax.dot_general(
        totals, pick_ref[...], (((1,), (1,)), ((), ())), precision=HIGHEST, preferred_element_type=F32
    )
    outs = gain_ref.shape[1]
    mean = spread[:1, :outs] / count
    var = spread[:1, outs:] / count - mean * mean
    a = lax.rsqrt(var + EPS) * gain_ref[...]
    b = shift_ref[...] - mean * a
    first = at_ref[0] - rows // 2
    for i in range(rows):
        at = pl.ds(i * cols, cols)
        y = silu(x_ref[at, :].astype(F32) * a + b)
        inside = jnp.logical_and(first + i >= 0, first + i < image_rows)
        out_ref[at, :] = jnp.where(inside, y, 0.0).astype(BF16)


def conv_two_kernel(cols, rows, image_rows, at_ref, x_ref, res_ref, bias_ref, w_ref, out_ref, S, acc):
    t = pl.program_id(0)
    outs = acc.shape[1]

    @pl.when(t == 0)
    def _():
        for i in range(rows + 2):
            for h in range(2):
                y = x_ref[h, pl.ds(i * cols, cols), :].astype(F32)
                put_shifted(S, i, cols, y, slice(h * outs, (h + 1) * outs))
        acc[...] = jnp.broadcast_to(bias_ref[...], acc.shape)

    start = pl.multiple_of((t // 3) * cols, cols)
    piece = w_ref[...].reshape(-1, outs)
    acc[...] += jnp.dot(S[t % 3, pl.ds(start, rows * cols), :], piece, preferred_element_type=F32)

    @pl.when(t == 8)
    def _():
        first = at_ref[0] - rows // 2
        for i in range(rows):
            at = pl.ds(i * cols, cols)
            y = acc[at, :] + res_ref[at, :].astype(F32)
            inside = jnp.logical_and(first + i >= 0, first + i < image_rows)
            out_ref[at, :] = jnp.where(inside, y, 0.0).astype(BF16)


def conv_up_kernel(cols, x_ref, bias_ref, w_ref, out_ref, S, acc, full):
    t = pl.program_id(0)
    outs = acc.shape[2]

    @pl.when(t == 0)
    def _():
        for i in range(3):
            for h in range(2):
                y = x_ref[h, pl.ds(i * cols, cols), :].astype(F32)
                put_shifted(S, i, cols, y, slice(h * outs, (h + 1) * outs))
        acc[...] = jnp.broadcast_to(bias_ref[...][None], acc.shape)

    a, c = t // 3, t % 3
    piece = w_ref[...].reshape(-1, outs)
    for p in range(2):
        for q in range(2):
            start = pl.multiple_of(((a + 1 + p) // 2) * cols, cols)
            acc[2 * p + q] += jnp.dot(
                S[(c + 1 + q) // 2, pl.ds(start, cols), :], piece, preferred_element_type=F32
            )

    @pl.when(t == 8)
    def _():
        for p in range(2):
            for q in range(2):
                for k in range(2):
                    lanes = slice(k * 128, (k + 1) * 128)
                    full[p, k, pl.ds(q, cols, stride=2), :] = acc[2 * p + q][:, lanes]
            for k in range(2):
                for half in range(2):
                    out_ref[half, p, :, k * 128 : (k + 1) * 128] = full[
                        p, k, half * cols : (half + 1) * cols, :
                    ].astype(BF16)


VM = pl.BlockSpec(memory_space=pltpu.VMEM)
SM = pl.BlockSpec(memory_space=pltpu.SMEM)


def weight_spec(gathered, base):
    n, _, rows, outs = gathered.shape
    return pl.BlockSpec((n, 1, rows, outs), lambda t: (0, base + t, 0, 0))


def on_device(
    features,
    first_gain,
    first_shift,
    first_weight,
    first_bias,
    second_gain,
    second_shift,
    second_weight,
    second_bias,
    upsample_weight,
    upsample_bias,
):
    _, breadth, channels = features.shape
    nx, nz, ncol = lax.axis_size("x"), lax.axis_size("z"), lax.axis_size("col")
    k_own = first_weight.shape[2]
    cols = breadth * ncol
    half = channels // ncol
    image_rows = nx * nz
    per_group = channels // G
    count = image_rows * cols * per_group
    c = lax.axis_index("col")
    at = (lax.axis_index("x") * nz + lax.axis_index("z")).astype(jnp.int32)[None]

    def reorder(v):
        return v.reshape(-1, nx, nz, k_own).transpose(0, 2, 1, 3).reshape(-1, channels)

    natural = lax.broadcasted_iota(jnp.int32, (channels, channels), 0)
    place = lax.broadcasted_iota(jnp.int32, (channels, channels), 1)
    source = (place // k_own) % nx * (nz * k_own) + place // (k_own * nx) * k_own + place % k_own
    move = (natural == source).astype(BF16)

    def moved(v):
        return jnp.dot(v, move, preferred_element_type=F32).astype(BF16)

    def own_half(v):
        return lax.dynamic_slice_in_dim(v, c * half, half, v.ndim - 1)

    taps = 9 * k_own
    hold = moved(
        jnp.concatenate([first_weight.reshape(taps, channels), second_weight.reshape(taps, channels)])
    )
    hold = jnp.concatenate([hold, upsample_weight.reshape(taps, channels)])
    hold = own_half(hold).reshape(1, 27, k_own, half)
    hold = lax.all_to_all(jnp.broadcast_to(hold, (nx, 27, k_own, half)), "x", 0, 0, tiled=True)
    hold = hold.transpose(1, 0, 2, 3).reshape(27, nx * k_own, half)
    weights = lax.all_gather(hold, "z")

    own = features[0]
    own_moved = moved(own)
    ext = jnp.stack(
        [shifted_rows(own_moved, ROW, d) if d else own_moved for d in range(-3, 4)]
    )
    ext = lax.all_gather(ext, "col", axis=1, tiled=True).reshape(7 * cols, channels)

    wide = own.astype(F32)
    chan = lax.broadcasted_iota(jnp.int32, (channels, G), 0) // per_group
    member = (chan == lax.broadcasted_iota(jnp.int32, (channels, G), 1)).astype(F32)
    sums = jnp.stack([jnp.sum(wide, axis=0), jnp.sum(wide * wide, axis=0)])
    sums = jnp.dot(sums, member, precision=HIGHEST).reshape(1, 2 * G)
    sums = jnp.pad(sums, ((0, 0), (0, 128 - 2 * G)))
    sums = jnp.sum(sum_over(sums, ("x", "col")), axis=0, keepdims=True)
    sums = jnp.sum(sum_over(sums, "z"), axis=0)
    mean = sums[:G] / count
    var = sums[G : 2 * G] / count - mean * mean
    factor = lax.rsqrt(var + EPS)
    both = jnp.repeat(jnp.stack([mean, factor]), per_group, axis=1)
    a = both[1] * first_gain
    b = first_shift - both[0] * a
    ab = reorder(jnp.stack([a, b]))

    vectors = reorder(jnp.stack([first_bias, second_gain, second_shift, second_bias]))
    vectors = own_half(jnp.concatenate([vectors, upsample_bias[None]]))
    bias_one, gain_two, shift_two, bias_two, bias_up = [vectors[i : i + 1] for i in range(5)]

    groups = G // ncol
    lane = jnp.arange(half)
    group = lane // (per_group // k_own * nx * k_own) * nx + lane // k_own % nx
    pick = group[:, None] == jnp.arange(128)[None, :]
    pick = jnp.concatenate([pick, jnp.roll(pick, groups, axis=1)]).astype(F32)

    rows = 5
    hidden, sums_two = pl.pallas_call(
        functools.partial(conv_one_kernel, cols, rows, image_rows),
        grid=(9,),
        out_shape=(
            jax.ShapeDtypeStruct((rows * cols, half), BF16),
            jax.ShapeDtypeStruct((8, 128), F32),
        ),
        in_specs=[SM, VM, VM, VM, VM, VM, weight_spec(weights, 0)],
        out_specs=(VM, VM),
        scratch_shapes=[
            pltpu.VMEM((3, (rows + 2) * cols, channels), BF16),
            pltpu.VMEM((rows * cols, half), F32),
        ],
        name="conv_one",
    )(at, ext, ab[:1], ab[1:], bias_one, pick, weights)

    stats = sum_over(sums_two[:1], ROW)
    normed = pl.pallas_call(
        functools.partial(norm_kernel, cols, rows, image_rows, count, groups),
        out_shape=jax.ShapeDtypeStruct((rows * cols, half), BF16),
        in_specs=[SM, VM, VM, VM, VM, VM],
        out_specs=VM,
        name="norm_two",
    )(at, hidden, stats, gain_two, shift_two, pick)
    normed = lax.all_gather(normed, "col")

    rows = 3
    residual = own_half(ext[2 * cols : 5 * cols])
    block = pl.pallas_call(
        functools.partial(conv_two_kernel, cols, rows, image_rows),
        grid=(9,),
        out_shape=jax.ShapeDtypeStruct((rows * cols, half), BF16),
        in_specs=[SM, VM, VM, VM, weight_spec(weights, 9)],
        out_specs=VM,
        scratch_shapes=[
            pltpu.VMEM((3, (rows + 2) * cols, channels), BF16),
            pltpu.VMEM((rows * cols, half), F32),
        ],
        name="conv_two",
    )(at, normed, residual, bias_two, weights)
    block = lax.all_gather(block, "col")

    up = pl.pallas_call(
        functools.partial(conv_up_kernel, cols),
        grid=(9,),
        out_shape=jax.ShapeDtypeStruct((ncol, 2, cols, half), BF16),
        in_specs=[VM, VM, weight_spec(weights, 18)],
        out_specs=VM,
        scratch_shapes=[
            pltpu.VMEM((3, 3 * cols, channels), BF16),
            pltpu.VMEM((4, cols, half), F32),
            pltpu.VMEM((2, 2, 2 * cols, 128), F32),
        ],
        name="conv_up",
    )(block, bias_up, weights)
    up = lax.all_to_all(up, "col", 0, 0, tiled=True)
    return up.transpose(1, 2, 0, 3).reshape(2, cols, channels)


def solution(mesh):
    finer = Mesh(
        mesh.devices.reshape(mesh.shape["img"], 4, 32, mesh.shape["col"]),
        ("img", "x", "z", "col"),
    )
    in_specs = (
        P(IMG_ROW, "col", None),
        P(),
        P(),
        P(None, None, ROW, None),
        P(),
        P(),
        P(),
        P(None, None, ROW, None),
        P(),
        P(None, None, ROW, None),
        P(),
    )
    return jax.shard_map(
        on_device,
        mesh=finer,
        in_specs=in_specs,
        out_specs=P(IMG_ROW, "col", None),
        check_vma=False,
    )
```

time: 735 us -> 291 us (0.40)
  waiting for transfers between devices: 381 us -> 91.1 us
  blocking collectives: 188 us -> 48.3 us
  local copies, waits for them, and re-layouts: 87.9 us -> 13.7 us
  starting transfers between devices: 27 us -> 93.6 us
  matrix products: 30.2 us -> 1.06 us
  Pallas kernels: 0 us -> 26.6 us
    all_gather x6 -> x1, waiting for transfers between devices: 374 us -> 56.9 us  [on_device(): weights = lax.all_gather(hold, 'z')]
    psum x6 -> x0, blocking collectives: 157 us -> none  [over_axes(): return functools.reduce(lax.psum, axes, x)]
    all_to_all x0 -> x3, starting transfers between devices: none -> 69.9 us  [sum_over(): return lax.all_to_all(sent, axes, 0, 0, tiled=True)]
    all_to_all x0 -> x3, waiting for transfers between devices: none -> 31.8 us  [sum_over(): return lax.all_to_all(sent, axes, 0, 0, tiled=True)]
    all_gather x6 -> x0, local copies, waits for them, and re-layouts: 31.3 us -> none  [gather_in_order(): parts = lax.all_gather(parts, axes[k])]
    dot_general x27 -> x3, matrix products: 30.2 us -> 1.06 us  [the longest x2 0.64 us: moved(): return jnp.dot(v, move, preferred_element_type=F32).astype(BF16)]
    transpose x3, local copies, waits for them, and re-layouts: 28.9 us -> 0.44 us  [the longest x1 0.19 us: reorder(): v.reshape(-1, nx, nz, k_own).transpose(0, 2, 1, 3).reshape(-1, channels)]
    pallas_call x0 -> x4, Pallas kernels: none -> 26.6 us  [the longest x1 9.12 us: on_device(): pl.pallas_call(functools.partial(conv_one_kernel, cols, rows, image_rows)...]
  transfers between devices with their start and end apart: 18 -> 10, of which waited for: 5 -> 5; matrix products, arithmetic and copies ran while one was open for 15% -> 3% of each run, Pallas kernels for 0% -> 0%
where the time goes in v1:
time: 291 us; the launch traced here: 289 us
  starting transfers between devices  93.6 us (32%)
  waiting for transfers between devices  91.1 us (31%)
  blocking collectives  48.3 us (17%)
  Pallas kernels  26.6 us (9%)
  between operations  13.8 us (5%)
  local copies, waits for them, and re-layouts  13.7 us (5%)
    all_to_all x3, starting transfers between devices, sum_over(): return lax.all_to_all(sent, axes, 0, 0, tiled=True)  69.9 us
    all_gather x1, waiting for transfers between devices, on_device(): weights = lax.all_gather(hold, 'z')  56.9 us
    all_to_all x3, waiting for transfers between devices, sum_over(): return lax.all_to_all(sent, axes, 0, 0, tiled=True)  31.8 us
    all_gather x1, blocking collectives, on_device(): normed = lax.all_gather(normed, 'col')  24.3 us
    ppermute x6, starting transfers between devices, shifted_rows(): return lax.ppermute(values, axis, pairs)  23.7 us
    all_to_all x1, blocking collectives, on_device(): lax.all_to_all(jnp.broadcast_to(hold, (nx, 27, k_own, half)), 'x', 0, 0,...  10.2 us
    pallas_call x1, Pallas kernels, on_device(): pl.pallas_call(functools.partial(conv_one_kernel, cols, rows, image_rows)...  9.12 us
    pallas_call x1, Pallas kernels, on_device(): pl.pallas_call(functools.partial(conv_up_kernel, cols), grid=(9,), out_sh...  7.53 us
  transfers between devices with their start and end apart: 10, of which 5 were waited for; matrix products, arithmetic and copies ran while one was open for 3% of the time, Pallas kernels for 0%

profile of v1, /device:TPU:33, one launch (start us, length us, event | category | flops | bytes accessed | tf_op | source)
XLA Modules:
  0.0 289.4 jit_solution(524432386018788854)
XLA Ops:
  9.5 10.2 %all_to_all.30 = bf16[4,27,4,256]{3,2,1,0:T(4,128)(2,1)S(1)} all-to-all(bf16[4,27,4,256]{3,2,1,0:T(4,128)(2,1)S(1)} %broadcast_in_dim.49), channel_id=1, replica_groups=mesh['img'=2,'x'=4,'z'=32,'col'=2] {'x'}, dimensions={0} | all-to-all | bytes 442368 | tf_op jit(solution)/shard_map/all_to_all | solution.py:208
  21.0 1.3 collective-permute-start.4
  22.3 1.3 collective-permute-start.3
  23.6 1.3 collective-permute-start.5
  24.9 5.1 %collective-permute-start.2 = (bf16[64,512]{1,0:T(8,128)(2,1)S(1)}, bf16[64,512]{1,0:T(8,128)(2,1)S(1)}, u32[]{:S(2)}, u32[]{:S(2)}) collective-permute-start(bf16[64,512]{1,0:T(8,128)(2,1)S(1)} %bitcast.56), channel_id=1, source_target_pairs={{0,2},{2,4},{4,6},{6,8},{8,10},{10,12},{12,14},{14,16},{16,18},{18... | collective-permute-start | bytes 196616 | tf_op jit(solution)/shard_map/ppermute | solution.py:28
  30.0 11.4 %collective-permute-start = (bf16[64,512]{1,0:T(8,128)(2,1)S(1)}, bf16[64,512]{1,0:T(8,128)(2,1)S(1)}, u32[]{:S(2)}, u32[]{:S(2)}) collective-permute-start(bf16[64,512]{1,0:T(8,128)(2,1)S(1)} %bitcast.57), channel_id=1, source_target_pairs={{0,6},{2,8},{4,10},{6,12},{8,14},{10,16},{12,18},{14,20},{16,22},{... | collective-permute-start | bytes 196616 | tf_op jit(solution)/shard_map/ppermute | solution.py:28
  42.5 44.8 %all-to-all-start = ((f32[8,1,128]{2,1,0:T(1,128)}), f32[8,1,128]{2,1,0:T(1,128)S(1)}, u32[]{:S(2)}, u32[]{:S(2)}) async-start(f32[8,1,128]{2,1,0:T(1,128)} %broadcast_in_dim.41), calls=%async_computation | async-start | bytes 8192 | tf_op jit(solution)/shard_map/all_to_all | solution.py:22
  90.3 1.6 all-to-all-done
  92.6 4.8 %all-to-all-start.1 = ((f32[32,1,128]{2,1,0:T(1,128)}), f32[32,1,128]{2,1,0:T(1,128)S(1)}, u32[]{:S(2)}, u32[]{:S(2)}) async-start(f32[32,1,128]{2,1,0:T(1,128)} %broadcast_in_dim.42), calls=%async_computation.1 | async-start | bytes 32768 | tf_op jit(solution)/shard_map/all_to_all | solution.py:22
  97.3 3.3 %collective-permute-start.1 = (bf16[64,512]{1,0:T(8,128)(2,1)S(1)}, bf16[64,512]{1,0:T(8,128)(2,1)S(1)}, u32[]{:S(2)}, u32[]{:S(2)}) collective-permute-start(bf16[64,512]{1,0:T(8,128)(2,1)S(1)} %bitcast.58), channel_id=1, source_target_pairs={{0,4},{2,6},{4,8},{6,10},{8,12},{10,14},{12,16},{14,18},{16,20},{1... | collective-permute-start | bytes 196616 | tf_op jit(solution)/shard_map/ppermute | solution.py:28
  100.7 2.3 collective-permute-done.1
  103.1 5.1 %all_gather.18 = bf16[7,128,512]{2,1,0:T(8,128)(2,1)} all-gather(bf16[7,64,512]{2,1,0:T(8,128)(2,1)S(1)} %bitcast_dynamic-update-slice_fusion.1), channel_id=1, replica_groups=mesh['img'=2,'x'=4,'z'=32,'col'=2] {'col'}, dimensions={1}, use_global_device_ids=true | all-gather | bytes 1376256 | tf_op jit(solution)/shard_map/all_gather | solution.py:217
  108.2 9.7 %all-to-all-done.1 = f32[32,1,128]{2,1,0:T(1,128)S(1)} async-done(((f32[32,1,128]{2,1,0:T(1,128)}), f32[32,1,128]{2,1,0:T(1,128)S(1)}, u32[]{:S(2)}, u32[]{:S(2)}) %all-to-all-start.1) | async-done | bytes 16416 | tf_op jit(solution)/shard_map/all_to_all | solution.py:22
  120.4 56.9 %all-gather.4.cloned.1.call-done.w_ref = bf16[32,27,16,256]{3,2,1,0:T(8,128)(2,1)} async-done(((bf16[1,27,16,256]{3,2,1,0:T(8,128)(2,1)}), bf16[32,27,16,256]{3,2,1,0:T(8,128)(2,1)}) %all-gather.4.cloned.1.call-update) | async-done | bytes 7077904 | tf_op jit(solution)/shard_map/all_gather | solution.py:210
  177.3 9.1 %conv_one.1 = (bf16[640,256]{1,0:T(8,128)(2,1)}, f32[8,128]{1,0:T(8,128)}) custom-call(s32[1]{0:T(128)} %bitcast.at_ref, bf16[896,512]{1,0:T(8,128)(2,1)} %bitcast.44, f32[1,512]{1,0:T(1,128)} %slice.61.a_ref, f32[1,512]{1,0:T(1,128)} %slice.63.b_ref, f32[1,256]{1,0:T(1,128)} %get-tuple-element.19.bias_ref, f32[512,128]{1,0:T(8,128)} %add_convert_fusion.pick_ref, ...), custom_call_target="tpu_custom_call" | custom-call | tf_op jit(solution)/shard_map/conv_one/pallas_call | solution.py:246
  187.7 20.4 %all-to-all-start.3 = ((f32[128,1,128]{2,1,0:T(1,128)}), f32[128,1,128]{2,1,0:T(1,128)S(1)}, u32[]{:S(2)}, u32[]{:S(2)}) async-start(f32[128,1,128]{2,1,0:T(1,128)} %broadcast_in_dim.50), calls=%async_computation.3 | async-start | bytes 131072 | tf_op jit(solution)/shard_map/all_to_all | solution.py:22
  208.1 1.0 slice.82
  209.8 20.5 %all-to-all-done.3 = f32[128,1,128]{2,1,0:T(1,128)S(1)} async-done(((f32[128,1,128]{2,1,0:T(1,128)}), f32[128,1,128]{2,1,0:T(1,128)S(1)}, u32[]{:S(2)}, u32[]{:S(2)}) %all-to-all-start.3) | async-done | bytes 65568 | tf_op jit(solution)/shard_map/all_to_all | solution.py:22
  231.0 2.4 norm_two.1
  233.4 24.3 %all-gather = bf16[1280,256]{1,0:T(8,128)(2,1)} all-gather(bf16[640,256]{1,0:T(8,128)(2,1)} %norm_two.1), channel_id=2, replica_groups=mesh['img'=2,'x'=4,'z'=32,'col'=2] {'col'}, dimensions={0}, use_global_device_ids=true | all-gather | bytes 983040 | tf_op jit(solution)/shard_map/all_gather | solution.py:270
  257.7 7.5 %conv_two.1 = bf16[384,256]{1,0:T(8,128)(2,1)} custom-call(s32[1]{0:T(128)} %bitcast.at_ref, bf16[2,640,256]{2,1,0:T(8,128)(2,1)} %bitcast.45, bf16[384,256]{1,0:T(8,128)(2,1)} %constant_dynamic-slice_fusion.res_ref, f32[1,256]{1,0:T(1,128)} %get-tuple-element.16.bias_ref, bf16[32,27,16,256]{3,2,1,0:T(8,128)(2,1)} %all-gather.4.cloned.1.call-done.w_ref), custom_call_target="tpu_custom_call" | custom-call | tf_op jit(solution)/shard_map/conv_two/pallas_call | solution.py:274
  265.2 3.7 %all-gather.1 = bf16[768,256]{1,0:T(8,128)(2,1)} all-gather(bf16[384,256]{1,0:T(8,128)(2,1)} %conv_two.1), channel_id=3, replica_groups=mesh['img'=2,'x'=4,'z'=32,'col'=2] {'col'}, dimensions={0}, use_global_device_ids=true | all-gather | bytes 589824 | tf_op jit(solution)/shard_map/all_gather | solution.py:286
  268.9 7.5 %conv_up.1 = bf16[2,2,128,256]{3,2,1,0:T(8,128)(2,1)} custom-call(bf16[2,384,256]{2,1,0:T(8,128)(2,1)} %bitcast.46, f32[1,256]{1,0:T(1,128)} %get-tuple-element.15.bias_ref, bf16[32,27,16,256]{3,2,1,0:T(8,128)(2,1)} %all-gather.4.cloned.1.call-done.w_ref), custom_call_target="tpu_custom_call" | custom-call | tf_op jit(solution)/shard_map/conv_up/pallas_call | solution.py:288
  276.5 5.0 %all_to_all.31 = bf16[2,2,128,256]{3,2,1,0:T(8,128)(2,1)S(1)} all-to-all(bf16[2,2,128,256]{3,2,1,0:T(8,128)(2,1)} %conv_up.1), channel_id=1, replica_groups=mesh['img'=2,'x'=4,'z'=32,'col'=2] {'col'}, dimensions={0} | all-to-all | bytes 524288 | tf_op jit(solution)/shard_map/all_to_all | solution.py:301
  (93 shorter events, 15.0 us)
Async XLA Ops:
  6.5 14.1 %copy-start.1 = (bf16[1,64,512]{2,1,0:T(8,128)(2,1)S(1)}, bf16[1,64,512]{2,1,0:T(8,128)(2,1)}, u32[]{:S(2)}) copy-start(bf16[1,64,512]{2,1,0:T(8,128)(2,1)} %param.11) | copy-start | bytes 196612
  6.5 170.7 %all-gather.4.cloned.1.call-start = ((), (), s32[]{:S(2)}) async-start(), calls=%async_computation.5 | async-start | bytes 7299072 | tf_op jit(solution)/shard_map/all_gather | solution.py:210
  9.0 78.5 %copy-start.2 = (f32[512]{0:T(512)S(1)}, f32[512]{0:T(512)}, u32[]{:S(2)}) copy-start(f32[512]{0:T(512)} %param.15) | copy-start | bytes 6148
  9.0 78.7 %copy-start.3 = (f32[512]{0:T(512)S(1)}, f32[512]{0:T(512)}, u32[]{:S(2)}) copy-start(f32[512]{0:T(512)} %param.16) | copy-start | bytes 6148
  9.0 78.9 %copy-start.4 = (f32[512]{0:T(512)S(1)}, f32[512]{0:T(512)}, u32[]{:S(2)}) copy-start(f32[512]{0:T(512)} %param.17) | copy-start | bytes 6148
  9.0 79.1 %copy-start.5 = (f32[512]{0:T(512)S(1)}, f32[512]{0:T(512)}, u32[]{:S(2)}) copy-start(f32[512]{0:T(512)} %param.19) | copy-start | bytes 6148
  9.0 79.8 %copy-start.6 = (f32[512]{0:T(512)S(1)}, f32[512]{0:T(512)}, u32[]{:S(2)}) copy-start(f32[512]{0:T(512)} %param.21) | copy-start | bytes 6148
  9.4 109.0 %copy-start.7 = (f32[512]{0:T(512)S(1)}, f32[512]{0:T(512)}, u32[]{:S(2)}) copy-start(f32[512]{0:T(512)} %param.13) | copy-start | bytes 6148
  9.4 109.0 %copy-start.8 = (f32[512]{0:T(512)S(1)}, f32[512]{0:T(512)}, u32[]{:S(2)}) copy-start(f32[512]{0:T(512)} %param.12) | copy-start | bytes 6148
  21.0 82.1 %collective-permute-start.4 = (bf16[64,512]{1,0:T(8,128)(2,1)S(1)}, bf16[64,512]{1,0:T(8,128)(2,1)S(1)}, u32[]{:S(2)}, u32[]{:S(2)}) collective-permute-start(bf16[64,512]{1,0:T(8,128)(2,1)S(1)} %bitcast.53), channel_id=1, source_target_pairs={{4,0},{6,2},{8,4},{10,6},{12,8},{14,10},{16,12},{18,14},{20,16},{2... | collective-permute-start | bytes 196616 | tf_op jit(solution)/shard_map/ppermute | solution.py:28
  22.3 80.8 %collective-permute-start.3 = (bf16[64,512]{1,0:T(8,128)(2,1)S(1)}, bf16[64,512]{1,0:T(8,128)(2,1)S(1)}, u32[]{:S(2)}, u32[]{:S(2)}) collective-permute-start(bf16[64,512]{1,0:T(8,128)(2,1)S(1)} %bitcast.54), channel_id=1, source_target_pairs={{2,0},{4,2},{6,4},{8,6},{10,8},{12,10},{14,12},{16,14},{18,16},{20... | collective-permute-start | bytes 196616 | tf_op jit(solution)/shard_map/ppermute | solution.py:28
  23.6 79.5 %collective-permute-start.5 = (bf16[64,512]{1,0:T(8,128)(2,1)S(1)}, bf16[64,512]{1,0:T(8,128)(2,1)S(1)}, u32[]{:S(2)}, u32[]{:S(2)}) collective-permute-start(bf16[64,512]{1,0:T(8,128)(2,1)S(1)} %bitcast.55), channel_id=1, source_target_pairs={{6,0},{8,2},{10,4},{12,6},{14,8},{16,10},{18,12},{20,14},{22,16},{... | collective-permute-start | bytes 196616 | tf_op jit(solution)/shard_map/ppermute | solution.py:28
  24.9 78.1 %collective-permute-start.2 = (bf16[64,512]{1,0:T(8,128)(2,1)S(1)}, bf16[64,512]{1,0:T(8,128)(2,1)S(1)}, u32[]{:S(2)}, u32[]{:S(2)}) collective-permute-start(bf16[64,512]{1,0:T(8,128)(2,1)S(1)} %bitcast.56), channel_id=1, source_target_pairs={{0,2},{2,4},{4,6},{6,8},{8,10},{10,12},{12,14},{14,16},{16,18},{18... | collective-permute-start | bytes 196616 | tf_op jit(solution)/shard_map/ppermute | solution.py:28
  30.0 67.3 %collective-permute-start = (bf16[64,512]{1,0:T(8,128)(2,1)S(1)}, bf16[64,512]{1,0:T(8,128)(2,1)S(1)}, u32[]{:S(2)}, u32[]{:S(2)}) collective-permute-start(bf16[64,512]{1,0:T(8,128)(2,1)S(1)} %bitcast.57), channel_id=1, source_target_pairs={{0,6},{2,8},{4,10},{6,12},{8,14},{10,16},{12,18},{14,20},{16,22},{... | collective-permute-start | bytes 196616 | tf_op jit(solution)/shard_map/ppermute | solution.py:28
  42.5 49.4 %all-to-all-start = ((f32[8,1,128]{2,1,0:T(1,128)}), f32[8,1,128]{2,1,0:T(1,128)S(1)}, u32[]{:S(2)}, u32[]{:S(2)}) async-start(f32[8,1,128]{2,1,0:T(1,128)} %broadcast_in_dim.41), calls=%async_computation | async-start | bytes 8192 | tf_op jit(solution)/shard_map/all_to_all | solution.py:22
  92.6 25.4 %all-to-all-start.1 = ((f32[32,1,128]{2,1,0:T(1,128)}), f32[32,1,128]{2,1,0:T(1,128)S(1)}, u32[]{:S(2)}, u32[]{:S(2)}) async-start(f32[32,1,128]{2,1,0:T(1,128)} %broadcast_in_dim.42), calls=%async_computation.1 | async-start | bytes 32768 | tf_op jit(solution)/shard_map/all_to_all | solution.py:22
  97.3 5.7 %collective-permute-start.1 = (bf16[64,512]{1,0:T(8,128)(2,1)S(1)}, bf16[64,512]{1,0:T(8,128)(2,1)S(1)}, u32[]{:S(2)}, u32[]{:S(2)}) collective-permute-start(bf16[64,512]{1,0:T(8,128)(2,1)S(1)} %bitcast.58), channel_id=1, source_target_pairs={{0,4},{2,6},{4,8},{6,10},{8,12},{10,14},{12,16},{14,18},{16,20},{1... | collective-permute-start | bytes 196616 | tf_op jit(solution)/shard_map/ppermute | solution.py:28
  187.7 42.6 %all-to-all-start.3 = ((f32[128,1,128]{2,1,0:T(1,128)}), f32[128,1,128]{2,1,0:T(1,128)S(1)}, u32[]{:S(2)}, u32[]{:S(2)}) async-start(f32[128,1,128]{2,1,0:T(1,128)} %broadcast_in_dim.50), calls=%async_computation.3 | async-start | bytes 131072 | tf_op jit(solution)/shard_map/all_to_all | solution.py:22
  230.3 0.6 copy-start
Sparse Core Ops, SparseCore 0:
  20.7 156.4 all-gather.3

commit v2 on v1

v2 whole, which is shorter than its diff:
```python
import functools

import jax
import jax.numpy as jnp
from jax import lax
from jax.experimental import pallas as pl
from jax.experimental.pallas import tpu as pltpu
from jax.sharding import Mesh
from jax.sharding import PartitionSpec as P

G = 32
EPS = 1e-06
F32, BF16 = jnp.float32, jnp.bfloat16
HIGHEST = lax.Precision.HIGHEST
ROW = ("x", "zh", "zl")
IMG_ROW = ("img",) + ROW


def sum_over(vector, axes):
    count = lax.axis_size(axes)
    sent = jnp.broadcast_to(vector, (count, vector.shape[1]))
    return lax.all_to_all(sent, axes, 0, 0, tiled=True)


def shifted_rows(values, axis, by):
    count = lax.axis_size(axis)
    pairs = [(i, i - by) for i in range(count) if 0 <= i - by < count]
    return lax.ppermute(values, axis, pairs)


def put_shifted(S, row, cols, y, lanes):
    at = pl.ds(row * cols, cols)
    column = lax.broadcasted_iota(jnp.int32, y.shape, 0)
    S[1, at, lanes] = y.astype(BF16)
    S[0, at, lanes] = jnp.where(column == 0, 0.0, pltpu.roll(y, 1, 0)).astype(BF16)
    S[2, at, lanes] = jnp.where(column == cols - 1, 0.0, pltpu.roll(y, cols - 1, 0)).astype(BF16)


def silu(u):
    return u / (1.0 + jnp.exp(-u))


def spread_stats(stats, pick, count, gain, shift):
    totals = jnp.sum(stats, axis=0, keepdims=True)
    totals = jnp.broadcast_to(totals, (8, totals.shape[1]))
    spread = lax.dot_general(
        totals, pick, (((1,), (1,)), ((), ())), precision=HIGHEST, preferred_element_type=F32
    )
    width = gain.shape[1]
    mean = spread[:1, :width] / count
    var = spread[:1, width:] / count - mean * mean
    a = lax.rsqrt(var + EPS) * gain
    return a, shift - mean * a


def conv_one_kernel(cols, image_rows, count, at_ref, x_ref, stats_ref, gain_ref, shift_ref, pick_ref, w_ref, out_ref, S):
    quad, depth = x_ref.shape[0], x_ref.shape[3]
    a, b = spread_stats(stats_ref[...], pick_ref[...], count, gain_ref[...], shift_ref[...])
    first = at_ref[0] // quad * quad - 1
    column = lax.broadcasted_iota(jnp.int32, (cols, depth), 0)
    for i in range(quad + 2):
        member = min(max(i - 1, 0), quad - 1)
        slot = 0 if 1 <= i <= quad else 1
        y = silu(x_ref[member, slot].astype(F32) * a + b)
        if slot:
            y = jnp.where(jnp.logical_and(first + i >= 0, first + i < image_rows), y, 0.0)
        at = slice(i * cols, (i + 1) * cols)
        left = jnp.where(column == 0, 0.0, pltpu.roll(y, 1, 0))
        right = jnp.where(column == cols - 1, 0.0, pltpu.roll(y, cols - 1, 0))
        S[at, 0 * depth : 1 * depth] = left.astype(BF16)
        S[at, 1 * depth : 2 * depth] = y.astype(BF16)
        S[at, 2 * depth : 3 * depth] = right.astype(BF16)
    outs = out_ref.shape[2]
    total = jnp.zeros((quad * cols, outs), F32)
    for r in range(3):
        piece = jnp.concatenate([w_ref[:, 3 * r + k].reshape(depth, outs) for k in range(3)], axis=0)
        total += jnp.dot(S[r * cols : (r + quad) * cols, :], piece, preferred_element_type=F32)
    out_ref[...] = total.reshape(quad, cols, outs)


def join_kernel(x_ref, bias_ref, pick_ref, out_ref, sums_ref):
    total = x_ref[0]
    for k in range(1, x_ref.shape[0]):
        total += x_ref[k]
    hidden = (total + bias_ref[...]).astype(BF16)
    out_ref[...] = hidden
    own = hidden.astype(F32)
    both = jnp.concatenate(
        [jnp.sum(own, axis=0, keepdims=True), jnp.sum(own * own, axis=0, keepdims=True)], axis=1
    )
    both = jnp.broadcast_to(both, (8, both.shape[1]))
    sums_ref[...] = jnp.dot(both, pick_ref[...], precision=HIGHEST, preferred_element_type=F32)


def norm_kernel(rows, image_rows, count, at_ref, *refs):
    stats_ref, gain_ref, shift_ref, pick_ref, out_ref = refs[rows:]
    a, b = spread_stats(stats_ref[...], pick_ref[...], count, gain_ref[...], shift_ref[...])
    first = at_ref[0] - rows // 2
    for i in range(rows):
        y = silu(refs[i][...].astype(F32) * a + b)
        inside = jnp.logical_and(first + i >= 0, first + i < image_rows)
        cols = y.shape[0]
        out_ref[i * cols : (i + 1) * cols, :] = jnp.where(inside, y, 0.0).astype(BF16)


def conv_two_kernel(cols, rows, image_rows, at_ref, x_ref, res_ref, bias_ref, w_ref, out_ref, S, acc):
    t = pl.program_id(0)
    outs = acc.shape[1]

    @pl.when(t == 0)
    def _():
        for i in range(rows + 2):
            for h in range(2):
                y = x_ref[h, pl.ds(i * cols, cols), :].astype(F32)
                put_shifted(S, i, cols, y, slice(h * outs, (h + 1) * outs))
        acc[...] = jnp.broadcast_to(bias_ref[...], acc.shape)

    start = pl.multiple_of((t // 3) * cols, cols)
    piece = w_ref[...].reshape(-1, outs)
    acc[...] += jnp.dot(S[t % 3, pl.ds(start, rows * cols), :], piece, preferred_element_type=F32)

    @pl.when(t == 8)
    def _():
        first = at_ref[0] - rows // 2
        for i in range(rows):
            at = pl.ds(i * cols, cols)
            y = acc[at, :] + res_ref[at, :].astype(F32)
            inside = jnp.logical_and(first + i >= 0, first + i < image_rows)
            out_ref[at, :] = jnp.where(inside, y, 0.0).astype(BF16)


def conv_up_kernel(cols, x_ref, bias_ref, w_ref, out_ref, S, acc, full):
    t = pl.program_id(0)
    outs = acc.shape[2]

    @pl.when(t == 0)
    def _():
        for i in range(3):
            for h in range(2):
                y = x_ref[h, pl.ds(i * cols, cols), :].astype(F32)
                put_shifted(S, i, cols, y, slice(h * outs, (h + 1) * outs))
        acc[...] = jnp.broadcast_to(bias_ref[...][None], acc.shape)

    a, c = t // 3, t % 3
    piece = w_ref[...].reshape(-1, outs)
    for p in range(2):
        for q in range(2):
            start = pl.multiple_of(((a + 1 + p) // 2) * cols, cols)
            acc[2 * p + q] += jnp.dot(
                S[(c + 1 + q) // 2, pl.ds(start, cols), :], piece, preferred_element_type=F32
            )

    @pl.when(t == 8)
    def _():
        for p in range(2):
            for q in range(2):
                for k in range(2):
                    lanes = slice(k * 128, (k + 1) * 128)
                    full[p, k, pl.ds(q, cols, stride=2), :] = acc[2 * p + q][:, lanes]
            for k in range(2):
                for half in range(2):
                    out_ref[half, p, :, k * 128 : (k + 1) * 128] = full[
                        p, k, half * cols : (half + 1) * cols, :
                    ].astype(BF16)


VM = pl.BlockSpec(memory_space=pltpu.VMEM)
SM = pl.BlockSpec(memory_space=pltpu.SMEM)


def weight_spec(gathered, base):
    n, _, rows, outs = gathered.shape
    return pl.BlockSpec((n, 1, rows, outs), lambda t: (0, base + t, 0, 0))


def on_device(
    features,
    first_gain,
    first_shift,
    first_weight,
    first_bias,
    second_gain,
    second_shift,
    second_weight,
    second_bias,
    upsample_weight,
    upsample_bias,
):
    _, breadth, channels = features.shape
    nx, nzh, nzl, ncol = (lax.axis_size(axis) for axis in ("x", "zh", "zl", "col"))
    nz = nzh * nzl
    k_own = first_weight.shape[2]
    cols = breadth * ncol
    half = channels // ncol
    depth = channels // nzl
    image_rows = nx * nz
    per_group = channels // G
    count = image_rows * cols * per_group
    c = lax.axis_index("col")
    zl = lax.axis_index("zl")
    at = lax.axis_index(ROW).astype(jnp.int32)[None]

    def order(v, axes):
        v = v.reshape(-1, nx, nzh, nzl, k_own).transpose(0, *[k + 1 for k in axes], 4)
        return v.reshape(-1, channels)

    place = lax.broadcasted_iota(jnp.int32, (channels, channels), 1)
    natural = lax.broadcasted_iota(jnp.int32, (channels, channels), 0)
    k, x = place % k_own, place // k_own % nx
    line = place // (k_own * nx)
    source = (x * nz + line) * k_own + k
    move = (natural == source).astype(BF16)
    source = (x * nz + line % nzh * nzl + line // nzh) * k_own + k
    move_one = (natural == source).astype(BF16)

    def moved(v, by):
        return jnp.dot(v, by, preferred_element_type=F32).astype(BF16)

    def own_half(v):
        return lax.dynamic_slice_in_dim(v, c * half, half, v.ndim - 1)

    taps = 9 * k_own
    hold = moved(
        jnp.concatenate([first_weight.reshape(taps, channels), second_weight.reshape(taps, channels)]),
        move,
    )
    hold = jnp.concatenate([hold, upsample_weight.reshape(taps, channels)])
    hold = own_half(hold).reshape(1, 27, k_own, half)
    hold = lax.all_to_all(jnp.broadcast_to(hold, (nx, 27, k_own, half)), "x", 0, 0, tiled=True)
    hold = hold.transpose(1, 0, 2, 3).reshape(27, nx * k_own, half)
    weights = lax.all_gather(hold[9:], ("zh", "zl"))
    weights_one = lax.all_gather(hold[:9], "zh")

    own = features[0]
    wide = own.astype(F32)
    chan = lax.broadcasted_iota(jnp.int32, (channels, G), 0) // per_group
    member = (chan == lax.broadcasted_iota(jnp.int32, (channels, G), 1)).astype(F32)
    sums = jnp.stack([jnp.sum(wide, axis=0), jnp.sum(wide * wide, axis=0)])
    sums = jnp.dot(sums, member, precision=HIGHEST).reshape(1, 2 * G)
    sums = jnp.pad(sums, ((0, 0), (0, 128 - 2 * G)))
    sums = jnp.sum(sum_over(sums, ("x", "col")), axis=0, keepdims=True)
    sums = sum_over(sums, ("zh", "zl"))

    up_row, down_row = shifted_rows(own, ROW, -1), shifted_rows(own, ROW, 1)
    three = lax.all_gather(jnp.stack([up_row, own, down_row]), "col", axis=1, tiled=True)
    residual = own_half(moved(three.reshape(3 * cols, channels), move))
    edge = jnp.where(zl == 0, three[0], three[2])
    sent = moved(jnp.concatenate([three[1], edge]), move_one)
    sent = sent.reshape(2, cols, nzl, depth).transpose(2, 0, 1, 3)
    quad = lax.all_to_all(sent, "zl", 0, 0, tiled=True)

    def own_depth(v):
        return lax.dynamic_slice_in_dim(v, zl * depth, depth, 1)

    gain_one = own_depth(order(first_gain, (2, 1, 0)))
    shift_one = own_depth(order(first_shift, (2, 1, 0)))
    vectors = order(jnp.stack([first_bias, second_gain, second_shift, second_bias]), (1, 2, 0))
    vectors = own_half(jnp.concatenate([vectors, upsample_bias[None]]))
    bias_one, gain_two, shift_two, bias_two, bias_up = [vectors[i : i + 1] for i in range(5)]

    def picks(group, groups):
        pick = group[:, None] == jnp.arange(128)[None, :]
        return jnp.concatenate([pick, jnp.roll(pick, groups, axis=1)]).astype(F32)

    lane = jnp.arange(depth)
    pick_one = picks(lane // k_own % nx * nzh + lane // (k_own * nx), G)
    lane = jnp.arange(half)
    pick = picks(lane // (k_own * nx * nzl) * nx + lane // k_own % nx, G // ncol)

    parts = pl.pallas_call(
        functools.partial(conv_one_kernel, cols, image_rows, count),
        out_shape=jax.ShapeDtypeStruct((nzl, cols, half), F32),
        in_specs=[SM] + [VM] * 6,
        out_specs=VM,
        scratch_shapes=[pltpu.VMEM(((nzl + 2) * cols, 3 * depth), BF16)],
        name="conv_one",
    )(at, quad, sums, gain_one, shift_one, pick_one, weights_one)
    parts = lax.all_to_all(parts, "zl", 0, 0, tiled=True)
    hidden, sums_two = pl.pallas_call(
        join_kernel,
        out_shape=(
            jax.ShapeDtypeStruct((cols, half), BF16),
            jax.ShapeDtypeStruct((8, 128), F32),
        ),
        in_specs=[VM] * 3,
        out_specs=(VM, VM),
        name="join_one",
    )(parts, bias_one, pick)

    stats = jnp.sum(sum_over(sums_two[:1], ("x", "zl")), axis=0, keepdims=True)
    stats = sum_over(stats, "zh")
    five = [hidden if d == 0 else shifted_rows(hidden, ROW, d) for d in range(-2, 3)]
    normed = pl.pallas_call(
        functools.partial(norm_kernel, 5, image_rows, count),
        out_shape=jax.ShapeDtypeStruct((5 * cols, half), BF16),
        in_specs=[SM] + [VM] * 9,
        out_specs=VM,
        name="norm_two",
    )(at, *five, stats, gain_two, shift_two, pick)
    normed = lax.all_gather(normed, "col")

    rows = 3
    block = pl.pallas_call(
        functools.partial(conv_two_kernel, cols, rows, image_rows),
        grid=(9,),
        out_shape=jax.ShapeDtypeStruct((rows * cols, half), BF16),
        in_specs=[SM, VM, VM, VM, weight_spec(weights, 0)],
        out_specs=VM,
        scratch_shapes=[
            pltpu.VMEM((3, (rows + 2) * cols, channels), BF16),
            pltpu.VMEM((rows * cols, half), F32),
        ],
        name="conv_two",
    )(at, normed, residual, bias_two, weights)
    block = lax.all_gather(block, "col")

    up = pl.pallas_call(
        functools.partial(conv_up_kernel, cols),
        grid=(9,),
        out_shape=jax.ShapeDtypeStruct((ncol, 2, cols, half), BF16),
        in_specs=[VM, VM, weight_spec(weights, 9)],
        out_specs=VM,
        scratch_shapes=[
            pltpu.VMEM((3, 3 * cols, channels), BF16),
            pltpu.VMEM((4, cols, half), F32),
            pltpu.VMEM((2, 2, 2 * cols, 128), F32),
        ],
        name="conv_up",
    )(block, bias_up, weights)
    up = lax.all_to_all(up, "col", 0, 0, tiled=True)
    return up.transpose(1, 2, 0, 3).reshape(2, cols, channels)


def solution(mesh):
    finer = Mesh(
        mesh.devices.reshape(mesh.shape["img"], 4, 8, 4, mesh.shape["col"]),
        IMG_ROW + ("col",),
    )
    in_specs = (
        P(IMG_ROW, "col", None),
        P(),
        P(),
        P(None, None, ROW, None),
        P(),
        P(),
        P(),
        P(None, None, ROW, None),
        P(),
        P(None, None, ROW, None),
        P(),
    )
    return jax.shard_map(
        on_device,
        mesh=finer,
        in_specs=in_specs,
        out_specs=P(IMG_ROW, "col", None),
        check_vma=False,
    )
```

time: 291 us -> 281 us (0.966)
  waiting for transfers between devices: 91.1 us -> 55 us
  blocking collectives: 48.3 us -> 78.6 us
  Pallas kernels: 26.6 us -> 22.6 us
    all_gather x1, waiting for transfers between devices: 56.9 us -> 0.01 us  [on_device(): weights = lax.all_gather(hold[9:], ('zh', 'zl'))]
    all_gather x1 -> x2, blocking collectives: 5.11 us -> 41.4 us  [the longest x1 39 us: on_device(): weights_one = lax.all_gather(hold[:9], 'zh')]
    all_to_all x0 -> x2, waiting for transfers between devices: none -> 13.7 us  [the longest x1 13.7 us: on_device(): parts = lax.all_to_all(parts, 'zl', 0, 0, tiled=True)]
    all_to_all x3 -> x4, waiting for transfers between devices: 31.8 us -> 41.3 us  [sum_over(): return lax.all_to_all(sent, axes, 0, 0, tiled=True)]
    all_to_all x0 -> x2, starting transfers between devices: none -> 9.24 us  [the longest x1 5.74 us: on_device(): parts = lax.all_to_all(parts, 'zl', 0, 0, tiled=True)]
    ppermute x6, starting transfers between devices: 23.7 us -> 15.2 us  [shifted_rows(): return lax.ppermute(values, axis, pairs)]
    all_gather x1, blocking collectives: 24.3 us -> 18.2 us  [on_device(): normed = lax.all_gather(normed, 'col')]
    pallas_call x2 -> x3, Pallas kernels: 11.6 us -> 7.52 us  [the longest x1 3.08 us: on_device(): pl.pallas_call(functools.partial(conv_one_kernel, cols, image_rows, count...]
  transfers between devices with their start and end apart: 10 -> 13, of which waited for: 5 -> 4; matrix products, arithmetic and copies ran while one was open for 3% -> 4% of each run, Pallas kernels for 0% -> 3%
where the time goes in v2:
time: 281 us; the launch traced here: 279 us
  starting transfers between devices  91.6 us (33%)
  blocking collectives  78.6 us (28%)
  waiting for transfers between devices  55 us (20%)
  Pallas kernels  22.6 us (8%)
  local copies, waits for them, and re-layouts  14.1 us (5%)
  between operations  13.9 us (5%)
    all_to_all x4, starting transfers between devices, sum_over(): return lax.all_to_all(sent, axes, 0, 0, tiled=True)  67.1 us
    all_to_all x4, waiting for transfers between devices, sum_over(): return lax.all_to_all(sent, axes, 0, 0, tiled=True)  41.3 us
    all_gather x1, blocking collectives, on_device(): weights_one = lax.all_gather(hold[:9], 'zh')  39 us
    all_gather x1, blocking collectives, on_device(): normed = lax.all_gather(normed, 'col')  18.2 us
    ppermute x6, starting transfers between devices, shifted_rows(): return lax.ppermute(values, axis, pairs)  15.2 us
    all_to_all x1, waiting for transfers between devices, on_device(): parts = lax.all_to_all(parts, 'zl', 0, 0, tiled=True)  13.7 us
    all_to_all x1, blocking collectives, on_device(): lax.all_to_all(jnp.broadcast_to(hold, (nx, 27, k_own, half)), 'x', 0, 0,...  10.2 us
    pallas_call x1, Pallas kernels, on_device(): pl.pallas_call(functools.partial(conv_up_kernel, cols), grid=(9,), out_sh...  7.53 us
  transfers between devices with their start and end apart: 13, of which 4 were waited for; matrix products, arithmetic and copies ran while one was open for 4% of the time, Pallas kernels for 3%

profile of v2, /device:TPU:33, one launch (start us, length us, event | category | flops | bytes accessed | tf_op | source)
XLA Modules:
  0.0 279.5 jit_solution(5760767117681464590)
XLA Ops:
  9.4 10.2 %all_to_all.48 = bf16[4,27,4,256]{3,2,1,0:T(4,128)(2,1)S(1)} all-to-all(bf16[4,27,4,256]{3,2,1,0:T(4,128)(2,1)S(1)} %broadcast_in_dim.20), channel_id=1, replica_groups=mesh['img'=2,'x'=4,'zh'=8,'zl'=4,'col'=2] {'x'}, dimensions={0} | all-to-all | bytes 442368 | tf_op jit(solution)/shard_map/all_to_all | solution.py:229
  20.5 4.4 %collective-permute-start = (bf16[64,512]{1,0:T(8,128)(2,1)S(1)}, bf16[64,512]{1,0:T(8,128)(2,1)S(1)}, u32[]{:S(2)}, u32[]{:S(2)}) collective-permute-start(bf16[64,512]{1,0:T(8,128)(2,1)S(1)} %bitcast.47), channel_id=1, source_target_pairs={{0,2},{2,4},{4,6},{6,8},{8,10},{10,12},{12,14},{14,16},{16,18},{18... | collective-permute-start | bytes 196616 | tf_op jit(solution)/shard_map/ppermute | solution.py:28
  27.5 46.9 %all-to-all-start.1 = ((f32[8,1,128]{2,1,0:T(1,128)}), f32[8,1,128]{2,1,0:T(1,128)S(1)}, u32[]{:S(2)}, u32[]{:S(2)}) async-start(f32[8,1,128]{2,1,0:T(1,128)} %broadcast_in_dim.17), calls=%async_computation.1 | async-start | bytes 8192 | tf_op jit(solution)/shard_map/all_to_all | solution.py:22
  74.4 4.5 %all-to-all-done.1 = f32[8,1,128]{2,1,0:T(1,128)S(1)} async-done(((f32[8,1,128]{2,1,0:T(1,128)}), f32[8,1,128]{2,1,0:T(1,128)S(1)}, u32[]{:S(2)}, u32[]{:S(2)}) %all-to-all-start.1) | async-done | bytes 4128 | tf_op jit(solution)/shard_map/all_to_all | solution.py:22
  79.5 4.7 %all-to-all-start.2 = ((f32[32,1,128]{2,1,0:T(1,128)}), f32[32,1,128]{2,1,0:T(1,128)S(1)}, u32[]{:S(2)}, u32[]{:S(2)}) async-start(f32[32,1,128]{2,1,0:T(1,128)} %broadcast_in_dim.18), calls=%async_computation.2 | async-start | bytes 32768 | tf_op jit(solution)/shard_map/all_to_all | solution.py:22
  84.3 2.5 all_gather.27
  88.1 16.5 %all-to-all-done.2 = f32[32,1,128]{2,1,0:T(1,128)S(1)} async-done(((f32[32,1,128]{2,1,0:T(1,128)}), f32[32,1,128]{2,1,0:T(1,128)S(1)}, u32[]{:S(2)}, u32[]{:S(2)}) %all-to-all-start.2) | async-done | bytes 16416 | tf_op jit(solution)/shard_map/all_to_all | solution.py:22
  104.6 3.5 %all-to-all-start = ((bf16[4,2,128,128]{3,2,1,0:T(8,128)(2,1)}), bf16[4,2,128,128]{3,2,1,0:T(8,128)(2,1)S(1)}, u32[]{:S(2)}, u32[]{:S(2)}) async-start(bf16[4,2,128,128]{3,2,1,0:T(8,128)(2,1)} %bitcast.34), calls=%async_computation | async-start | bytes 524288 | tf_op jit(solution)/shard_map/all_to_all | solution.py:250
  110.4 39.0 %all_gather.29.w_ref = bf16[8,9,16,256]{3,2,1,0:T(8,128)(2,1)} all-gather(bf16[1,9,16,256]{3,2,1,0:T(8,128)(2,1)S(1)} %all_gather.28), channel_id=1, replica_groups=mesh['img'=2,'x'=4,'zh'=8,'zl'=4,'col'=2] {'zh'}, dimensions={0}, use_global_device_ids=true | all-gather | bytes 663552 | tf_op jit(solution)/shard_map/all_gather | solution.py:232
  150.1 3.1 %conv_one.1 = f32[4,128,256]{2,1,0:T(8,128)} custom-call(s32[1]{0:T(128)} %bitcast.at_ref, bf16[4,2,128,128]{3,2,1,0:T(8,128)(2,1)} %copy-done.1, f32[32,128]{1,0:T(8,128)} %bitcast.50, f32[1,128]{1,0:T(1,128)} %get-tuple-element.27.gain_ref, f32[1,128]{1,0:T(1,128)} %get-tuple-element.26.shift_ref, f32[256,128]{1,0:T(8,128)} %add_convert_fusion.1.pick_ref, ...), custom_call_target="tpu_custom_call" | custom-call | tf_op jit(solution)/shard_map/conv_one/pallas_call | solution.py:270
  153.2 5.7 %all-to-all-start.4 = ((f32[4,128,256]{2,1,0:T(8,128)}), f32[4,128,256]{2,1,0:T(8,128)S(1)}, u32[]{:S(2)}, u32[]{:S(2)}) async-start(f32[4,128,256]{2,1,0:T(8,128)} %conv_one.1), calls=%async_computation.4 | async-start | bytes 1048576 | tf_op jit(solution)/shard_map/all_to_all | solution.py:278
  161.7 13.7 %all-to-all-done.4.x_ref = f32[4,128,256]{2,1,0:T(8,128)S(1)} async-done(((f32[4,128,256]{2,1,0:T(8,128)}), f32[4,128,256]{2,1,0:T(8,128)S(1)}, u32[]{:S(2)}, u32[]{:S(2)}) %all-to-all-start.4) | async-done | bytes 524320 | tf_op jit(solution)/shard_map/all_to_all | solution.py:278
  176.3 2.0 join_one.1
  179.6 3.9 %all-to-all-start.5 = ((f32[16,1,128]{2,1,0:T(1,128)}), f32[16,1,128]{2,1,0:T(1,128)S(1)}, u32[]{:S(2)}, u32[]{:S(2)}) async-start(f32[16,1,128]{2,1,0:T(1,128)} %broadcast_in_dim.22), calls=%async_computation.5 | async-start | bytes 16384 | tf_op jit(solution)/shard_map/all_to_all | solution.py:22
  183.9 3.7 %collective-permute-start.2 = (bf16[128,256]{1,0:T(8,128)(2,1)S(1)}, bf16[128,256]{1,0:T(8,128)(2,1)S(1)}, u32[]{:S(2)}, u32[]{:S(2)}) collective-permute-start(bf16[128,256]{1,0:T(8,128)(2,1)S(1)} %copy-done.4), channel_id=1, source_target_pairs={{0,4},{2,6},{4,8},{6,10},{8,12},{10,14},{12,16},{14,18},{16,20},{1... | collective-permute-start | bytes 196616 | tf_op jit(solution)/shard_map/ppermute | solution.py:28
  187.6 3.1 %collective-permute-start.3 = (bf16[128,256]{1,0:T(8,128)(2,1)S(1)}, bf16[128,256]{1,0:T(8,128)(2,1)S(1)}, u32[]{:S(2)}, u32[]{:S(2)}) collective-permute-start(bf16[128,256]{1,0:T(8,128)(2,1)S(1)} %copy-done.4), channel_id=1, source_target_pairs={{0,2},{2,4},{4,6},{6,8},{8,10},{10,12},{12,14},{14,16},{16,18},{18... | collective-permute-start | bytes 196616 | tf_op jit(solution)/shard_map/ppermute | solution.py:28
  194.0 11.6 %all-to-all-start.6 = ((f32[8,1,128]{2,1,0:T(1,128)}), f32[8,1,128]{2,1,0:T(1,128)S(1)}, u32[]{:S(2)}, u32[]{:S(2)}) async-start(f32[8,1,128]{2,1,0:T(1,128)} %broadcast_in_dim.46), calls=%async_computation.6 | async-start | bytes 8192 | tf_op jit(solution)/shard_map/all_to_all | solution.py:22
  206.4 20.2 %all-to-all-done.6 = f32[8,1,128]{2,1,0:T(1,128)S(1)} async-done(((f32[8,1,128]{2,1,0:T(1,128)}), f32[8,1,128]{2,1,0:T(1,128)S(1)}, u32[]{:S(2)}, u32[]{:S(2)}) %all-to-all-start.6) | async-done | bytes 4128 | tf_op jit(solution)/shard_map/all_to_all | solution.py:22
  227.2 2.4 norm_two.1
  229.6 18.2 %all-gather = bf16[1280,256]{1,0:T(8,128)(2,1)} all-gather(bf16[640,256]{1,0:T(8,128)(2,1)} %norm_two.1), channel_id=2, replica_groups=mesh['img'=2,'x'=4,'zh'=8,'zl'=4,'col'=2] {'col'}, dimensions={0}, use_global_device_ids=true | all-gather | bytes 983040 | tf_op jit(solution)/shard_map/all_gather | solution.py:300
  247.8 7.5 %conv_two.1 = bf16[384,256]{1,0:T(8,128)(2,1)} custom-call(s32[1]{0:T(128)} %bitcast.at_ref, bf16[2,640,256]{2,1,0:T(8,128)(2,1)} %bitcast.37, bf16[384,256]{1,0:T(8,128)(2,1)} %dynamic-slice_convert_fusion.res_ref, f32[1,256]{1,0:T(1,128)} %get-tuple-element.14.bias_ref, bf16[32,18,16,256]{3,2,1,0:T(8,128)(2,1)} %all-gather.4.cloned.1.call-done.w_ref), custom_call_target="tpu_custom_call" | custom-call | tf_op jit(solution)/shard_map/conv_two/pallas_call | solution.py:303
  255.4 3.7 %all-gather.1 = bf16[768,256]{1,0:T(8,128)(2,1)} all-gather(bf16[384,256]{1,0:T(8,128)(2,1)} %conv_two.1), channel_id=3, replica_groups=mesh['img'=2,'x'=4,'zh'=8,'zl'=4,'col'=2] {'col'}, dimensions={0}, use_global_device_ids=true | all-gather | bytes 589824 | tf_op jit(solution)/shard_map/all_gather | solution.py:315
  259.1 7.5 %conv_up.1 = bf16[2,2,128,256]{3,2,1,0:T(8,128)(2,1)} custom-call(bf16[2,384,256]{2,1,0:T(8,128)(2,1)} %bitcast.39, f32[1,256]{1,0:T(1,128)} %get-tuple-element.13.bias_ref, bf16[32,18,16,256]{3,2,1,0:T(8,128)(2,1)} %all-gather.4.cloned.1.call-done.w_ref), custom_call_target="tpu_custom_call" | custom-call | tf_op jit(solution)/shard_map/conv_up/pallas_call | solution.py:317
  266.6 5.0 %all_to_all.49 = bf16[2,2,128,256]{3,2,1,0:T(8,128)(2,1)S(1)} all-to-all(bf16[2,2,128,256]{3,2,1,0:T(8,128)(2,1)} %conv_up.1), channel_id=1, replica_groups=mesh['img'=2,'x'=4,'zh'=8,'zl'=4,'col'=2] {'col'}, dimensions={0} | all-to-all | bytes 524288 | tf_op jit(solution)/shard_map/all_to_all | solution.py:330
  (110 shorter events, 21.8 us)
Async XLA Ops:
  6.5 241.3 %all-gather.4.cloned.1.call-start = ((), (), s32[]{:S(2)}) async-start(), calls=%async_computation.8 | async-start | bytes 4866048 | tf_op jit(solution)/shard_map/all_gather | solution.py:231
  20.5 63.7 %collective-permute-start = (bf16[64,512]{1,0:T(8,128)(2,1)S(1)}, bf16[64,512]{1,0:T(8,128)(2,1)S(1)}, u32[]{:S(2)}, u32[]{:S(2)}) collective-permute-start(bf16[64,512]{1,0:T(8,128)(2,1)S(1)} %bitcast.47), channel_id=1, source_target_pairs={{0,2},{2,4},{4,6},{6,8},{8,10},{10,12},{12,14},{14,16},{16,18},{18... | collective-permute-start | bytes 196616 | tf_op jit(solution)/shard_map/ppermute | solution.py:28
  25.0 59.3 %collective-permute-start.1 = (bf16[64,512]{1,0:T(8,128)(2,1)S(1)}, bf16[64,512]{1,0:T(8,128)(2,1)S(1)}, u32[]{:S(2)}, u32[]{:S(2)}) collective-permute-start(bf16[64,512]{1,0:T(8,128)(2,1)S(1)} %bitcast.48), channel_id=1, source_target_pairs={{2,0},{4,2},{6,4},{8,6},{10,8},{12,10},{14,12},{16,14},{18,16},{20... | collective-permute-start | bytes 196616 | tf_op jit(solution)/shard_map/ppermute | solution.py:28
  27.5 51.5 %all-to-all-start.1 = ((f32[8,1,128]{2,1,0:T(1,128)}), f32[8,1,128]{2,1,0:T(1,128)S(1)}, u32[]{:S(2)}, u32[]{:S(2)}) async-start(f32[8,1,128]{2,1,0:T(1,128)} %broadcast_in_dim.17), calls=%async_computation.1 | async-start | bytes 8192 | tf_op jit(solution)/shard_map/all_to_all | solution.py:22
  79.5 25.1 %all-to-all-start.2 = ((f32[32,1,128]{2,1,0:T(1,128)}), f32[32,1,128]{2,1,0:T(1,128)S(1)}, u32[]{:S(2)}, u32[]{:S(2)}) async-start(f32[32,1,128]{2,1,0:T(1,128)} %broadcast_in_dim.18), calls=%async_computation.2 | async-start | bytes 32768 | tf_op jit(solution)/shard_map/all_to_all | solution.py:22
  86.8 21.3 %copy-start.10 = (f32[512]{0:T(512)S(1)}, f32[512]{0:T(512)}, u32[]{:S(2)}) copy-start(f32[512]{0:T(512)} %param.12) | copy-start | bytes 6148
  86.8 21.7 %copy-start.11 = (f32[512]{0:T(512)S(1)}, f32[512]{0:T(512)}, u32[]{:S(2)}) copy-start(f32[512]{0:T(512)} %param.13) | copy-start | bytes 6148
  87.2 71.7 %copy-start.12 = (f32[512]{0:T(512)S(1)}, f32[512]{0:T(512)}, u32[]{:S(2)}) copy-start(f32[512]{0:T(512)} %param.15) | copy-start | bytes 6148
  87.3 71.8 %copy-start.13 = (f32[512]{0:T(512)S(1)}, f32[512]{0:T(512)}, u32[]{:S(2)}) copy-start(f32[512]{0:T(512)} %param.16) | copy-start | bytes 6148
  87.3 71.9 %copy-start.14 = (f32[512]{0:T(512)S(1)}, f32[512]{0:T(512)}, u32[]{:S(2)}) copy-start(f32[512]{0:T(512)} %param.17) | copy-start | bytes 6148
  87.3 72.1 %copy-start.15 = (f32[512]{0:T(512)S(1)}, f32[512]{0:T(512)}, u32[]{:S(2)}) copy-start(f32[512]{0:T(512)} %param.19) | copy-start | bytes 6148
  87.3 73.0 %copy-start.16 = (f32[512]{0:T(512)S(1)}, f32[512]{0:T(512)}, u32[]{:S(2)}) copy-start(f32[512]{0:T(512)} %param.21) | copy-start | bytes 6148
  104.6 44.7 %copy-start.3 = (f32[32,1,128]{2,1,0:T(1,128)}, f32[32,1,128]{2,1,0:T(1,128)S(1)}, u32[]{:S(2)}) copy-start(f32[32,1,128]{2,1,0:T(1,128)S(1)} %all-to-all-done.2) | copy-start | bytes 49156
  104.6 44.7 %all-to-all-start = ((bf16[4,2,128,128]{3,2,1,0:T(8,128)(2,1)}), bf16[4,2,128,128]{3,2,1,0:T(8,128)(2,1)S(1)}, u32[]{:S(2)}, u32[]{:S(2)}) async-start(bf16[4,2,128,128]{3,2,1,0:T(8,128)(2,1)} %bitcast.34), calls=%async_computation | async-start | bytes 524288 | tf_op jit(solution)/shard_map/all_to_all | solution.py:250
  153.2 22.3 %all-to-all-start.4 = ((f32[4,128,256]{2,1,0:T(8,128)}), f32[4,128,256]{2,1,0:T(8,128)S(1)}, u32[]{:S(2)}, u32[]{:S(2)}) async-start(f32[4,128,256]{2,1,0:T(8,128)} %conv_one.1), calls=%async_computation.4 | async-start | bytes 1048576 | tf_op jit(solution)/shard_map/all_to_all | solution.py:278
  179.6 13.8 %all-to-all-start.5 = ((f32[16,1,128]{2,1,0:T(1,128)}), f32[16,1,128]{2,1,0:T(1,128)S(1)}, u32[]{:S(2)}, u32[]{:S(2)}) async-start(f32[16,1,128]{2,1,0:T(1,128)} %broadcast_in_dim.22), calls=%async_computation.5 | async-start | bytes 16384 | tf_op jit(solution)/shard_map/all_to_all | solution.py:22
  183.9 22.4 %collective-permute-start.2 = (bf16[128,256]{1,0:T(8,128)(2,1)S(1)}, bf16[128,256]{1,0:T(8,128)(2,1)S(1)}, u32[]{:S(2)}, u32[]{:S(2)}) collective-permute-start(bf16[128,256]{1,0:T(8,128)(2,1)S(1)} %copy-done.4), channel_id=1, source_target_pairs={{0,4},{2,6},{4,8},{6,10},{8,12},{10,14},{12,16},{14,18},{16,20},{1... | collective-permute-start | bytes 196616 | tf_op jit(solution)/shard_map/ppermute | solution.py:28
  187.6 18.7 %collective-permute-start.3 = (bf16[128,256]{1,0:T(8,128)(2,1)S(1)}, bf16[128,256]{1,0:T(8,128)(2,1)S(1)}, u32[]{:S(2)}, u32[]{:S(2)}) collective-permute-start(bf16[128,256]{1,0:T(8,128)(2,1)S(1)} %copy-done.4), channel_id=1, source_target_pairs={{0,2},{2,4},{4,6},{6,8},{8,10},{10,12},{12,14},{14,16},{16,18},{18... | collective-permute-start | bytes 196616 | tf_op jit(solution)/shard_map/ppermute | solution.py:28
  190.7 15.6 %collective-permute-start.4 = (bf16[128,256]{1,0:T(8,128)(2,1)S(1)}, bf16[128,256]{1,0:T(8,128)(2,1)S(1)}, u32[]{:S(2)}, u32[]{:S(2)}) collective-permute-start(bf16[128,256]{1,0:T(8,128)(2,1)S(1)} %copy-done.4), channel_id=1, source_target_pairs={{2,0},{4,2},{6,4},{8,6},{10,8},{12,10},{14,12},{16,14},{18,16},{20... | collective-permute-start | bytes 196616 | tf_op jit(solution)/shard_map/ppermute | solution.py:28
  192.1 14.3 %collective-permute-start.5 = (bf16[128,256]{1,0:T(8,128)(2,1)S(1)}, bf16[128,256]{1,0:T(8,128)(2,1)S(1)}, u32[]{:S(2)}, u32[]{:S(2)}) collective-permute-start(bf16[128,256]{1,0:T(8,128)(2,1)S(1)} %copy-done.4), channel_id=1, source_target_pairs={{4,0},{6,2},{8,4},{10,6},{12,8},{14,10},{16,12},{18,14},{20,16},{2... | collective-permute-start | bytes 196616 | tf_op jit(solution)/shard_map/ppermute | solution.py:28
  194.0 32.6 %all-to-all-start.6 = ((f32[8,1,128]{2,1,0:T(1,128)}), f32[8,1,128]{2,1,0:T(1,128)S(1)}, u32[]{:S(2)}, u32[]{:S(2)}) async-start(f32[8,1,128]{2,1,0:T(1,128)} %broadcast_in_dim.46), calls=%async_computation.6 | async-start | bytes 8192 | tf_op jit(solution)/shard_map/all_to_all | solution.py:22
  206.3 20.3 %copy-start.5 = (bf16[128,256]{1,0:T(8,128)(2,1)}, bf16[128,256]{1,0:T(8,128)(2,1)S(1)}, u32[]{:S(2)}) copy-start(bf16[128,256]{1,0:T(8,128)(2,1)S(1)} %collective-permute-done.2.refs_0_) | copy-start | bytes 196612
  206.3 20.3 %copy-start.6 = (bf16[128,256]{1,0:T(8,128)(2,1)}, bf16[128,256]{1,0:T(8,128)(2,1)S(1)}, u32[]{:S(2)}) copy-start(bf16[128,256]{1,0:T(8,128)(2,1)S(1)} %collective-permute-done.3.refs_1_) | copy-start | bytes 196612
  206.3 20.3 %copy-start.7 = (bf16[128,256]{1,0:T(8,128)(2,1)}, bf16[128,256]{1,0:T(8,128)(2,1)S(1)}, u32[]{:S(2)}) copy-start(bf16[128,256]{1,0:T(8,128)(2,1)S(1)} %collective-permute-done.4.refs_3_) | copy-start | bytes 196612
  (6 other events, 42.0 us)
Sparse Core Ops, SparseCore 0:
  20.6 165.8 all-gather.3

commit v3 on v2

--- a/solution.py
+++ b/solution.py
@@ -54,14 +54,15 @@
 
 
 def conv_one_kernel(cols, image_rows, count, at_ref, x_ref, stats_ref, gain_ref, shift_ref, pick_ref, w_ref, out_ref, S):
-    quad, depth = x_ref.shape[0], x_ref.shape[3]
+    quad, depth = x_ref.shape[0], x_ref.shape[4]
     a, b = spread_stats(stats_ref[...], pick_ref[...], count, gain_ref[...], shift_ref[...])
     first = at_ref[0] // quad * quad - 1
     column = lax.broadcasted_iota(jnp.int32, (cols, depth), 0)
     for i in range(quad + 2):
         member = min(max(i - 1, 0), quad - 1)
         slot = 0 if 1 <= i <= quad else 1
-        y = silu(x_ref[member, slot].astype(F32) * a + b)
+        x = jnp.concatenate([x_ref[member, h, slot] for h in range(x_ref.shape[1])], axis=0)
+        y = silu(x.astype(F32) * a + b)
         if slot:
             y = jnp.where(jnp.logical_and(first + i >= 0, first + i < image_rows), y, 0.0)
         at = slice(i * cols, (i + 1) * cols)
@@ -75,13 +76,13 @@
     for r in range(3):
         piece = jnp.concatenate([w_ref[:, 3 * r + k].reshape(depth, outs) for k in range(3)], axis=0)
         total += jnp.dot(S[r * cols : (r + quad) * cols, :], piece, preferred_element_type=F32)
-    out_ref[...] = total.reshape(quad, cols, outs)
+    out_ref[...] = total.astype(BF16).reshape(quad, cols, outs)
 
 
 def join_kernel(x_ref, bias_ref, pick_ref, out_ref, sums_ref):
-    total = x_ref[0]
+    total = x_ref[0].astype(F32)
     for k in range(1, x_ref.shape[0]):
-        total += x_ref[k]
+        total += x_ref[k].astype(F32)
     hidden = (total + bias_ref[...]).astype(BF16)
     out_ref[...] = hidden
     own = hidden.astype(F32)
@@ -92,15 +93,16 @@
     sums_ref[...] = jnp.dot(both, pick_ref[...], precision=HIGHEST, preferred_element_type=F32)
 
 
-def norm_kernel(rows, image_rows, count, at_ref, *refs):
-    stats_ref, gain_ref, shift_ref, pick_ref, out_ref = refs[rows:]
+def norm_kernel(image_rows, count, at_ref, x_ref, stats_ref, gain_ref, shift_ref, pick_ref, out_ref):
     a, b = spread_stats(stats_ref[...], pick_ref[...], count, gain_ref[...], shift_ref[...])
+    halves, rows, cols, half = x_ref.shape
     first = at_ref[0] - rows // 2
     for i in range(rows):
-        y = silu(refs[i][...].astype(F32) * a + b)
         inside = jnp.logical_and(first + i >= 0, first + i < image_rows)
-        cols = y.shape[0]
-        out_ref[i * cols : (i + 1) * cols, :] = jnp.where(inside, y, 0.0).astype(BF16)
+        for h in range(halves):
+            lanes = slice(h * half, (h + 1) * half)
+            y = silu(x_ref[h, i].astype(F32) * a[:, lanes] + b[:, lanes])
+            out_ref[h, i * cols : (i + 1) * cols, :] = jnp.where(inside, y, 0.0).astype(BF16)
 
 
 def conv_two_kernel(cols, rows, image_rows, at_ref, x_ref, res_ref, bias_ref, w_ref, out_ref, S, acc):
@@ -115,11 +117,14 @@
                 put_shifted(S, i, cols, y, slice(h * outs, (h + 1) * outs))
         acc[...] = jnp.broadcast_to(bias_ref[...], acc.shape)
 
-    start = pl.multiple_of((t // 3) * cols, cols)
-    piece = w_ref[...].reshape(-1, outs)
-    acc[...] += jnp.dot(S[t % 3, pl.ds(start, rows * cols), :], piece, preferred_element_type=F32)
-
-    @pl.when(t == 8)
+    start = pl.multiple_of(t * cols, cols)
+    total = acc[...]
+    for k in range(3):
+        piece = w_ref[:, k].reshape(-1, outs)
+        total += jnp.dot(S[k, pl.ds(start, rows * cols), :], piece, preferred_element_type=F32)
+    acc[...] = total
+
+    @pl.when(t == 2)
     def _():
         first = at_ref[0] - rows // 2
         for i in range(rows):
@@ -141,16 +146,19 @@
                 put_shifted(S, i, cols, y, slice(h * outs, (h + 1) * outs))
         acc[...] = jnp.broadcast_to(bias_ref[...][None], acc.shape)
 
-    a, c = t // 3, t % 3
-    piece = w_ref[...].reshape(-1, outs)
     for p in range(2):
+        start = pl.multiple_of(((t + 1 + p) // 2) * cols, cols)
         for q in range(2):
-            start = pl.multiple_of(((a + 1 + p) // 2) * cols, cols)
-            acc[2 * p + q] += jnp.dot(
-                S[(c + 1 + q) // 2, pl.ds(start, cols), :], piece, preferred_element_type=F32
-            )
-
-    @pl.when(t == 8)
+            total = acc[2 * p + q]
+            for k in range(3):
+                total += jnp.dot(
+                    S[(k + 1 + q) // 2, pl.ds(start, cols), :],
+                    w_ref[:, k].reshape(-1, outs),
+                    preferred_element_type=F32,
+                )
+            acc[2 * p + q] = total
+
+    @pl.when(t == 2)
     def _():
         for p in range(2):
             for q in range(2):
@@ -170,7 +178,7 @@
 
 def weight_spec(gathered, base):
     n, _, rows, outs = gathered.shape
-    return pl.BlockSpec((n, 1, rows, outs), lambda t: (0, base + t, 0, 0))
+    return pl.BlockSpec((n, 3, rows, outs), lambda t: (0, base + t, 0, 0))
 
 
 def on_device(
@@ -229,7 +237,7 @@
     hold = lax.all_to_all(jnp.broadcast_to(hold, (nx, 27, k_own, half)), "x", 0, 0, tiled=True)
     hold = hold.transpose(1, 0, 2, 3).reshape(27, nx * k_own, half)
     weights = lax.all_gather(hold[9:], ("zh", "zl"))
-    weights_one = lax.all_gather(hold[:9], "zh")
+    hold_one = hold[:9]
 
     own = features[0]
     wide = own.astype(F32)
@@ -239,24 +247,29 @@
     sums = jnp.dot(sums, member, precision=HIGHEST).reshape(1, 2 * G)
     sums = jnp.pad(sums, ((0, 0), (0, 128 - 2 * G)))
     sums = jnp.sum(sum_over(sums, ("x", "col")), axis=0, keepdims=True)
+
+    up_row, down_row = shifted_rows(own, ROW, -1), shifted_rows(own, ROW, 1)
+    edge = jnp.where(zl == 0, up_row, down_row)
+    sent = moved(jnp.concatenate([own, edge]), move_one)
+    sent = sent.reshape(2, breadth, nzl, depth).transpose(2, 0, 1, 3)
+    sent = jnp.broadcast_to(sent[:, None], (nzl, ncol, 2, breadth, depth))
+    sent = sent.reshape(nzl * ncol, 2, breadth, depth)
+    quad = lax.all_to_all(sent, ("zl", "col"), 0, 0, tiled=True)
+
+    sums, hold_one, quad = lax.optimization_barrier((sums, hold_one, quad))
     sums = sum_over(sums, ("zh", "zl"))
-
-    up_row, down_row = shifted_rows(own, ROW, -1), shifted_rows(own, ROW, 1)
-    three = lax.all_gather(jnp.stack([up_row, own, down_row]), "col", axis=1, tiled=True)
-    residual = own_half(moved(three.reshape(3 * cols, channels), move))
-    edge = jnp.where(zl == 0, three[0], three[2])
-    sent = moved(jnp.concatenate([three[1], edge]), move_one)
-    sent = sent.reshape(2, cols, nzl, depth).transpose(2, 0, 1, 3)
-    quad = lax.all_to_all(sent, "zl", 0, 0, tiled=True)
+    weights_one = lax.all_gather(hold_one, "zh")
+    quad = quad.reshape(nzl, ncol, 2, breadth, depth)
 
     def own_depth(v):
         return lax.dynamic_slice_in_dim(v, zl * depth, depth, 1)
 
     gain_one = own_depth(order(first_gain, (2, 1, 0)))
     shift_one = own_depth(order(first_shift, (2, 1, 0)))
-    vectors = order(jnp.stack([first_bias, second_gain, second_shift, second_bias]), (1, 2, 0))
-    vectors = own_half(jnp.concatenate([vectors, upsample_bias[None]]))
-    bias_one, gain_two, shift_two, bias_two, bias_up = [vectors[i : i + 1] for i in range(5)]
+    vectors = order(jnp.stack([second_gain, second_shift, first_bias, second_bias]), (1, 2, 0))
+    gain_two, shift_two = vectors[:1], vectors[1:2]
+    vectors = own_half(jnp.concatenate([vectors[2:], upsample_bias[None]]))
+    bias_one, bias_two, bias_up = [vectors[i : i + 1] for i in range(3)]
 
     def picks(group, groups):
         pick = group[:, None] == jnp.arange(128)[None, :]
@@ -264,12 +277,14 @@
 
     lane = jnp.arange(depth)
     pick_one = picks(lane // k_own % nx * nzh + lane // (k_own * nx), G)
-    lane = jnp.arange(half)
-    pick = picks(lane // (k_own * nx * nzl) * nx + lane // k_own % nx, G // ncol)
+    lane = jnp.arange(channels)
+    group = lane // (k_own * nx * nzl) * nx + lane // k_own % nx
+    pick_two = picks(group, G)
+    pick_own = picks(group[:half] + c * (G // ncol), G)
 
     parts = pl.pallas_call(
         functools.partial(conv_one_kernel, cols, image_rows, count),
-        out_shape=jax.ShapeDtypeStruct((nzl, cols, half), F32),
+        out_shape=jax.ShapeDtypeStruct((nzl, cols, half), BF16),
         in_specs=[SM] + [VM] * 6,
         out_specs=VM,
         scratch_shapes=[pltpu.VMEM(((nzl + 2) * cols, 3 * depth), BF16)],
@@ -285,24 +300,27 @@
         in_specs=[VM] * 3,
         out_specs=(VM, VM),
         name="join_one",
-    )(parts, bias_one, pick)
-
-    stats = jnp.sum(sum_over(sums_two[:1], ("x", "zl")), axis=0, keepdims=True)
+    )(parts, bias_one, pick_own)
+
+    stats = jnp.sum(sum_over(sums_two[:1], ("x", "zl", "col")), axis=0, keepdims=True)
+    hidden, three, stats = lax.optimization_barrier((hidden, jnp.stack([up_row, own, down_row]), stats))
     stats = sum_over(stats, "zh")
-    five = [hidden if d == 0 else shifted_rows(hidden, ROW, d) for d in range(-2, 3)]
+    five = jnp.stack([shifted_rows(hidden, ROW, d) if d else hidden for d in range(-2, 3)])
+    five = lax.all_gather(five, "col")
+    three = lax.all_gather(three, "col", axis=1, tiled=True)
+    residual = own_half(moved(three.reshape(3 * cols, channels), move))
     normed = pl.pallas_call(
-        functools.partial(norm_kernel, 5, image_rows, count),
-        out_shape=jax.ShapeDtypeStruct((5 * cols, half), BF16),
-        in_specs=[SM] + [VM] * 9,
+        functools.partial(norm_kernel, image_rows, count),
+        out_shape=jax.ShapeDtypeStruct((ncol, 5 * cols, half), BF16),
+        in_specs=[SM] + [VM] * 5,
         out_specs=VM,
         name="norm_two",
-    )(at, *five, stats, gain_two, shift_two, pick)
-    normed = lax.all_gather(normed, "col")
+    )(at, five, stats, gain_two, shift_two, pick_two)
 
     rows = 3
     block = pl.pallas_call(
         functools.partial(conv_two_kernel, cols, rows, image_rows),
-        grid=(9,),
+        grid=(3,),
         out_shape=jax.ShapeDtypeStruct((rows * cols, half), BF16),
         in_specs=[SM, VM, VM, VM, weight_spec(weights, 0)],
         out_specs=VM,
@@ -316,9 +334,9 @@
 
     up = pl.pallas_call(
         functools.partial(conv_up_kernel, cols),
-        grid=(9,),
+        grid=(3,),
         out_shape=jax.ShapeDtypeStruct((ncol, 2, cols, half), BF16),
-        in_specs=[VM, VM, weight_spec(weights, 9)],
+        in_specs=[VM, VM, weight_spec(weights, 3)],
         out_specs=VM,
         scratch_shapes=[
             pltpu.VMEM((3, 3 * cols, channels), BF16),

time: 281 us -> 267 us (0.950)
  waiting for transfers between devices: 55 us -> 35 us
  starting transfers between devices: 91.6 us -> 104 us
  Pallas kernels: 22.6 us -> 17.1 us
    all_to_all x4, waiting for transfers between devices: 41.3 us -> 22.4 us  [sum_over(): return lax.all_to_all(sent, axes, 0, 0, tiled=True)]
    all_to_all x4, starting transfers between devices: 67.1 us -> 82.5 us  [sum_over(): return lax.all_to_all(sent, axes, 0, 0, tiled=True)]
    all_to_all x1, waiting for transfers between devices: 13.7 us -> 4.82 us  [on_device(): parts = lax.all_to_all(parts, 'zl', 0, 0, tiled=True)]
    all_to_all x1, waiting for transfers between devices: 0.01 us -> 7.65 us  [on_device(): quad = lax.all_to_all(sent, ('zl', 'col'), 0, 0, tiled=True)]
    all_gather x3, blocking collectives: 59.7 us -> 54.3 us  [the longest x1 48 us: on_device(): weights_one = lax.all_gather(hold_one, 'zh')]
    all_gather x1, blocking collectives: 3.7 us -> 6.76 us  [on_device(): block = lax.all_gather(block, 'col')]
    pallas_call x1, Pallas kernels: 7.53 us -> 4.52 us  [on_device(): pl.pallas_call(functools.partial(conv_two_kernel, cols, rows, image_rows)...]
  transfers between devices with their start and end apart: 13 -> 13, of which waited for: 4 -> 5; matrix products, arithmetic and copies ran while one was open for 4% -> 5% of each run, Pallas kernels for 3% -> 3%
where the time goes in v3:
time: 267 us; the launch traced here: 266 us
  starting transfers between devices  104 us (39%)
  blocking collectives  76 us (28%)
  waiting for transfers between devices  35 us (13%)
  Pallas kernels  17.1 us (6%)
  local copies, waits for them, and re-layouts  15.5 us (6%)
  between operations  14 us (5%)
  other arithmetic  3.14 us (1%)
    all_to_all x4, starting transfers between devices, sum_over(): return lax.all_to_all(sent, axes, 0, 0, tiled=True)  82.5 us
    all_gather x1, blocking collectives, on_device(): weights_one = lax.all_gather(hold_one, 'zh')  48 us
    all_to_all x4, waiting for transfers between devices, sum_over(): return lax.all_to_all(sent, axes, 0, 0, tiled=True)  22.4 us
    ppermute x6, starting transfers between devices, shifted_rows(): return lax.ppermute(values, axis, pairs)  12.8 us
    all_to_all x1, blocking collectives, on_device(): lax.all_to_all(jnp.broadcast_to(hold, (nx, 27, k_own, half)), 'x', 0, 0,...  10.2 us
    all_to_all x1, waiting for transfers between devices, on_device(): quad = lax.all_to_all(sent, ('zl', 'col'), 0, 0, tiled=True)  7.65 us
    all_gather x1, blocking collectives, on_device(): block = lax.all_gather(block, 'col')  6.76 us
  transfers between devices with their start and end apart: 13, of which 5 were waited for; matrix products, arithmetic and copies ran while one was open for 5% of the time, Pallas kernels for 3%

profile of v3, /device:TPU:33, one launch (start us, length us, event | category | flops | bytes accessed | tf_op | source)
XLA Modules:
  0.0 266.0 jit_solution(15373850187696670097)
XLA Ops:
  9.4 10.2 %all_to_all.48 = bf16[4,27,4,256]{3,2,1,0:T(4,128)(2,1)S(1)} all-to-all(bf16[4,27,4,256]{3,2,1,0:T(4,128)(2,1)S(1)} %broadcast_in_dim.26), channel_id=1, replica_groups=mesh['img'=2,'x'=4,'zh'=8,'zl'=4,'col'=2] {'x'}, dimensions={0} | all-to-all | bytes 442368 | tf_op jit(solution)/shard_map/all_to_all | solution.py:237
  20.5 4.4 %collective-permute-start = (bf16[64,512]{1,0:T(8,128)(2,1)S(1)}, bf16[64,512]{1,0:T(8,128)(2,1)S(1)}, u32[]{:S(2)}, u32[]{:S(2)}) collective-permute-start(bf16[64,512]{1,0:T(8,128)(2,1)S(1)} %bitcast.65), channel_id=1, source_target_pairs={{0,2},{2,4},{4,6},{6,8},{8,10},{10,12},{12,14},{14,16},{16,18},{18... | collective-permute-start | bytes 196616 | tf_op jit(solution)/shard_map/ppermute | solution.py:28
  27.5 46.9 %all-to-all-start = ((f32[8,1,128]{2,1,0:T(1,128)}), f32[8,1,128]{2,1,0:T(1,128)S(1)}, u32[]{:S(2)}, u32[]{:S(2)}) async-start(f32[8,1,128]{2,1,0:T(1,128)} %broadcast_in_dim.23), calls=%async_computation | async-start | bytes 8192 | tf_op jit(solution)/shard_map/all_to_all | solution.py:22
  75.0 4.0 %all-to-all-done = f32[8,1,128]{2,1,0:T(1,128)S(1)} async-done(((f32[8,1,128]{2,1,0:T(1,128)}), f32[8,1,128]{2,1,0:T(1,128)S(1)}, u32[]{:S(2)}, u32[]{:S(2)}) %all-to-all-start) | async-done | bytes 4128 | tf_op jit(solution)/shard_map/all_to_all | solution.py:22
  79.7 4.0 %all-to-all-start.2 = ((bf16[8,2,64,128]{3,2,1,0:T(8,128)(2,1)}), bf16[8,2,64,128]{3,2,1,0:T(8,128)(2,1)S(1)}, u32[]{:S(2)}, u32[]{:S(2)}) async-start(bf16[8,2,64,128]{3,2,1,0:T(8,128)(2,1)} %bitcast.9), calls=%async_computation.2 | async-start | bytes 524288 | tf_op jit(solution)/shard_map/all_to_all | solution.py:257
  86.6 7.7 %all-to-all-done.2 = bf16[8,2,64,128]{3,2,1,0:T(8,128)(2,1)S(1)} async-done(((bf16[8,2,64,128]{3,2,1,0:T(8,128)(2,1)}), bf16[8,2,64,128]{3,2,1,0:T(8,128)(2,1)S(1)}, u32[]{:S(2)}, u32[]{:S(2)}) %all-to-all-start.2) | async-done | bytes 262176 | tf_op jit(solution)/shard_map/all_to_all | solution.py:257
  94.9 6.8 %all-to-all-start.3 = ((f32[32,1,128]{2,1,0:T(1,128)}), f32[32,1,128]{2,1,0:T(1,128)S(1)}, u32[]{:S(2)}, u32[]{:S(2)}) async-start(f32[32,1,128]{2,1,0:T(1,128)} %broadcast_in_dim.28), calls=%async_computation.3 | async-start | bytes 32768 | tf_op jit(solution)/shard_map/all_to_all | solution.py:22
  101.7 48.0 %all-gather = bf16[72,16,256]{2,1,0:T(8,128)(2,1)} all-gather(bf16[9,16,256]{2,1,0:T(8,128)(2,1)S(1)} %slice.70), channel_id=2, replica_groups=mesh['img'=2,'x'=4,'zh'=8,'zl'=4,'col'=2] {'zh'}, dimensions={0}, use_global_device_ids=true | all-gather | bytes 663552 | tf_op jit(solution)/shard_map/all_gather | solution.py:261
  150.3 3.0 %conv_one.1 = bf16[4,128,256]{2,1,0:T(8,128)(2,1)} custom-call(s32[1]{0:T(128)} %bitcast.at_ref, bf16[4,2,2,64,128]{4,3,2,1,0:T(8,128)(2,1)} %bitcast.54, f32[32,128]{1,0:T(8,128)} %bitcast.69, f32[1,128]{1,0:T(1,128)} %get-tuple-element.37.gain_ref, f32[1,128]{1,0:T(1,128)} %get-tuple-element.36.shift_ref, f32[256,128]{1,0:T(8,128)} %add_convert_fusion.2.pick_ref, ...), custom_call_target="tpu_custom_call" | custom-call | tf_op jit(solution)/shard_map/conv_one/pallas_call | solution.py:285
  153.3 4.4 %all-to-all-start.4 = ((bf16[4,128,256]{2,1,0:T(8,128)(2,1)}), bf16[4,128,256]{2,1,0:T(8,128)(2,1)S(1)}, u32[]{:S(2)}, u32[]{:S(2)}) async-start(bf16[4,128,256]{2,1,0:T(8,128)(2,1)} %conv_one.1), calls=%async_computation.4 | async-start | bytes 524288 | tf_op jit(solution)/shard_map/all_to_all | solution.py:293
  160.1 4.8 %all-to-all-done.4.x_ref = bf16[4,128,256]{2,1,0:T(8,128)(2,1)S(1)} async-done(((bf16[4,128,256]{2,1,0:T(8,128)(2,1)}), bf16[4,128,256]{2,1,0:T(8,128)(2,1)S(1)}, u32[]{:S(2)}, u32[]{:S(2)}) %all-to-all-start.4) | async-done | bytes 262176 | tf_op jit(solution)/shard_map/all_to_all | solution.py:293
  168.9 13.2 %all-to-all-start.5 = ((f32[32,1,128]{2,1,0:T(1,128)}), f32[32,1,128]{2,1,0:T(1,128)S(1)}, u32[]{:S(2)}, u32[]{:S(2)}) async-start(f32[32,1,128]{2,1,0:T(1,128)} %broadcast_in_dim.59), calls=%async_computation.5 | async-start | bytes 32768 | tf_op jit(solution)/shard_map/all_to_all | solution.py:22
  184.5 5.0 %all-to-all-done.5 = f32[32,1,128]{2,1,0:T(1,128)S(1)} async-done(((f32[32,1,128]{2,1,0:T(1,128)}), f32[32,1,128]{2,1,0:T(1,128)S(1)}, u32[]{:S(2)}, u32[]{:S(2)}) %all-to-all-start.5) | async-done | bytes 16416 | tf_op jit(solution)/shard_map/all_to_all | solution.py:22
  189.5 2.1 collective-permute-start.2
  191.6 2.4 collective-permute-start.3
  197.2 15.6 %all-to-all-start.6 = ((f32[8,1,128]{2,1,0:T(1,128)}), f32[8,1,128]{2,1,0:T(1,128)S(1)}, u32[]{:S(2)}, u32[]{:S(2)}) async-start(f32[8,1,128]{2,1,0:T(1,128)} %broadcast_in_dim.61), calls=%async_computation.6 | async-start | bytes 8192 | tf_op jit(solution)/shard_map/all_to_all | solution.py:22
  212.8 3.8 %all_gather.31 = bf16[3,128,512]{2,1,0:T(8,128)(2,1)S(1)} all-gather(bf16[3,64,512]{2,1,0:T(8,128)(2,1)S(1)} %pad_maximum_fusion), channel_id=1, replica_groups=mesh['img'=2,'x'=4,'zh'=8,'zl'=4,'col'=2] {'col'}, dimensions={1}, use_global_device_ids=true | all-gather | bytes 589824 | tf_op jit(solution)/shard_map/all_gather | solution.py:310
  217.9 2.5 all-gather.1
  220.3 13.5 %all-to-all-done.6 = f32[8,1,128]{2,1,0:T(1,128)S(1)} async-done(((f32[8,1,128]{2,1,0:T(1,128)}), f32[8,1,128]{2,1,0:T(1,128)S(1)}, u32[]{:S(2)}, u32[]{:S(2)}) %all-to-all-start.6) | async-done | bytes 4128 | tf_op jit(solution)/shard_map/all_to_all | solution.py:22
  234.4 3.1 %norm_two.1.x_ref = bf16[2,640,256]{2,1,0:T(8,128)(2,1)} custom-call(s32[1]{0:T(128)} %bitcast.at_ref, bf16[2,5,128,256]{3,2,1,0:T(8,128)(2,1)} %bitcast.49, f32[8,128]{1,0:T(8,128)} %bitcast.71, f32[1,512]{1,0:T(1,128)} %slice.82.gain_ref, f32[1,512]{1,0:T(1,128)} %slice.84.shift_ref, f32[1024,128]{1,0:T(8,128)} %add_convert_fusion.pick_ref), custom_call_target="tpu_custom_call" | custom-call | tf_op jit(solution)/shard_map/norm_two/pallas_call | solution.py:312
  237.5 4.5 %conv_two.1 = bf16[384,256]{1,0:T(8,128)(2,1)} custom-call(s32[1]{0:T(128)} %bitcast.at_ref, bf16[2,640,256]{2,1,0:T(8,128)(2,1)} %norm_two.1.x_ref, bf16[384,256]{1,0:T(8,128)(2,1)} %dynamic-slice_convert_fusion.res_ref, f32[1,256]{1,0:T(1,128)} %get-tuple-element.26.bias_ref, bf16[32,18,16,256]{3,2,1,0:T(8,128)(2,1)} %all-gather.5.cloned.1.call-done.w_ref), custom_call_target="tpu_custom_call" | custom-call | tf_op jit(solution)/shard_map/conv_two/pallas_call | solution.py:321
  242.1 6.8 %all-gather.2 = bf16[768,256]{1,0:T(8,128)(2,1)} all-gather(bf16[384,256]{1,0:T(8,128)(2,1)} %conv_two.1), channel_id=4, replica_groups=mesh['img'=2,'x'=4,'zh'=8,'zl'=4,'col'=2] {'col'}, dimensions={0}, use_global_device_ids=true | all-gather | bytes 589824 | tf_op jit(solution)/shard_map/all_gather | solution.py:333
  248.8 4.5 %conv_up.1 = bf16[2,2,128,256]{3,2,1,0:T(8,128)(2,1)} custom-call(bf16[2,384,256]{2,1,0:T(8,128)(2,1)} %bitcast.51, f32[1,256]{1,0:T(1,128)} %get-tuple-element.25.bias_ref, bf16[32,18,16,256]{3,2,1,0:T(8,128)(2,1)} %all-gather.5.cloned.1.call-done.w_ref), custom_call_target="tpu_custom_call" | custom-call | tf_op jit(solution)/shard_map/conv_up/pallas_call | solution.py:335
  253.4 4.8 %all_to_all.49 = bf16[2,2,128,256]{3,2,1,0:T(8,128)(2,1)S(1)} all-to-all(bf16[2,2,128,256]{3,2,1,0:T(8,128)(2,1)} %conv_up.1), channel_id=1, replica_groups=mesh['img'=2,'x'=4,'zh'=8,'zl'=4,'col'=2] {'col'}, dimensions={0} | all-to-all | bytes 524288 | tf_op jit(solution)/shard_map/all_to_all | solution.py:348
  (118 shorter events, 26.1 us)
Async XLA Ops:
  6.5 14.0 %copy-start.2 = (bf16[1,64,512]{2,1,0:T(8,128)(2,1)S(1)}, bf16[1,64,512]{2,1,0:T(8,128)(2,1)}, u32[]{:S(2)}) copy-start(bf16[1,64,512]{2,1,0:T(8,128)(2,1)} %param.11) | copy-start | bytes 196612
  6.5 231.0 %all-gather.5.cloned.1.call-start = ((), (), s32[]{:S(2)}) async-start(), calls=%async_computation.8 | async-start | bytes 4866048 | tf_op jit(solution)/shard_map/all_gather | solution.py:239
  20.5 53.9 %collective-permute-start = (bf16[64,512]{1,0:T(8,128)(2,1)S(1)}, bf16[64,512]{1,0:T(8,128)(2,1)S(1)}, u32[]{:S(2)}, u32[]{:S(2)}) collective-permute-start(bf16[64,512]{1,0:T(8,128)(2,1)S(1)} %bitcast.65), channel_id=1, source_target_pairs={{0,2},{2,4},{4,6},{6,8},{8,10},{10,12},{12,14},{14,16},{16,18},{18... | collective-permute-start | bytes 196616 | tf_op jit(solution)/shard_map/ppermute | solution.py:28
  25.0 49.4 %collective-permute-start.1 = (bf16[64,512]{1,0:T(8,128)(2,1)S(1)}, bf16[64,512]{1,0:T(8,128)(2,1)S(1)}, u32[]{:S(2)}, u32[]{:S(2)}) collective-permute-start(bf16[64,512]{1,0:T(8,128)(2,1)S(1)} %bitcast.66), channel_id=1, source_target_pairs={{2,0},{4,2},{6,4},{8,6},{10,8},{12,10},{14,12},{16,14},{18,16},{20... | collective-permute-start | bytes 196616 | tf_op jit(solution)/shard_map/ppermute | solution.py:28
  27.5 51.5 %all-to-all-start = ((f32[8,1,128]{2,1,0:T(1,128)}), f32[8,1,128]{2,1,0:T(1,128)S(1)}, u32[]{:S(2)}, u32[]{:S(2)}) async-start(f32[8,1,128]{2,1,0:T(1,128)} %broadcast_in_dim.23), calls=%async_computation | async-start | bytes 8192 | tf_op jit(solution)/shard_map/all_to_all | solution.py:22
  74.4 9.3 %copy-start.6 = (f32[512]{0:T(512)S(1)}, f32[512]{0:T(512)}, u32[]{:S(2)}) copy-start(f32[512]{0:T(512)} %param.12) | copy-start | bytes 6148
  74.4 9.6 %copy-start.7 = (f32[512]{0:T(512)S(1)}, f32[512]{0:T(512)}, u32[]{:S(2)}) copy-start(f32[512]{0:T(512)} %param.13) | copy-start | bytes 6148
  74.5 10.1 %copy-start.8 = (f32[512]{0:T(512)S(1)}, f32[512]{0:T(512)}, u32[]{:S(2)}) copy-start(f32[512]{0:T(512)} %param.16) | copy-start | bytes 6148
  74.5 10.2 %copy-start.9 = (f32[512]{0:T(512)S(1)}, f32[512]{0:T(512)}, u32[]{:S(2)}) copy-start(f32[512]{0:T(512)} %param.17) | copy-start | bytes 6148
  74.5 10.4 %copy-start.10 = (f32[512]{0:T(512)S(1)}, f32[512]{0:T(512)}, u32[]{:S(2)}) copy-start(f32[512]{0:T(512)} %param.15) | copy-start | bytes 6148
  74.5 10.5 %copy-start.11 = (f32[512]{0:T(512)S(1)}, f32[512]{0:T(512)}, u32[]{:S(2)}) copy-start(f32[512]{0:T(512)} %param.19) | copy-start | bytes 6148
  74.9 83.7 %copy-start.12 = (f32[512]{0:T(512)S(1)}, f32[512]{0:T(512)}, u32[]{:S(2)}) copy-start(f32[512]{0:T(512)} %param.21) | copy-start | bytes 6148
  79.7 14.5 %all-to-all-start.2 = ((bf16[8,2,64,128]{3,2,1,0:T(8,128)(2,1)}), bf16[8,2,64,128]{3,2,1,0:T(8,128)(2,1)S(1)}, u32[]{:S(2)}, u32[]{:S(2)}) async-start(bf16[8,2,64,128]{3,2,1,0:T(8,128)(2,1)} %bitcast.9), calls=%async_computation.2 | async-start | bytes 524288 | tf_op jit(solution)/shard_map/all_to_all | solution.py:257
  94.2 55.5 %copy-start.1 = (bf16[8,2,64,128]{3,2,1,0:T(8,128)(2,1)}, bf16[8,2,64,128]{3,2,1,0:T(8,128)(2,1)S(1)}, u32[]{:S(2)}) copy-start(bf16[8,2,64,128]{3,2,1,0:T(8,128)(2,1)S(1)} %all-to-all-done.2) | copy-start | bytes 786436
  94.9 54.8 %all-to-all-start.3 = ((f32[32,1,128]{2,1,0:T(1,128)}), f32[32,1,128]{2,1,0:T(1,128)S(1)}, u32[]{:S(2)}, u32[]{:S(2)}) async-start(f32[32,1,128]{2,1,0:T(1,128)} %broadcast_in_dim.28), calls=%async_computation.3 | async-start | bytes 32768 | tf_op jit(solution)/shard_map/all_to_all | solution.py:22
  153.3 11.7 %all-to-all-start.4 = ((bf16[4,128,256]{2,1,0:T(8,128)(2,1)}), bf16[4,128,256]{2,1,0:T(8,128)(2,1)S(1)}, u32[]{:S(2)}, u32[]{:S(2)}) async-start(bf16[4,128,256]{2,1,0:T(8,128)(2,1)} %conv_one.1), calls=%async_computation.4 | async-start | bytes 524288 | tf_op jit(solution)/shard_map/all_to_all | solution.py:293
  165.0 0.7 copy-start
  168.9 20.6 %all-to-all-start.5 = ((f32[32,1,128]{2,1,0:T(1,128)}), f32[32,1,128]{2,1,0:T(1,128)S(1)}, u32[]{:S(2)}, u32[]{:S(2)}) async-start(f32[32,1,128]{2,1,0:T(1,128)} %broadcast_in_dim.59), calls=%async_computation.5 | async-start | bytes 32768 | tf_op jit(solution)/shard_map/all_to_all | solution.py:22
  183.0 34.8 %copy-start.4 = (bf16[128,256]{1,0:T(8,128)(2,1)S(1)}, bf16[128,256]{1,0:T(8,128)(2,1)}, u32[]{:S(2)}) copy-start(bf16[128,256]{1,0:T(8,128)(2,1)} %get-tuple-element.18) | copy-start | bytes 196612
  189.5 28.3 %collective-permute-start.2 = (bf16[128,256]{1,0:T(8,128)(2,1)}, bf16[128,256]{1,0:T(8,128)(2,1)S(1)}, u32[]{:S(2)}, u32[]{:S(2)}) collective-permute-start(bf16[128,256]{1,0:T(8,128)(2,1)} %get-tuple-element.18), channel_id=1, source_target_pairs={{0,4},{2,6},{4,8},{6,10},{8,12},{10,14},{12,16},{14,18},{16,20},{1... | collective-permute-start | bytes 196616 | tf_op jit(solution)/shard_map/ppermute | solution.py:28
  191.6 26.1 %collective-permute-start.3 = (bf16[128,256]{1,0:T(8,128)(2,1)}, bf16[128,256]{1,0:T(8,128)(2,1)S(1)}, u32[]{:S(2)}, u32[]{:S(2)}) collective-permute-start(bf16[128,256]{1,0:T(8,128)(2,1)} %get-tuple-element.18), channel_id=1, source_target_pairs={{0,2},{2,4},{4,6},{6,8},{8,10},{10,12},{12,14},{14,16},{16,18},{18... | collective-permute-start | bytes 196616 | tf_op jit(solution)/shard_map/ppermute | solution.py:28
  194.0 23.8 %collective-permute-start.4 = (bf16[128,256]{1,0:T(8,128)(2,1)}, bf16[128,256]{1,0:T(8,128)(2,1)S(1)}, u32[]{:S(2)}, u32[]{:S(2)}) collective-permute-start(bf16[128,256]{1,0:T(8,128)(2,1)} %get-tuple-element.18), channel_id=1, source_target_pairs={{2,0},{4,2},{6,4},{8,6},{10,8},{12,10},{14,12},{16,14},{18,16},{20... | collective-permute-start | bytes 196616 | tf_op jit(solution)/shard_map/ppermute | solution.py:28
  195.3 22.5 %collective-permute-start.5 = (bf16[128,256]{1,0:T(8,128)(2,1)}, bf16[128,256]{1,0:T(8,128)(2,1)S(1)}, u32[]{:S(2)}, u32[]{:S(2)}) collective-permute-start(bf16[128,256]{1,0:T(8,128)(2,1)} %get-tuple-element.18), channel_id=1, source_target_pairs={{4,0},{6,2},{8,4},{10,6},{12,8},{14,10},{16,12},{18,14},{20,16},{2... | collective-permute-start | bytes 196616 | tf_op jit(solution)/shard_map/ppermute | solution.py:28
  197.2 36.6 %all-to-all-start.6 = ((f32[8,1,128]{2,1,0:T(1,128)}), f32[8,1,128]{2,1,0:T(1,128)S(1)}, u32[]{:S(2)}, u32[]{:S(2)}) async-start(f32[8,1,128]{2,1,0:T(1,128)} %broadcast_in_dim.61), calls=%async_computation.6 | async-start | bytes 8192 | tf_op jit(solution)/shard_map/all_to_all | solution.py:22
  (2 other events, 1.2 us)
Sparse Core Ops, SparseCore 0:
  20.7 162.2 all-gather.4

commit v4 on v3

--- a/solution.py
+++ b/solution.py
@@ -28,6 +28,11 @@
     return lax.ppermute(values, axis, pairs)
 
 
+def fetch(count, by):
+    above = [(2 * (i - by), 2 * i) for i in range(by, count)]
+    return above + [(2 * (i + by) + 1, 2 * i + 1) for i in range(count - by)]
+
+
 def put_shifted(S, row, cols, y, lanes):
     at = pl.ds(row * cols, cols)
     column = lax.broadcasted_iota(jnp.int32, y.shape, 0)
@@ -40,8 +45,7 @@
     return u / (1.0 + jnp.exp(-u))
 
 
-def spread_stats(stats, pick, count, gain, shift):
-    totals = jnp.sum(stats, axis=0, keepdims=True)
+def spread_stats(totals, pick, count, gain, shift):
     totals = jnp.broadcast_to(totals, (8, totals.shape[1]))
     spread = lax.dot_general(
         totals, pick, (((1,), (1,)), ((), ())), precision=HIGHEST, preferred_element_type=F32
@@ -53,9 +57,10 @@
     return a, shift - mean * a
 
 
-def conv_one_kernel(cols, image_rows, count, at_ref, x_ref, stats_ref, gain_ref, shift_ref, pick_ref, w_ref, out_ref, S):
+def conv_one_kernel(cols, image_rows, count, at_ref, x_ref, gain_ref, shift_ref, pick_ref, w_ref, out_ref, S):
     quad, depth = x_ref.shape[0], x_ref.shape[4]
-    a, b = spread_stats(stats_ref[...], pick_ref[...], count, gain_ref[...], shift_ref[...])
+    totals = jnp.sum(w_ref[:, 9, :, :128].astype(F32).reshape(-1, 128), axis=0, keepdims=True)
+    a, b = spread_stats(totals, pick_ref[...], count, gain_ref[...], shift_ref[...])
     first = at_ref[0] // quad * quad - 1
     column = lax.broadcasted_iota(jnp.int32, (cols, depth), 0)
     for i in range(quad + 2):
@@ -93,16 +98,18 @@
     sums_ref[...] = jnp.dot(both, pick_ref[...], precision=HIGHEST, preferred_element_type=F32)
 
 
-def norm_kernel(image_rows, count, at_ref, x_ref, stats_ref, gain_ref, shift_ref, pick_ref, out_ref):
-    a, b = spread_stats(stats_ref[...], pick_ref[...], count, gain_ref[...], shift_ref[...])
-    halves, rows, cols, half = x_ref.shape
-    first = at_ref[0] - rows // 2
-    for i in range(rows):
-        inside = jnp.logical_and(first + i >= 0, first + i < image_rows)
+def norm_kernel(image_rows, count, at_ref, own_ref, far_ref, stats_ref, gain_ref, shift_ref, pick_ref, out_ref):
+    totals = jnp.sum(stats_ref[...], axis=0, keepdims=True)
+    a, b = spread_stats(totals, pick_ref[...], count, gain_ref[...], shift_ref[...])
+    halves, cols, half = own_ref.shape
+    for d in range(-2, 3):
+        row = at_ref[0] + d
+        inside = jnp.logical_and(row >= 0, row < image_rows)
         for h in range(halves):
             lanes = slice(h * half, (h + 1) * half)
-            y = silu(x_ref[h, i].astype(F32) * a[:, lanes] + b[:, lanes])
-            out_ref[h, i * cols : (i + 1) * cols, :] = jnp.where(inside, y, 0.0).astype(BF16)
+            x = far_ref[int(d > 0), abs(d) - 1, h] if d else own_ref[h]
+            y = silu(x.astype(F32) * a[:, lanes] + b[:, lanes])
+            out_ref[h, (d + 2) * cols : (d + 3) * cols, :] = jnp.where(inside, y, 0.0).astype(BF16)
 
 
 def conv_two_kernel(cols, rows, image_rows, at_ref, x_ref, res_ref, bias_ref, w_ref, out_ref, S, acc):
@@ -246,19 +253,22 @@
     sums = jnp.stack([jnp.sum(wide, axis=0), jnp.sum(wide * wide, axis=0)])
     sums = jnp.dot(sums, member, precision=HIGHEST).reshape(1, 2 * G)
     sums = jnp.pad(sums, ((0, 0), (0, 128 - 2 * G)))
-    sums = jnp.sum(sum_over(sums, ("x", "col")), axis=0, keepdims=True)
-
-    up_row, down_row = shifted_rows(own, ROW, -1), shifted_rows(own, ROW, 1)
-    edge = jnp.where(zl == 0, up_row, down_row)
+    sums = jnp.sum(sum_over(sums, ("x", "zl", "col")), axis=0, keepdims=True)
+    high = lax.reduce_precision(sums, 8, 7)
+    low = lax.reduce_precision(sums - high, 8, 7)
+    terms = jnp.concatenate([high, low, sums - high - low]).astype(BF16)
+    terms = jnp.pad(terms, ((0, nx * k_own - 3), (0, half - 128)))
+    weights_one = lax.all_gather(jnp.concatenate([hold_one, terms[None]]), "zh")
+
+    last = nx * nz - 1
+    pairs = [(i, i + 1) for i in range(nzl - 1, last, nzl)] + [(i, i - 1) for i in range(nzl, last, nzl)]
+    edge = lax.ppermute(own, ROW, pairs)
     sent = moved(jnp.concatenate([own, edge]), move_one)
     sent = sent.reshape(2, breadth, nzl, depth).transpose(2, 0, 1, 3)
     sent = jnp.broadcast_to(sent[:, None], (nzl, ncol, 2, breadth, depth))
     sent = sent.reshape(nzl * ncol, 2, breadth, depth)
     quad = lax.all_to_all(sent, ("zl", "col"), 0, 0, tiled=True)
 
-    sums, hold_one, quad = lax.optimization_barrier((sums, hold_one, quad))
-    sums = sum_over(sums, ("zh", "zl"))
-    weights_one = lax.all_gather(hold_one, "zh")
     quad = quad.reshape(nzl, ncol, 2, breadth, depth)
 
     def own_depth(v):
@@ -285,12 +295,14 @@
     parts = pl.pallas_call(
         functools.partial(conv_one_kernel, cols, image_rows, count),
         out_shape=jax.ShapeDtypeStruct((nzl, cols, half), BF16),
-        in_specs=[SM] + [VM] * 6,
+        in_specs=[SM] + [VM] * 5,
         out_specs=VM,
         scratch_shapes=[pltpu.VMEM(((nzl + 2) * cols, 3 * depth), BF16)],
         name="conv_one",
-    )(at, quad, sums, gain_one, shift_one, pick_one, weights_one)
+    )(at, quad, gain_one, shift_one, pick_one, weights_one)
+    parts, own = lax.optimization_barrier((parts, own))
     parts = lax.all_to_all(parts, "zl", 0, 0, tiled=True)
+    three = jnp.stack([shifted_rows(own, ROW, -1), own, shifted_rows(own, ROW, 1)])
     hidden, sums_two = pl.pallas_call(
         join_kernel,
         out_shape=(
@@ -303,19 +315,20 @@
     )(parts, bias_one, pick_own)
 
     stats = jnp.sum(sum_over(sums_two[:1], ("x", "zl", "col")), axis=0, keepdims=True)
-    hidden, three, stats = lax.optimization_barrier((hidden, jnp.stack([up_row, own, down_row]), stats))
+    both = lax.all_gather(hidden, "col")
     stats = sum_over(stats, "zh")
-    five = jnp.stack([shifted_rows(hidden, ROW, d) if d else hidden for d in range(-2, 3)])
-    five = lax.all_gather(five, "col")
+    far = jnp.stack([lax.ppermute(both, ROW + ("col",), fetch(nx * nz, d)) for d in (1, 2)])
+    far, three = lax.optimization_barrier((far, three))
+    far = lax.all_gather(far, "col")
     three = lax.all_gather(three, "col", axis=1, tiled=True)
     residual = own_half(moved(three.reshape(3 * cols, channels), move))
     normed = pl.pallas_call(
         functools.partial(norm_kernel, image_rows, count),
         out_shape=jax.ShapeDtypeStruct((ncol, 5 * cols, half), BF16),
-        in_specs=[SM] + [VM] * 5,
+        in_specs=[SM] + [VM] * 6,
         out_specs=VM,
         name="norm_two",
-    )(at, five, stats, gain_two, shift_two, pick_two)
+    )(at, both, far, stats, gain_two, shift_two, pick_two)
 
     rows = 3
     block = pl.pallas_call(
@@ -367,6 +380,7 @@
         P(None, None, ROW, None),
         P(),
     )
+
     return jax.shard_map(
         on_device,
         mesh=finer,

time: 267 us -> 244 us (0.914)
  starting transfers between devices: 104 us -> 90.6 us
  waiting for transfers between devices: 35 us -> 26.3 us
    all_to_all x4 -> x3, starting transfers between devices: 82.5 us -> 70.6 us  [sum_over(): return lax.all_to_all(sent, axes, 0, 0, tiled=True)]
    all_to_all x1, waiting for transfers between devices: 7.65 us -> 0.01 us  [on_device(): quad = lax.all_to_all(sent, ('zl', 'col'), 0, 0, tiled=True)]
    ppermute x6 -> x2, starting transfers between devices: 12.8 us -> 5.27 us  [shifted_rows(): return lax.ppermute(values, axis, pairs)]
    all_to_all x1, waiting for transfers between devices: 4.82 us -> 0.2 us  [on_device(): parts = lax.all_to_all(parts, 'zl', 0, 0, tiled=True)]
    all_to_all x4 -> x3, waiting for transfers between devices: 22.4 us -> 26 us  [sum_over(): return lax.all_to_all(sent, axes, 0, 0, tiled=True)]
    ppermute x0 -> x3, starting transfers between devices: none -> 3.27 us  [the longest x2 2.6 us: on_device(): lax.ppermute(both, ROW + ('col',), fetch(nx * nz, d))]
    all_to_all x1, starting transfers between devices: 4.44 us -> 7.43 us  [on_device(): parts = lax.all_to_all(parts, 'zl', 0, 0, tiled=True)]
    all_gather x2 -> x3, blocking collectives: 50.5 us -> 52 us  [the longest x1 39.2 us: on_device(): weights_one = lax.all_gather(jnp.concatenate([hold_one, terms[None]]), 'zh')]
  transfers between devices with their start and end apart: 13 -> 11, of which waited for: 5 -> 4; matrix products, arithmetic and copies ran while one was open for 5% -> 5% of each run, Pallas kernels for 3% -> 3%
where the time goes in v4:
time: 244 us; the launch traced here: 243 us
  starting transfers between devices  90.6 us (37%)
  blocking collectives  75.3 us (31%)
  waiting for transfers between devices  26.3 us (11%)
  Pallas kernels  17.1 us (7%)
  local copies, waits for them, and re-layouts  14.9 us (6%)
  between operations  13.9 us (6%)
  other arithmetic  3.2 us (1%)
    all_to_all x3, starting transfers between devices, sum_over(): return lax.all_to_all(sent, axes, 0, 0, tiled=True)  70.6 us
    all_gather x1, blocking collectives, on_device(): weights_one = lax.all_gather(jnp.concatenate([hold_one, terms[None]]), 'zh')  39.2 us
    all_to_all x3, waiting for transfers between devices, sum_over(): return lax.all_to_all(sent, axes, 0, 0, tiled=True)  26 us
    all_gather x1, blocking collectives, on_device(): both = lax.all_gather(hidden, 'col')  10.5 us
    all_to_all x1, blocking collectives, on_device(): lax.all_to_all(jnp.broadcast_to(hold, (nx, 27, k_own, half)), 'x', 0, 0,...  10.2 us
    all_to_all x1, starting transfers between devices, on_device(): parts = lax.all_to_all(parts, 'zl', 0, 0, tiled=True)  7.43 us
    all_gather x1, blocking collectives, on_device(): block = lax.all_gather(block, 'col')  5.58 us
    ppermute x2, starting transfers between devices, shifted_rows(): return lax.ppermute(values, axis, pairs)  5.27 us
  transfers between devices with their start and end apart: 11, of which 4 were waited for; matrix products, arithmetic and copies ran while one was open for 5% of the time, Pallas kernels for 3%

profile of v4, /device:TPU:33, one launch (start us, length us, event | category | flops | bytes accessed | tf_op | source)
XLA Modules:
  0.0 242.9 jit_solution(17450523315238148154)
XLA Ops:
  9.4 10.2 %all_to_all.40 = bf16[4,27,4,256]{3,2,1,0:T(4,128)(2,1)S(1)} all-to-all(bf16[4,27,4,256]{3,2,1,0:T(4,128)(2,1)S(1)} %broadcast_in_dim.21), channel_id=1, replica_groups=mesh['img'=2,'x'=4,'zh'=8,'zl'=4,'col'=2] {'x'}, dimensions={0} | all-to-all | bytes 442368 | tf_op jit(solution)/shard_map/all_to_all | solution.py:244
  22.4 50.4 %all-to-all-start.2 = ((f32[32,1,128]{2,1,0:T(1,128)}), f32[32,1,128]{2,1,0:T(1,128)S(1)}, u32[]{:S(2)}, u32[]{:S(2)}) async-start(f32[32,1,128]{2,1,0:T(1,128)} %broadcast_in_dim.22), calls=%async_computation.2 | async-start | bytes 32768 | tf_op jit(solution)/shard_map/all_to_all | solution.py:22
  73.4 6.6 %all-to-all-done.2 = f32[32,1,128]{2,1,0:T(1,128)S(1)} async-done(((f32[32,1,128]{2,1,0:T(1,128)}), f32[32,1,128]{2,1,0:T(1,128)S(1)}, u32[]{:S(2)}, u32[]{:S(2)}) %all-to-all-start.2) | async-done | bytes 16416 | tf_op jit(solution)/shard_map/all_to_all | solution.py:22
  80.7 4.0 %all-to-all-start = ((bf16[8,2,64,128]{3,2,1,0:T(8,128)(2,1)}), bf16[8,2,64,128]{3,2,1,0:T(8,128)(2,1)S(1)}, u32[]{:S(2)}, u32[]{:S(2)}) async-start(bf16[8,2,64,128]{3,2,1,0:T(8,128)(2,1)} %bitcast.3), calls=%async_computation | async-start | bytes 524288 | tf_op jit(solution)/shard_map/all_to_all | solution.py:270
  87.6 39.2 %all-gather = bf16[80,16,256]{2,1,0:T(8,128)(2,1)} all-gather(bf16[10,16,256]{2,1,0:T(8,128)(2,1)S(1)} %pad_maximum_fusion.2), channel_id=2, replica_groups=mesh['img'=2,'x'=4,'zh'=8,'zl'=4,'col'=2] {'zh'}, dimensions={0}, use_global_device_ids=true | all-gather | bytes 737280 | tf_op jit(solution)/shard_map/all_gather | solution.py:261
  127.5 3.0 %conv_one.1 = bf16[4,128,256]{2,1,0:T(8,128)(2,1)} custom-call(s32[1]{0:T(128)} %bitcast.at_ref, bf16[4,2,2,64,128]{4,3,2,1,0:T(8,128)(2,1)} %bitcast.52, f32[1,128]{1,0:T(1,128)} %get-tuple-element.36.gain_ref, f32[1,128]{1,0:T(1,128)} %get-tuple-element.35.shift_ref, f32[256,128]{1,0:T(8,128)} %add_convert_fusion.2.pick_ref, bf16[8,10,16,256]{3,2,1,0:T(8,128)(2,1)} %bitcast.47), custom_call_target="tpu_custom_call" | custom-call | tf_op jit(solution)/shard_map/conv_one/pallas_call | solution.py:295
  130.5 7.4 %all-to-all-start.3 = ((bf16[4,128,256]{2,1,0:T(8,128)(2,1)}), bf16[4,128,256]{2,1,0:T(8,128)(2,1)S(1)}, u32[]{:S(2)}, u32[]{:S(2)}) async-start(bf16[4,128,256]{2,1,0:T(8,128)(2,1)} %conv_one.1), calls=%async_computation.3 | async-start | bytes 524288 | tf_op jit(solution)/shard_map/all_to_all | solution.py:304
  140.3 4.0 %collective-permute-start.3 = (bf16[64,512]{1,0:T(8,128)(2,1)S(1)}, bf16[64,512]{1,0:T(8,128)(2,1)S(1)}, u32[]{:S(2)}, u32[]{:S(2)}) collective-permute-start(bf16[64,512]{1,0:T(8,128)(2,1)S(1)} %bitcast.66), channel_id=1, source_target_pairs={{0,2},{2,4},{4,6},{6,8},{8,10},{10,12},{12,14},{14,16},{16,18},{18... | collective-permute-start | bytes 196616 | tf_op jit(solution)/shard_map/ppermute | solution.py:28
  144.3 1.3 collective-permute-start.4
  146.5 1.9 join_one.1
  148.4 10.5 %all-gather.1 = bf16[256,256]{1,0:T(8,128)(2,1)S(1)} all-gather(bf16[128,256]{1,0:T(8,128)(2,1)} %get-tuple-element.12), channel_id=3, replica_groups=mesh['img'=2,'x'=4,'zh'=8,'zl'=4,'col'=2] {'col'}, dimensions={0}, use_global_device_ids=true | all-gather | bytes 196608 | tf_op jit(solution)/shard_map/all_gather | solution.py:318
  159.0 1.3 collective-permute-start.1
  160.3 1.3 collective-permute-start.2
  162.9 9.0 %all-to-all-start.4 = ((f32[32,1,128]{2,1,0:T(1,128)}), f32[32,1,128]{2,1,0:T(1,128)S(1)}, u32[]{:S(2)}, u32[]{:S(2)}) async-start(f32[32,1,128]{2,1,0:T(1,128)} %broadcast_in_dim.25), calls=%async_computation.4 | async-start | bytes 32768 | tf_op jit(solution)/shard_map/all_to_all | solution.py:22
  174.4 4.7 %all-to-all-done.4 = f32[32,1,128]{2,1,0:T(1,128)S(1)} async-done(((f32[32,1,128]{2,1,0:T(1,128)}), f32[32,1,128]{2,1,0:T(1,128)S(1)}, u32[]{:S(2)}, u32[]{:S(2)}) %all-to-all-start.4) | async-done | bytes 16416 | tf_op jit(solution)/shard_map/all_to_all | solution.py:22
  179.7 11.2 %all-to-all-start.5 = ((f32[8,1,128]{2,1,0:T(1,128)}), f32[8,1,128]{2,1,0:T(1,128)S(1)}, u32[]{:S(2)}, u32[]{:S(2)}) async-start(f32[8,1,128]{2,1,0:T(1,128)} %broadcast_in_dim.26), calls=%async_computation.5 | async-start | bytes 8192 | tf_op jit(solution)/shard_map/all_to_all | solution.py:22
  190.9 2.7 %all_gather.39 = bf16[3,128,512]{2,1,0:T(8,128)(2,1)S(1)} all-gather(bf16[3,64,512]{2,1,0:T(8,128)(2,1)S(1)} %pad_maximum_fusion.1), channel_id=1, replica_groups=mesh['img'=2,'x'=4,'zh'=8,'zl'=4,'col'=2] {'col'}, dimensions={1}, use_global_device_ids=true | all-gather | bytes 589824 | tf_op jit(solution)/shard_map/all_gather | solution.py:323
  193.6 2.3 all-gather.2
  197.1 14.8 %all-to-all-done.5 = f32[8,1,128]{2,1,0:T(1,128)S(1)} async-done(((f32[8,1,128]{2,1,0:T(1,128)}), f32[8,1,128]{2,1,0:T(1,128)S(1)}, u32[]{:S(2)}, u32[]{:S(2)}) %all-to-all-start.5) | async-done | bytes 4128 | tf_op jit(solution)/shard_map/all_to_all | solution.py:22
  212.4 3.1 %norm_two.1.x_ref = bf16[2,640,256]{2,1,0:T(8,128)(2,1)} custom-call(s32[1]{0:T(128)} %bitcast.at_ref, bf16[2,128,256]{2,1,0:T(8,128)(2,1)} %bitcast.59, bf16[2,2,2,128,256]{4,3,2,1,0:T(8,128)(2,1)} %bitcast.48, f32[8,128]{1,0:T(8,128)} %bitcast.75, f32[1,512]{1,0:T(1,128)} %slice.82.gain_ref, f32[1,512]{1,0:T(1,128)} %slice.84.shift_ref, ...), custom_call_target="tpu_custom_call" | custom-call | tf_op jit(solution)/shard_map/norm_two/pallas_call | solution.py:325
  215.6 4.5 %conv_two.1 = bf16[384,256]{1,0:T(8,128)(2,1)} custom-call(s32[1]{0:T(128)} %bitcast.at_ref, bf16[2,640,256]{2,1,0:T(8,128)(2,1)} %norm_two.1.x_ref, bf16[384,256]{1,0:T(8,128)(2,1)} %dynamic-slice_convert_fusion.res_ref, f32[1,256]{1,0:T(1,128)} %get-tuple-element.22.bias_ref, bf16[32,18,16,256]{3,2,1,0:T(8,128)(2,1)} %all-gather.6.cloned.1.call-done.w_ref), custom_call_target="tpu_custom_call" | custom-call | tf_op jit(solution)/shard_map/conv_two/pallas_call | solution.py:334
  220.1 5.6 %all-gather.3 = bf16[768,256]{1,0:T(8,128)(2,1)} all-gather(bf16[384,256]{1,0:T(8,128)(2,1)} %conv_two.1), channel_id=5, replica_groups=mesh['img'=2,'x'=4,'zh'=8,'zl'=4,'col'=2] {'col'}, dimensions={0}, use_global_device_ids=true | all-gather | bytes 589824 | tf_op jit(solution)/shard_map/all_gather | solution.py:346
  225.7 4.5 %conv_up.1 = bf16[2,2,128,256]{3,2,1,0:T(8,128)(2,1)} custom-call(bf16[2,384,256]{2,1,0:T(8,128)(2,1)} %bitcast.49, f32[1,256]{1,0:T(1,128)} %get-tuple-element.21.bias_ref, bf16[32,18,16,256]{3,2,1,0:T(8,128)(2,1)} %all-gather.6.cloned.1.call-done.w_ref), custom_call_target="tpu_custom_call" | custom-call | tf_op jit(solution)/shard_map/conv_up/pallas_call | solution.py:348
  230.2 4.8 %all_to_all.41 = bf16[2,2,128,256]{3,2,1,0:T(8,128)(2,1)S(1)} all-to-all(bf16[2,2,128,256]{3,2,1,0:T(8,128)(2,1)} %conv_up.1), channel_id=1, replica_groups=mesh['img'=2,'x'=4,'zh'=8,'zl'=4,'col'=2] {'col'}, dimensions={0} | all-to-all | bytes 524288 | tf_op jit(solution)/shard_map/all_to_all | solution.py:361
  (110 shorter events, 20.6 us)
Async XLA Ops:
  6.5 14.0 %copy-start.3 = (bf16[1,64,512]{2,1,0:T(8,128)(2,1)S(1)}, bf16[1,64,512]{2,1,0:T(8,128)(2,1)}, u32[]{:S(2)}) copy-start(bf16[1,64,512]{2,1,0:T(8,128)(2,1)} %param.11) | copy-start | bytes 196612
  6.5 209.0 %all-gather.6.cloned.1.call-start = ((), (), s32[]{:S(2)}) async-start(), calls=%async_computation.7 | async-start | bytes 4866048 | tf_op jit(solution)/shard_map/all_gather | solution.py:246
  20.6 52.4 %collective-permute-start = (bf16[64,512]{1,0:T(8,128)(2,1)S(1)}, bf16[64,512]{1,0:T(8,128)(2,1)S(1)}, u32[]{:S(2)}, u32[]{:S(2)}) collective-permute-start(bf16[64,512]{1,0:T(8,128)(2,1)S(1)} %bitcast.64), channel_id=1, source_target_pairs={{6,8},{14,16},{22,24},{30,32},{38,40},{46,48},{54,56},{62,64},{70,... | collective-permute-start | bytes 196616 | tf_op jit(solution)/shard_map/ppermute | solution.py:265
  22.4 57.6 %all-to-all-start.2 = ((f32[32,1,128]{2,1,0:T(1,128)}), f32[32,1,128]{2,1,0:T(1,128)S(1)}, u32[]{:S(2)}, u32[]{:S(2)}) async-start(f32[32,1,128]{2,1,0:T(1,128)} %broadcast_in_dim.22), calls=%async_computation.2 | async-start | bytes 32768 | tf_op jit(solution)/shard_map/all_to_all | solution.py:22
  72.9 11.8 %copy-start.5 = (f32[512]{0:T(512)S(1)}, f32[512]{0:T(512)}, u32[]{:S(2)}) copy-start(f32[512]{0:T(512)} %param.12) | copy-start | bytes 6148
  72.9 12.1 %copy-start.6 = (f32[512]{0:T(512)S(1)}, f32[512]{0:T(512)}, u32[]{:S(2)}) copy-start(f32[512]{0:T(512)} %param.13) | copy-start | bytes 6148
  72.9 12.7 %copy-start.7 = (f32[512]{0:T(512)S(1)}, f32[512]{0:T(512)}, u32[]{:S(2)}) copy-start(f32[512]{0:T(512)} %param.16) | copy-start | bytes 6148
  72.9 12.8 %copy-start.8 = (f32[512]{0:T(512)S(1)}, f32[512]{0:T(512)}, u32[]{:S(2)}) copy-start(f32[512]{0:T(512)} %param.17) | copy-start | bytes 6148
  72.9 12.9 %copy-start.9 = (f32[512]{0:T(512)S(1)}, f32[512]{0:T(512)}, u32[]{:S(2)}) copy-start(f32[512]{0:T(512)} %param.15) | copy-start | bytes 6148
  72.9 13.1 %copy-start.10 = (f32[512]{0:T(512)S(1)}, f32[512]{0:T(512)}, u32[]{:S(2)}) copy-start(f32[512]{0:T(512)} %param.19) | copy-start | bytes 6148
  73.3 65.5 %copy-start.11 = (f32[512]{0:T(512)S(1)}, f32[512]{0:T(512)}, u32[]{:S(2)}) copy-start(f32[512]{0:T(512)} %param.21) | copy-start | bytes 6148
  80.7 46.1 %all-to-all-start = ((bf16[8,2,64,128]{3,2,1,0:T(8,128)(2,1)}), bf16[8,2,64,128]{3,2,1,0:T(8,128)(2,1)S(1)}, u32[]{:S(2)}, u32[]{:S(2)}) async-start(bf16[8,2,64,128]{3,2,1,0:T(8,128)(2,1)} %bitcast.3), calls=%async_computation | async-start | bytes 524288 | tf_op jit(solution)/shard_map/all_to_all | solution.py:270
  126.8 0.7 copy-start.1
  130.5 15.3 %all-to-all-start.3 = ((bf16[4,128,256]{2,1,0:T(8,128)(2,1)}), bf16[4,128,256]{2,1,0:T(8,128)(2,1)S(1)}, u32[]{:S(2)}, u32[]{:S(2)}) async-start(bf16[4,128,256]{2,1,0:T(8,128)(2,1)} %conv_one.1), calls=%async_computation.3 | async-start | bytes 524288 | tf_op jit(solution)/shard_map/all_to_all | solution.py:304
  140.3 34.1 %collective-permute-start.3 = (bf16[64,512]{1,0:T(8,128)(2,1)S(1)}, bf16[64,512]{1,0:T(8,128)(2,1)S(1)}, u32[]{:S(2)}, u32[]{:S(2)}) collective-permute-start(bf16[64,512]{1,0:T(8,128)(2,1)S(1)} %bitcast.66), channel_id=1, source_target_pairs={{0,2},{2,4},{4,6},{6,8},{8,10},{10,12},{12,14},{14,16},{16,18},{18... | collective-permute-start | bytes 196616 | tf_op jit(solution)/shard_map/ppermute | solution.py:28
  144.3 30.1 %collective-permute-start.4 = (bf16[64,512]{1,0:T(8,128)(2,1)S(1)}, bf16[64,512]{1,0:T(8,128)(2,1)S(1)}, u32[]{:S(2)}, u32[]{:S(2)}) collective-permute-start(bf16[64,512]{1,0:T(8,128)(2,1)S(1)} %bitcast.67), channel_id=1, source_target_pairs={{2,0},{4,2},{6,4},{8,6},{10,8},{12,10},{14,12},{16,14},{18,16},{20... | collective-permute-start | bytes 196616 | tf_op jit(solution)/shard_map/ppermute | solution.py:28
  145.8 0.7 copy-start
  159.0 37.4 %copy-start.2 = (bf16[256,256]{1,0:T(8,128)(2,1)}, bf16[256,256]{1,0:T(8,128)(2,1)S(1)}, u32[]{:S(2)}) copy-start(bf16[256,256]{1,0:T(8,128)(2,1)S(1)} %all-gather.1) | copy-start | bytes 393220
  159.0 31.9 %collective-permute-start.1 = (bf16[2,128,256]{2,1,0:T(8,128)(2,1)S(1)}, bf16[2,128,256]{2,1,0:T(8,128)(2,1)S(1)}, u32[]{:S(2)}, u32[]{:S(2)}) collective-permute-start(bf16[2,128,256]{2,1,0:T(8,128)(2,1)S(1)} %bitcast.57), channel_id=1, source_target_pairs={{0,2},{2,4},{4,6},{6,8},{8,10},{10,12},{12,14},{14,16},{16,18},{18... | collective-permute-start | bytes 393224 | tf_op jit(solution)/shard_map/ppermute | solution.py:320
  160.3 30.6 %collective-permute-start.2 = (bf16[2,128,256]{2,1,0:T(8,128)(2,1)S(1)}, bf16[2,128,256]{2,1,0:T(8,128)(2,1)S(1)}, u32[]{:S(2)}, u32[]{:S(2)}) collective-permute-start(bf16[2,128,256]{2,1,0:T(8,128)(2,1)S(1)} %bitcast.58), channel_id=1, source_target_pairs={{0,4},{2,6},{4,8},{6,10},{8,12},{10,14},{12,16},{14,18},{16,20},{1... | collective-permute-start | bytes 393224 | tf_op jit(solution)/shard_map/ppermute | solution.py:320
  162.9 16.2 %all-to-all-start.4 = ((f32[32,1,128]{2,1,0:T(1,128)}), f32[32,1,128]{2,1,0:T(1,128)S(1)}, u32[]{:S(2)}, u32[]{:S(2)}) async-start(f32[32,1,128]{2,1,0:T(1,128)} %broadcast_in_dim.25), calls=%async_computation.4 | async-start | bytes 32768 | tf_op jit(solution)/shard_map/all_to_all | solution.py:22
  179.7 32.2 %all-to-all-start.5 = ((f32[8,1,128]{2,1,0:T(1,128)}), f32[8,1,128]{2,1,0:T(1,128)S(1)}, u32[]{:S(2)}, u32[]{:S(2)}) async-start(f32[8,1,128]{2,1,0:T(1,128)} %broadcast_in_dim.26), calls=%async_computation.5 | async-start | bytes 8192 | tf_op jit(solution)/shard_map/all_to_all | solution.py:22
  211.9 0.6 copy-start.4
Sparse Core Ops, SparseCore 0:
  20.7 165.4 all-gather.5

commit v5 on v4

--- a/solution.py
+++ b/solution.py
@@ -112,80 +112,74 @@
             out_ref[h, (d + 2) * cols : (d + 3) * cols, :] = jnp.where(inside, y, 0.0).astype(BF16)
 
 
-def conv_two_kernel(cols, rows, image_rows, at_ref, x_ref, res_ref, bias_ref, w_ref, out_ref, S, acc):
-    t = pl.program_id(0)
-    outs = acc.shape[1]
-
-    @pl.when(t == 0)
-    def _():
-        for i in range(rows + 2):
-            for h in range(2):
-                y = x_ref[h, pl.ds(i * cols, cols), :].astype(F32)
-                put_shifted(S, i, cols, y, slice(h * outs, (h + 1) * outs))
-        acc[...] = jnp.broadcast_to(bias_ref[...], acc.shape)
-
-    start = pl.multiple_of(t * cols, cols)
-    total = acc[...]
-    for k in range(3):
-        piece = w_ref[:, k].reshape(-1, outs)
-        total += jnp.dot(S[k, pl.ds(start, rows * cols), :], piece, preferred_element_type=F32)
-    acc[...] = total
-
-    @pl.when(t == 2)
-    def _():
-        first = at_ref[0] - rows // 2
-        for i in range(rows):
-            at = pl.ds(i * cols, cols)
-            y = acc[at, :] + res_ref[at, :].astype(F32)
-            inside = jnp.logical_and(first + i >= 0, first + i < image_rows)
-            out_ref[at, :] = jnp.where(inside, y, 0.0).astype(BF16)
-
-
-def conv_up_kernel(cols, x_ref, bias_ref, w_ref, out_ref, S, acc, full):
-    t = pl.program_id(0)
-    outs = acc.shape[2]
-
-    @pl.when(t == 0)
-    def _():
-        for i in range(3):
-            for h in range(2):
-                y = x_ref[h, pl.ds(i * cols, cols), :].astype(F32)
-                put_shifted(S, i, cols, y, slice(h * outs, (h + 1) * outs))
-        acc[...] = jnp.broadcast_to(bias_ref[...][None], acc.shape)
-
+def fetch_weights(w_ref, base, held, arrived):
+    copies = [
+        pltpu.make_async_copy(w_ref.at[:, pl.ds(base + 3 * r, 3)], held.at[r], arrived.at[r])
+        for r in range(3)
+    ]
+    for copy in copies:
+        copy.start()
+    return copies
+
+
+def conv_two_kernel(cols, rows, image_rows, at_ref, x_ref, res_ref, bias_ref, w_ref, out_ref, S, held, arrived):
+    copies = fetch_weights(w_ref, 0, held, arrived)
+    outs = out_ref.shape[1]
+    for i in range(rows + 2):
+        for h in range(2):
+            y = x_ref[h, i * cols : (i + 1) * cols, :].astype(F32)
+            put_shifted(S, i, cols, y, slice(h * outs, (h + 1) * outs))
+    total = jnp.broadcast_to(bias_ref[...], out_ref.shape)
+    for r in range(3):
+        copies[r].wait()
+        for k in range(3):
+            piece = held[r, :, k].reshape(-1, outs)
+            total += jnp.dot(
+                S[k, r * cols : (r + rows) * cols, :], piece, preferred_element_type=F32
+            )
+    first = at_ref[0] - rows // 2
+    for i in range(rows):
+        at = slice(i * cols, (i + 1) * cols)
+        y = total[at] + res_ref[at, :].astype(F32)
+        inside = jnp.logical_and(first + i >= 0, first + i < image_rows)
+        out_ref[at, :] = jnp.where(inside, y, 0.0).astype(BF16)
+
+
+def conv_up_kernel(cols, at_ref, x_ref, bias_ref, w_ref, out_ref, S, full, held, arrived):
+    copies = fetch_weights(w_ref, 9, held, arrived)
+    outs = out_ref.shape[2]
+    part = out_ref.shape[1] // 2
+    for i in range(3):
+        for h in range(2):
+            y = x_ref[h, i * cols : (i + 1) * cols, :].astype(F32)
+            put_shifted(S, i, cols, y, slice(h * outs, (h + 1) * outs))
+    begin = at_ref[0] * part
+    totals = [jnp.broadcast_to(bias_ref[...], (part, outs)) for _ in range(4)]
+    for r in range(3):
+        copies[r].wait()
+        for k in range(3):
+            piece = held[r, :, k].reshape(-1, outs)
+            for p in range(2):
+                start = pl.multiple_of((r + 1 + p) // 2 * cols + begin, part)
+                for q in range(2):
+                    totals[2 * p + q] += jnp.dot(
+                        S[(k + 1 + q) // 2, pl.ds(start, part), :], piece, preferred_element_type=F32
+                    )
     for p in range(2):
-        start = pl.multiple_of(((t + 1 + p) // 2) * cols, cols)
-        for q in range(2):
-            total = acc[2 * p + q]
-            for k in range(3):
-                total += jnp.dot(
-                    S[(k + 1 + q) // 2, pl.ds(start, cols), :],
-                    w_ref[:, k].reshape(-1, outs),
-                    preferred_element_type=F32,
-                )
-            acc[2 * p + q] = total
-
-    @pl.when(t == 2)
-    def _():
-        for p in range(2):
+        for k in range(2):
+            lanes = slice(k * 128, (k + 1) * 128)
             for q in range(2):
-                for k in range(2):
-                    lanes = slice(k * 128, (k + 1) * 128)
-                    full[p, k, pl.ds(q, cols, stride=2), :] = acc[2 * p + q][:, lanes]
-            for k in range(2):
-                for half in range(2):
-                    out_ref[half, p, :, k * 128 : (k + 1) * 128] = full[
-                        p, k, half * cols : (half + 1) * cols, :
-                    ].astype(BF16)
+                full[p, k, pl.ds(q, part, stride=2), :] = totals[2 * p + q][:, lanes]
+            out_ref[p, :, lanes] = full[p, k].astype(BF16)
+
+
+def grant(mebibytes):
+    return pltpu.CompilerParams(vmem_limit_bytes=mebibytes << 20)
 
 
 VM = pl.BlockSpec(memory_space=pltpu.VMEM)
 SM = pl.BlockSpec(memory_space=pltpu.SMEM)
-
-
-def weight_spec(gathered, base):
-    n, _, rows, outs = gathered.shape
-    return pl.BlockSpec((n, 3, rows, outs), lambda t: (0, base + t, 0, 0))
+HB = pl.BlockSpec(memory_space=pltpu.HBM)
 
 
 def on_device(
@@ -298,6 +292,7 @@
         in_specs=[SM] + [VM] * 5,
         out_specs=VM,
         scratch_shapes=[pltpu.VMEM(((nzl + 2) * cols, 3 * depth), BF16)],
+        compiler_params=grant(16),
         name="conv_one",
     )(at, quad, gain_one, shift_one, pick_one, weights_one)
     parts, own = lax.optimization_barrier((parts, own))
@@ -311,55 +306,65 @@
         ),
         in_specs=[VM] * 3,
         out_specs=(VM, VM),
+        compiler_params=grant(8),
         name="join_one",
     )(parts, bias_one, pick_own)
 
     stats = jnp.sum(sum_over(sums_two[:1], ("x", "zl", "col")), axis=0, keepdims=True)
     both = lax.all_gather(hidden, "col")
+    three = lax.all_gather(three, "col", axis=1, tiled=True)
+    residual = own_half(moved(three.reshape(3 * cols, channels), move))
+    stats, both, residual = lax.optimization_barrier((stats, both, residual))
     stats = sum_over(stats, "zh")
     far = jnp.stack([lax.ppermute(both, ROW + ("col",), fetch(nx * nz, d)) for d in (1, 2)])
-    far, three = lax.optimization_barrier((far, three))
     far = lax.all_gather(far, "col")
-    three = lax.all_gather(three, "col", axis=1, tiled=True)
-    residual = own_half(moved(three.reshape(3 * cols, channels), move))
     normed = pl.pallas_call(
         functools.partial(norm_kernel, image_rows, count),
         out_shape=jax.ShapeDtypeStruct((ncol, 5 * cols, half), BF16),
         in_specs=[SM] + [VM] * 6,
         out_specs=VM,
+        compiler_params=grant(12),
         name="norm_two",
     )(at, both, far, stats, gain_two, shift_two, pick_two)
 
     rows = 3
+    held = [
+        pltpu.VMEM((3, weights.shape[0], 3) + weights.shape[2:], BF16),
+        pltpu.SemaphoreType.DMA((3,)),
+    ]
     block = pl.pallas_call(
         functools.partial(conv_two_kernel, cols, rows, image_rows),
-        grid=(3,),
         out_shape=jax.ShapeDtypeStruct((rows * cols, half), BF16),
-        in_specs=[SM, VM, VM, VM, weight_spec(weights, 0)],
+        in_specs=[SM, VM, VM, VM, HB],
         out_specs=VM,
-        scratch_shapes=[
-            pltpu.VMEM((3, (rows + 2) * cols, channels), BF16),
-            pltpu.VMEM((rows * cols, half), F32),
-        ],
+        scratch_shapes=[pltpu.VMEM((3, (rows + 2) * cols, channels), BF16)] + held,
+        compiler_params=grant(58),
         name="conv_two",
     )(at, normed, residual, bias_two, weights)
     block = lax.all_gather(block, "col")
 
-    up = pl.pallas_call(
-        functools.partial(conv_up_kernel, cols),
-        grid=(3,),
-        out_shape=jax.ShapeDtypeStruct((ncol, 2, cols, half), BF16),
-        in_specs=[VM, VM, weight_spec(weights, 3)],
-        out_specs=VM,
-        scratch_shapes=[
-            pltpu.VMEM((3, 3 * cols, channels), BF16),
-            pltpu.VMEM((4, cols, half), F32),
-            pltpu.VMEM((2, 2, 2 * cols, 128), F32),
-        ],
-        name="conv_up",
-    )(block, bias_up, weights)
-    up = lax.all_to_all(up, "col", 0, 0, tiled=True)
-    return up.transpose(1, 2, 0, 3).reshape(2, cols, channels)
+    def up(part):
+        return pl.pallas_call(
+            functools.partial(conv_up_kernel, cols),
+            out_shape=jax.ShapeDtypeStruct((2, cols, half), BF16),
+            in_specs=[SM, VM, VM, HB],
+            out_specs=VM,
+            scratch_shapes=[
+                pltpu.VMEM((3, 3 * cols, channels), BF16),
+                pltpu.VMEM((2, 2, cols, 128), F32),
+            ]
+            + held,
+            compiler_params=grant(58),
+            cost_estimate=pl.CostEstimate(flops=4_000_000_000, bytes_accessed=3 << 20, transcendentals=0),
+            name="conv_up",
+        )(part, block, bias_up, weights)
+
+    mine = c.astype(jnp.int32)[None]
+    theirs = lax.ppermute(up(1 - mine), "col", [(0, 1), (1, 0)])
+    ours = up(mine)
+    return jnp.where(
+        c == 0, jnp.concatenate([ours, theirs], axis=2), jnp.concatenate([theirs, ours], axis=2)
+    )
 
 
 def solution(mesh):

time: 244 us -> 240 us (0.984)
  blocking collectives: 75.3 us -> 64.5 us
  waiting for transfers between devices: 26.3 us -> 34.7 us
  local copies, waits for them, and re-layouts: 14.9 us -> 10.3 us
  starting transfers between devices: 90.6 us -> 95 us
    all_gather x1, blocking collectives: 10.5 us -> 2.26 us  [on_device(): both = lax.all_gather(hidden, 'col')]
    ppermute x2, waiting for transfers between devices: 0.01 us -> 5.26 us  [shifted_rows(): return lax.ppermute(values, axis, pairs)]
    all_to_all x1 -> x0, blocking collectives: 4.78 us -> none  [on_device(): up = lax.all_to_all(up, 'col', 0, 0, tiled=True)]
    pallas_call x1 -> x2, Pallas kernels: 4.53 us -> 8.5 us  [up(): pl.pallas_call(functools.partial(conv_up_kernel, cols), out_shape=jax.Sha...]
    all_gather x1, blocking collectives: 2.65 us -> 6.49 us  [on_device(): three = lax.all_gather(three, 'col', axis=1, tiled=True)]
    all_to_all x3, waiting for transfers between devices: 26 us -> 29.3 us  [sum_over(): return lax.all_to_all(sent, axes, 0, 0, tiled=True)]
  transfers between devices with their start and end apart: 11 -> 12, of which waited for: 4 -> 5; matrix products, arithmetic and copies ran while one was open for 5% -> 3% of each run, Pallas kernels for 3% -> 3%
where the time goes in v5:
time: 240 us; the launch traced here: 239 us
  starting transfers between devices  95 us (40%)
  blocking collectives  64.5 us (27%)
  waiting for transfers between devices  34.7 us (14%)
  Pallas kernels  16.5 us (7%)
  between operations  14 us (6%)
  local copies, waits for them, and re-layouts  10.3 us (4%)
  other arithmetic  2.8 us (1%)
    all_to_all x3, starting transfers between devices, sum_over(): return lax.all_to_all(sent, axes, 0, 0, tiled=True)  71.2 us
    all_gather x1, blocking collectives, on_device(): weights_one = lax.all_gather(jnp.concatenate([hold_one, terms[None]]), 'zh')  38.3 us
    all_to_all x3, waiting for transfers between devices, sum_over(): return lax.all_to_all(sent, axes, 0, 0, tiled=True)  29.3 us
    all_to_all x1, blocking collectives, on_device(): lax.all_to_all(jnp.broadcast_to(hold, (nx, 27, k_own, half)), 'x', 0, 0,...  10.2 us
    all_to_all x1, starting transfers between devices, on_device(): parts = lax.all_to_all(parts, 'zl', 0, 0, tiled=True)  9.04 us
    pallas_call x2, Pallas kernels, up(): pl.pallas_call(functools.partial(conv_up_kernel, cols), out_shape=jax.Sha...  8.5 us
    all_gather x1, blocking collectives, on_device(): three = lax.all_gather(three, 'col', axis=1, tiled=True)  6.49 us
    ppermute x2, starting transfers between devices, shifted_rows(): return lax.ppermute(values, axis, pairs)  5.44 us
  transfers between devices with their start and end apart: 12, of which 5 were waited for; matrix products, arithmetic and copies ran while one was open for 3% of the time, Pallas kernels for 3%

profile of v5, /device:TPU:33, one launch (start us, length us, event | category | flops | bytes accessed | tf_op | source)
XLA Modules:
  0.0 239.3 jit_solution(17386172891305754416)
XLA Ops:
  9.4 10.2 %all_to_all.35 = bf16[4,27,4,256]{3,2,1,0:T(4,128)(2,1)S(1)} all-to-all(bf16[4,27,4,256]{3,2,1,0:T(4,128)(2,1)S(1)} %broadcast_in_dim.26), channel_id=1, replica_groups=mesh['img'=2,'x'=4,'zh'=8,'zl'=4,'col'=2] {'x'}, dimensions={0} | all-to-all | bytes 442368 | tf_op jit(solution)/shard_map/all_to_all | solution.py:238
  22.4 50.4 %all-to-all-start.2 = ((f32[32,1,128]{2,1,0:T(1,128)}), f32[32,1,128]{2,1,0:T(1,128)S(1)}, u32[]{:S(2)}, u32[]{:S(2)}) async-start(f32[32,1,128]{2,1,0:T(1,128)} %broadcast_in_dim.27), calls=%async_computation.2 | async-start | bytes 32768 | tf_op jit(solution)/shard_map/all_to_all | solution.py:22
  73.4 6.6 %all-to-all-done.2 = f32[32,1,128]{2,1,0:T(1,128)S(1)} async-done(((f32[32,1,128]{2,1,0:T(1,128)}), f32[32,1,128]{2,1,0:T(1,128)S(1)}, u32[]{:S(2)}, u32[]{:S(2)}) %all-to-all-start.2) | async-done | bytes 16416 | tf_op jit(solution)/shard_map/all_to_all | solution.py:22
  80.7 4.0 %all-to-all-start = ((bf16[8,2,64,128]{3,2,1,0:T(8,128)(2,1)}), bf16[8,2,64,128]{3,2,1,0:T(8,128)(2,1)S(1)}, u32[]{:S(2)}, u32[]{:S(2)}) async-start(bf16[8,2,64,128]{3,2,1,0:T(8,128)(2,1)} %bitcast.4), calls=%async_computation | async-start | bytes 524288 | tf_op jit(solution)/shard_map/all_to_all | solution.py:264
  86.8 38.3 %all-gather = bf16[80,16,256]{2,1,0:T(8,128)(2,1)S(1)} all-gather(bf16[10,16,256]{2,1,0:T(8,128)(2,1)S(1)} %pad_maximum_fusion.2), channel_id=2, replica_groups=mesh['img'=2,'x'=4,'zh'=8,'zl'=4,'col'=2] {'zh'}, dimensions={0}, use_global_device_ids=true | all-gather | bytes 737280 | tf_op jit(solution)/shard_map/all_gather | solution.py:255
  125.1 1.8 conv_one.1
  126.9 9.0 %all-to-all-start.3 = ((bf16[4,128,256]{2,1,0:T(8,128)(2,1)}), bf16[4,128,256]{2,1,0:T(8,128)(2,1)S(1)}, u32[]{:S(2)}, u32[]{:S(2)}) async-start(bf16[4,128,256]{2,1,0:T(8,128)(2,1)} %conv_one.1), calls=%async_computation.3 | async-start | bytes 524288 | tf_op jit(solution)/shard_map/all_to_all | solution.py:299
  136.8 4.1 %collective-permute-start.1 = (bf16[64,512]{1,0:T(8,128)(2,1)S(1)}, bf16[64,512]{1,0:T(8,128)(2,1)S(1)}, u32[]{:S(2)}, u32[]{:S(2)}) collective-permute-start(bf16[64,512]{1,0:T(8,128)(2,1)S(1)} %bitcast.67), channel_id=1, source_target_pairs={{0,2},{2,4},{4,6},{6,8},{8,10},{10,12},{12,14},{14,16},{16,18},{18... | collective-permute-start | bytes 196616 | tf_op jit(solution)/shard_map/ppermute | solution.py:28
  140.9 1.3 collective-permute-start.2
  142.9 4.7 %collective-permute-done.2 = bf16[64,512]{1,0:T(8,128)(2,1)S(1)} collective-permute-done((bf16[64,512]{1,0:T(8,128)(2,1)S(1)}, bf16[64,512]{1,0:T(8,128)(2,1)S(1)}, u32[]{:S(2)}, u32[]{:S(2)}) %collective-permute-start.2) | collective-permute-done | bytes 65568 | tf_op jit(solution)/shard_map/ppermute | solution.py:28
  147.7 6.5 %all_gather.37 = bf16[3,128,512]{2,1,0:T(8,128)(2,1)S(1)} all-gather(bf16[3,64,512]{2,1,0:T(8,128)(2,1)S(1)} %pad_maximum_fusion.1), channel_id=1, replica_groups=mesh['img'=2,'x'=4,'zh'=8,'zl'=4,'col'=2] {'col'}, dimensions={1}, use_global_device_ids=true | all-gather | bytes 589824 | tf_op jit(solution)/shard_map/all_gather | solution.py:315
  155.5 5.6 %all-to-all-start.4 = ((f32[32,1,128]{2,1,0:T(1,128)}), f32[32,1,128]{2,1,0:T(1,128)S(1)}, u32[]{:S(2)}, u32[]{:S(2)}) async-start(f32[32,1,128]{2,1,0:T(1,128)} %broadcast_in_dim.58), calls=%async_computation.4 | async-start | bytes 32768 | tf_op jit(solution)/shard_map/all_to_all | solution.py:22
  161.8 2.3 all-gather.1
  164.1 4.2 %all-to-all-done.4 = f32[32,1,128]{2,1,0:T(1,128)S(1)} async-done(((f32[32,1,128]{2,1,0:T(1,128)}), f32[32,1,128]{2,1,0:T(1,128)S(1)}, u32[]{:S(2)}, u32[]{:S(2)}) %all-to-all-start.4) | async-done | bytes 16416 | tf_op jit(solution)/shard_map/all_to_all | solution.py:22
  169.7 1.3 collective-permute-start.4
  172.3 15.2 %all-to-all-start.5 = ((f32[8,1,128]{2,1,0:T(1,128)}), f32[8,1,128]{2,1,0:T(1,128)S(1)}, u32[]{:S(2)}, u32[]{:S(2)}) async-start(f32[8,1,128]{2,1,0:T(1,128)} %broadcast_in_dim.60), calls=%async_computation.5 | async-start | bytes 8192 | tf_op jit(solution)/shard_map/all_to_all | solution.py:22
  187.6 2.4 %all-gather.2 = bf16[4,2,128,256]{3,2,1,0:T(8,128)(2,1)S(1)} all-gather(bf16[2,2,128,256]{3,2,1,0:T(8,128)(2,1)S(1)} %pad_maximum_fusion), channel_id=4, replica_groups=mesh['img'=2,'x'=4,'zh'=8,'zl'=4,'col'=2] {'col'}, dimensions={0}, use_global_device_ids=true | all-gather | bytes 786432 | tf_op jit(solution)/shard_map/all_gather | solution.py:320
  190.0 18.5 %all-to-all-done.5 = f32[8,1,128]{2,1,0:T(1,128)S(1)} async-done(((f32[8,1,128]{2,1,0:T(1,128)}), f32[8,1,128]{2,1,0:T(1,128)S(1)}, u32[]{:S(2)}, u32[]{:S(2)}) %all-to-all-start.5) | async-done | bytes 4128 | tf_op jit(solution)/shard_map/all_to_all | solution.py:22
  210.4 4.9 %conv_two.1 = bf16[384,256]{1,0:T(8,128)(2,1)} custom-call(s32[1]{0:T(128)} %bitcast.1.at_ref, bf16[2,640,256]{2,1,0:T(8,128)(2,1)} %copy-done, bf16[384,256]{1,0:T(8,128)(2,1)} %dynamic-slice_convert_fusion.res_ref, f32[1,256]{1,0:T(1,128)} %get-tuple-element.24.bias_ref, bf16[32,18,16,256]{3,2,1,0:T(8,128)(2,1)} %all-gather.6.cloned.1.call-done.w_ref), custom_call_target="tpu_custom_call" | custom-call | tf_op jit(solution)/shard_map/conv_two/pallas_call | solution.py:335
  215.3 4.7 %all-gather.3 = bf16[768,256]{1,0:T(8,128)(2,1)} all-gather(bf16[384,256]{1,0:T(8,128)(2,1)} %conv_two.1), channel_id=5, replica_groups=mesh['img'=2,'x'=4,'zh'=8,'zl'=4,'col'=2] {'col'}, dimensions={0}, use_global_device_ids=true | all-gather | bytes 589824 | tf_op jit(solution)/shard_map/all_gather | solution.py:344
  220.1 4.2 %conv_up.3 = bf16[2,128,256]{2,1,0:T(8,128)(2,1)} custom-call(s32[1]{0:T(128)S(6)} %sub.109.at_ref, bf16[2,384,256]{2,1,0:T(8,128)(2,1)} %bitcast.60, f32[1,256]{1,0:T(1,128)} %get-tuple-element.23.bias_ref, bf16[32,18,16,256]{3,2,1,0:T(8,128)(2,1)} %all-gather.6.cloned.1.call-done.w_ref), custom_call_target="tpu_custom_call" | custom-call | flops 4000000000 | bytes 3145728 | tf_op jit(solution)/shard_map/conv_up/pallas_call | solution.py:347
  224.3 2.1 collective-permute-start.5
  226.4 4.3 %conv_up.2 = bf16[2,128,256]{2,1,0:T(8,128)(2,1)} custom-call(s32[1]{0:T(128)} %bitcast.at_ref, bf16[2,384,256]{2,1,0:T(8,128)(2,1)} %bitcast.61, f32[1,256]{1,0:T(1,128)} %get-tuple-element.23.bias_ref, bf16[32,18,16,256]{3,2,1,0:T(8,128)(2,1)} %all-gather.6.cloned.1.call-done.w_ref), custom_call_target="tpu_custom_call" | custom-call | flops 4000000000 | bytes 3145728 | tf_op jit(solution)/shard_map/conv_up/pallas_call | solution.py:347
  230.7 1.8 maximum_select_fusion
  (105 shorter events, 16.8 us)
Async XLA Ops:
  6.5 14.0 %copy-start.1 = (bf16[1,64,512]{2,1,0:T(8,128)(2,1)S(1)}, bf16[1,64,512]{2,1,0:T(8,128)(2,1)}, u32[]{:S(2)}) copy-start(bf16[1,64,512]{2,1,0:T(8,128)(2,1)} %param.11) | copy-start | bytes 196612
  6.5 203.9 %all-gather.6.cloned.1.call-start = ((), (), s32[]{:S(2)}) async-start(), calls=%async_computation.6 | async-start | bytes 4866048 | tf_op jit(solution)/shard_map/all_gather | solution.py:240
  20.6 52.4 %collective-permute-start = (bf16[64,512]{1,0:T(8,128)(2,1)S(1)}, bf16[64,512]{1,0:T(8,128)(2,1)S(1)}, u32[]{:S(2)}, u32[]{:S(2)}) collective-permute-start(bf16[64,512]{1,0:T(8,128)(2,1)S(1)} %bitcast.65), channel_id=1, source_target_pairs={{6,8},{14,16},{22,24},{30,32},{38,40},{46,48},{54,56},{62,64},{70,... | collective-permute-start | bytes 196616 | tf_op jit(solution)/shard_map/ppermute | solution.py:259
  22.4 57.6 %all-to-all-start.2 = ((f32[32,1,128]{2,1,0:T(1,128)}), f32[32,1,128]{2,1,0:T(1,128)S(1)}, u32[]{:S(2)}, u32[]{:S(2)}) async-start(f32[32,1,128]{2,1,0:T(1,128)} %broadcast_in_dim.27), calls=%async_computation.2 | async-start | bytes 32768 | tf_op jit(solution)/shard_map/all_to_all | solution.py:22
  72.9 11.8 %copy-start.2 = (f32[512]{0:T(512)S(1)}, f32[512]{0:T(512)}, u32[]{:S(2)}) copy-start(f32[512]{0:T(512)} %param.12) | copy-start | bytes 6148
  72.9 12.1 %copy-start.3 = (f32[512]{0:T(512)S(1)}, f32[512]{0:T(512)}, u32[]{:S(2)}) copy-start(f32[512]{0:T(512)} %param.13) | copy-start | bytes 6148
  72.9 12.7 %copy-start.4 = (f32[512]{0:T(512)S(1)}, f32[512]{0:T(512)}, u32[]{:S(2)}) copy-start(f32[512]{0:T(512)} %param.16) | copy-start | bytes 6148
  72.9 12.8 %copy-start.5 = (f32[512]{0:T(512)S(1)}, f32[512]{0:T(512)}, u32[]{:S(2)}) copy-start(f32[512]{0:T(512)} %param.17) | copy-start | bytes 6148
  72.9 12.9 %copy-start.6 = (f32[512]{0:T(512)S(1)}, f32[512]{0:T(512)}, u32[]{:S(2)}) copy-start(f32[512]{0:T(512)} %param.15) | copy-start | bytes 6148
  72.9 13.1 %copy-start.7 = (f32[512]{0:T(512)S(1)}, f32[512]{0:T(512)}, u32[]{:S(2)}) copy-start(f32[512]{0:T(512)} %param.19) | copy-start | bytes 6148
  73.3 62.8 %copy-start.8 = (f32[512]{0:T(512)S(1)}, f32[512]{0:T(512)}, u32[]{:S(2)}) copy-start(f32[512]{0:T(512)} %param.21) | copy-start | bytes 6148
  80.7 44.4 %all-to-all-start = ((bf16[8,2,64,128]{3,2,1,0:T(8,128)(2,1)}), bf16[8,2,64,128]{3,2,1,0:T(8,128)(2,1)S(1)}, u32[]{:S(2)}, u32[]{:S(2)}) async-start(bf16[8,2,64,128]{3,2,1,0:T(8,128)(2,1)} %bitcast.4), calls=%async_computation | async-start | bytes 524288 | tf_op jit(solution)/shard_map/all_to_all | solution.py:264
  126.9 27.7 %all-to-all-start.3 = ((bf16[4,128,256]{2,1,0:T(8,128)(2,1)}), bf16[4,128,256]{2,1,0:T(8,128)(2,1)S(1)}, u32[]{:S(2)}, u32[]{:S(2)}) async-start(bf16[4,128,256]{2,1,0:T(8,128)(2,1)} %conv_one.1), calls=%async_computation.3 | async-start | bytes 524288 | tf_op jit(solution)/shard_map/all_to_all | solution.py:299
  136.8 6.1 %collective-permute-start.1 = (bf16[64,512]{1,0:T(8,128)(2,1)S(1)}, bf16[64,512]{1,0:T(8,128)(2,1)S(1)}, u32[]{:S(2)}, u32[]{:S(2)}) collective-permute-start(bf16[64,512]{1,0:T(8,128)(2,1)S(1)} %bitcast.67), channel_id=1, source_target_pairs={{0,2},{2,4},{4,6},{6,8},{8,10},{10,12},{12,14},{14,16},{16,18},{18... | collective-permute-start | bytes 196616 | tf_op jit(solution)/shard_map/ppermute | solution.py:28
  140.9 6.7 %collective-permute-start.2 = (bf16[64,512]{1,0:T(8,128)(2,1)S(1)}, bf16[64,512]{1,0:T(8,128)(2,1)S(1)}, u32[]{:S(2)}, u32[]{:S(2)}) collective-permute-start(bf16[64,512]{1,0:T(8,128)(2,1)S(1)} %bitcast.68), channel_id=1, source_target_pairs={{2,0},{4,2},{6,4},{8,6},{10,8},{12,10},{14,12},{16,14},{18,16},{20... | collective-permute-start | bytes 196616 | tf_op jit(solution)/shard_map/ppermute | solution.py:28
  155.5 12.8 %all-to-all-start.4 = ((f32[32,1,128]{2,1,0:T(1,128)}), f32[32,1,128]{2,1,0:T(1,128)S(1)}, u32[]{:S(2)}, u32[]{:S(2)}) async-start(f32[32,1,128]{2,1,0:T(1,128)} %broadcast_in_dim.58), calls=%async_computation.4 | async-start | bytes 32768 | tf_op jit(solution)/shard_map/all_to_all | solution.py:22
  168.4 19.2 %collective-permute-start.3 = (bf16[2,128,256]{2,1,0:T(8,128)(2,1)S(1)}, bf16[2,128,256]{2,1,0:T(8,128)(2,1)S(1)}, u32[]{:S(2)}, u32[]{:S(2)}) collective-permute-start(bf16[2,128,256]{2,1,0:T(8,128)(2,1)S(1)} %bitcast.51), channel_id=1, source_target_pairs={{0,2},{2,4},{4,6},{6,8},{8,10},{10,12},{12,14},{14,16},{16,18},{18... | collective-permute-start | bytes 393224 | tf_op jit(solution)/shard_map/ppermute | solution.py:319
  169.7 17.9 %collective-permute-start.4 = (bf16[2,128,256]{2,1,0:T(8,128)(2,1)S(1)}, bf16[2,128,256]{2,1,0:T(8,128)(2,1)S(1)}, u32[]{:S(2)}, u32[]{:S(2)}) collective-permute-start(bf16[2,128,256]{2,1,0:T(8,128)(2,1)S(1)} %bitcast.52), channel_id=1, source_target_pairs={{0,4},{2,6},{4,8},{6,10},{8,12},{10,14},{12,16},{14,18},{16,20},{1... | collective-permute-start | bytes 393224 | tf_op jit(solution)/shard_map/ppermute | solution.py:319
  172.3 36.1 %all-to-all-start.5 = ((f32[8,1,128]{2,1,0:T(1,128)}), f32[8,1,128]{2,1,0:T(1,128)S(1)}, u32[]{:S(2)}, u32[]{:S(2)}) async-start(f32[8,1,128]{2,1,0:T(1,128)} %broadcast_in_dim.60), calls=%async_computation.5 | async-start | bytes 8192 | tf_op jit(solution)/shard_map/all_to_all | solution.py:22
  209.6 0.9 copy-start
  224.3 6.4 %collective-permute-start.5 = (bf16[2,128,256]{2,1,0:T(8,128)(2,1)}, bf16[2,128,256]{2,1,0:T(8,128)(2,1)S(1)}, u32[]{:S(2)}, u32[]{:S(2)}) collective-permute-start(bf16[2,128,256]{2,1,0:T(8,128)(2,1)} %conv_up.3), channel_id=1, source_target_pairs={{0,1},{1,0},{2,3},{3,2},{4,5},{5,4},{6,7},{7,6},{8,9},{9,8},{10,11... | collective-permute-start | bytes 393224 | tf_op jit(solution)/shard_map/ppermute | solution.py:363
Sparse Core Ops, SparseCore 0:
  20.7 165.3 all-gather.5

commit v6 on v5

--- a/solution.py
+++ b/solution.py
@@ -114,8 +114,7 @@
 
 def fetch_weights(w_ref, base, held, arrived):
     copies = [
-        pltpu.make_async_copy(w_ref.at[:, pl.ds(base + 3 * r, 3)], held.at[r], arrived.at[r])
-        for r in range(3)
+        pltpu.make_async_copy(w_ref.at[:, base + t], held.at[t], arrived.at[t]) for t in range(9)
     ]
     for copy in copies:
         copy.start()
@@ -131,9 +130,9 @@
             put_shifted(S, i, cols, y, slice(h * outs, (h + 1) * outs))
     total = jnp.broadcast_to(bias_ref[...], out_ref.shape)
     for r in range(3):
-        copies[r].wait()
         for k in range(3):
-            piece = held[r, :, k].reshape(-1, outs)
+            copies[3 * r + k].wait()
+            piece = held[3 * r + k].reshape(-1, outs)
             total += jnp.dot(
                 S[k, r * cols : (r + rows) * cols, :], piece, preferred_element_type=F32
             )
@@ -145,32 +144,43 @@
         out_ref[at, :] = jnp.where(inside, y, 0.0).astype(BF16)
 
 
-def conv_up_kernel(cols, at_ref, x_ref, bias_ref, w_ref, out_ref, S, full, held, arrived):
+def conv_up_kernel(cols, at_ref, x_ref, bias_ref, w_ref, mine_ref, theirs_ref, S, full, held, arrived):
     copies = fetch_weights(w_ref, 9, held, arrived)
-    outs = out_ref.shape[2]
-    part = out_ref.shape[1] // 2
+    outs = mine_ref.shape[2]
     for i in range(3):
         for h in range(2):
             y = x_ref[h, i * cols : (i + 1) * cols, :].astype(F32)
             put_shifted(S, i, cols, y, slice(h * outs, (h + 1) * outs))
-    begin = at_ref[0] * part
-    totals = [jnp.broadcast_to(bias_ref[...], (part, outs)) for _ in range(4)]
+    total = jnp.broadcast_to(bias_ref[...], (4 * cols, outs))
     for r in range(3):
-        copies[r].wait()
         for k in range(3):
-            piece = held[r, :, k].reshape(-1, outs)
+            copies[3 * r + k].wait()
+            piece = held[3 * r + k].reshape(-1, outs)
+            phases = []
             for p in range(2):
-                start = pl.multiple_of((r + 1 + p) // 2 * cols + begin, part)
-                for q in range(2):
-                    totals[2 * p + q] += jnp.dot(
-                        S[(k + 1 + q) // 2, pl.ds(start, part), :], piece, preferred_element_type=F32
-                    )
+                start = (r + 1 + p) // 2 * cols
+                phases += [S[(k + 1 + q) // 2, start : start + cols, :] for q in range(2)]
+            total += jnp.dot(jnp.concatenate(phases), piece, preferred_element_type=F32)
+    mine = pl.multiple_of(at_ref[0] * cols, cols)
+    theirs = pl.multiple_of((1 - at_ref[0]) * cols, cols)
     for p in range(2):
         for k in range(2):
             lanes = slice(k * 128, (k + 1) * 128)
             for q in range(2):
-                full[p, k, pl.ds(q, part, stride=2), :] = totals[2 * p + q][:, lanes]
-            out_ref[p, :, lanes] = full[p, k].astype(BF16)
+                phase = (2 * p + q) * cols
+                full[p, k, pl.ds(q, cols, stride=2), :] = total[phase : phase + cols, lanes]
+            mine_ref[p, :, lanes] = full[p, k, pl.ds(mine, cols), :].astype(BF16)
+            theirs_ref[p, :, lanes] = full[p, k, pl.ds(theirs, cols), :].astype(BF16)
+
+
+def sides_kernel(at_ref, mine_ref, theirs_ref, out_ref):
+    outs = mine_ref.shape[2]
+    for k, first, second in ((0, mine_ref, theirs_ref), (1, theirs_ref, mine_ref)):
+
+        @pl.when(at_ref[0] == k)
+        def _():
+            out_ref[:, :, :outs] = first[...]
+            out_ref[:, :, outs:] = second[...]
 
 
 def grant(mebibytes):
@@ -297,7 +307,7 @@
     )(at, quad, gain_one, shift_one, pick_one, weights_one)
     parts, own = lax.optimization_barrier((parts, own))
     parts = lax.all_to_all(parts, "zl", 0, 0, tiled=True)
-    three = jnp.stack([shifted_rows(own, ROW, -1), own, shifted_rows(own, ROW, 1)])
+    three = [shifted_rows(own, ROW, -1), own, shifted_rows(own, ROW, 1)]
     hidden, sums_two = pl.pallas_call(
         join_kernel,
         out_shape=(
@@ -310,9 +320,10 @@
         name="join_one",
     )(parts, bias_one, pick_own)
 
+    both = lax.all_gather(hidden, "col")
+    three, _ = lax.optimization_barrier((three, sums_two))
     stats = jnp.sum(sum_over(sums_two[:1], ("x", "zl", "col")), axis=0, keepdims=True)
-    both = lax.all_gather(hidden, "col")
-    three = lax.all_gather(three, "col", axis=1, tiled=True)
+    three = lax.all_gather(jnp.stack(three), "col", axis=1, tiled=True)
     residual = own_half(moved(three.reshape(3 * cols, channels), move))
     stats, both, residual = lax.optimization_barrier((stats, both, residual))
     stats = sum_over(stats, "zh")
@@ -329,8 +340,8 @@
 
     rows = 3
     held = [
-        pltpu.VMEM((3, weights.shape[0], 3) + weights.shape[2:], BF16),
-        pltpu.SemaphoreType.DMA((3,)),
+        pltpu.VMEM((9, weights.shape[0]) + weights.shape[2:], BF16),
+        pltpu.SemaphoreType.DMA((9,)),
     ]
     block = pl.pallas_call(
         functools.partial(conv_two_kernel, cols, rows, image_rows),
@@ -343,28 +354,30 @@
     )(at, normed, residual, bias_two, weights)
     block = lax.all_gather(block, "col")
 
-    def up(part):
-        return pl.pallas_call(
-            functools.partial(conv_up_kernel, cols),
-            out_shape=jax.ShapeDtypeStruct((2, cols, half), BF16),
-            in_specs=[SM, VM, VM, HB],
-            out_specs=VM,
-            scratch_shapes=[
-                pltpu.VMEM((3, 3 * cols, channels), BF16),
-                pltpu.VMEM((2, 2, cols, 128), F32),
-            ]
-            + held,
-            compiler_params=grant(58),
-            cost_estimate=pl.CostEstimate(flops=4_000_000_000, bytes_accessed=3 << 20, transcendentals=0),
-            name="conv_up",
-        )(part, block, bias_up, weights)
-
-    mine = c.astype(jnp.int32)[None]
-    theirs = lax.ppermute(up(1 - mine), "col", [(0, 1), (1, 0)])
-    ours = up(mine)
-    return jnp.where(
-        c == 0, jnp.concatenate([ours, theirs], axis=2), jnp.concatenate([theirs, ours], axis=2)
-    )
+    core = c.astype(jnp.int32)[None]
+    side = jax.ShapeDtypeStruct((2, cols, half), BF16)
+    mine, theirs = pl.pallas_call(
+        functools.partial(conv_up_kernel, cols),
+        out_shape=(side, side),
+        in_specs=[SM, VM, VM, HB],
+        out_specs=(VM, VM),
+        scratch_shapes=[
+            pltpu.VMEM((3, 3 * cols, channels), BF16),
+            pltpu.VMEM((2, 2, 2 * cols, 128), F32),
+        ]
+        + held,
+        compiler_params=grant(58),
+        name="conv_up",
+    )(core, block, bias_up, weights)
+    theirs = lax.ppermute(theirs, "col", [(0, 1), (1, 0)])
+    return pl.pallas_call(
+        sides_kernel,
+        out_shape=jax.ShapeDtypeStruct((2, cols, channels), BF16),
+        in_specs=[SM, VM, VM],
+        out_specs=VM,
+        compiler_params=grant(8),
+        name="sides",
+    )(core, mine, theirs)
 
 
 def solution(mesh):

time: 240 us -> 238 us (level)
  starting transfers between devices: 95 us -> 99.3 us
  blocking collectives: 64.5 us -> 61.6 us
    all_to_all x3, starting transfers between devices: 71.2 us -> 76.2 us  [sum_over(): return lax.all_to_all(sent, axes, 0, 0, tiled=True)]
    all_gather x1, blocking collectives: 6.49 us -> 2.47 us  [on_device(): three = lax.all_gather(jnp.stack(three), 'col', axis=1, tiled=True)]
    all_to_all x3, waiting for transfers between devices: 29.3 us -> 26.7 us  [sum_over(): return lax.all_to_all(sent, axes, 0, 0, tiled=True)]
  transfers between devices with their start and end apart: 12 -> 12, of which waited for: 5 -> 6; matrix products, arithmetic and copies ran while one was open for 3% -> 4% of each run, Pallas kernels for 3% -> 1%
where the time goes in v6:
time: 238 us; the launch traced here: 237 us
  starting transfers between devices  99.3 us (42%)
  blocking collectives  61.6 us (26%)
  waiting for transfers between devices  33.6 us (14%)
  Pallas kernels  14.6 us (6%)
  between operations  14 us (6%)
  local copies, waits for them, and re-layouts  11.2 us (5%)
    all_to_all x3, starting transfers between devices, sum_over(): return lax.all_to_all(sent, axes, 0, 0, tiled=True)  76.2 us
    all_gather x1, blocking collectives, on_device(): weights_one = lax.all_gather(jnp.concatenate([hold_one, terms[None]]), 'zh')  39.6 us
    all_to_all x3, waiting for transfers between devices, sum_over(): return lax.all_to_all(sent, axes, 0, 0, tiled=True)  26.7 us
    all_to_all x1, blocking collectives, on_device(): lax.all_to_all(jnp.broadcast_to(hold, (nx, 27, k_own, half)), 'x', 0, 0,...  10.2 us
    all_to_all x1, starting transfers between devices, on_device(): parts = lax.all_to_all(parts, 'zl', 0, 0, tiled=True)  8.4 us
    pallas_call x1, Pallas kernels, on_device(): pl.pallas_call(functools.partial(conv_up_kernel, cols), out_shape=(side,...  5.59 us
    ppermute x2, starting transfers between devices, shifted_rows(): return lax.ppermute(values, axis, pairs)  5.43 us
    ppermute x2, waiting for transfers between devices, shifted_rows(): return lax.ppermute(values, axis, pairs)  5.39 us
  transfers between devices with their start and end apart: 12, of which 6 were waited for; matrix products, arithmetic and copies ran while one was open for 4% of the time, Pallas kernels for 1%

profile of v6, /device:TPU:33, one launch (start us, length us, event | category | flops | bytes accessed | tf_op | source)
XLA Modules:
  0.0 236.9 jit_solution(4526098455399447012)
XLA Ops:
  9.4 10.2 %all_to_all.35 = bf16[4,27,4,256]{3,2,1,0:T(4,128)(2,1)S(1)} all-to-all(bf16[4,27,4,256]{3,2,1,0:T(4,128)(2,1)S(1)} %broadcast_in_dim.26), channel_id=1, replica_groups=mesh['img'=2,'x'=4,'zh'=8,'zl'=4,'col'=2] {'x'}, dimensions={0} | all-to-all | bytes 442368 | tf_op jit(solution)/shard_map/all_to_all | solution.py:248
  22.4 50.4 %all-to-all-start.2 = ((f32[32,1,128]{2,1,0:T(1,128)}), f32[32,1,128]{2,1,0:T(1,128)S(1)}, u32[]{:S(2)}, u32[]{:S(2)}) async-start(f32[32,1,128]{2,1,0:T(1,128)} %broadcast_in_dim.27), calls=%async_computation.2 | async-start | bytes 32768 | tf_op jit(solution)/shard_map/all_to_all | solution.py:22
  73.4 6.6 %all-to-all-done.2 = f32[32,1,128]{2,1,0:T(1,128)S(1)} async-done(((f32[32,1,128]{2,1,0:T(1,128)}), f32[32,1,128]{2,1,0:T(1,128)S(1)}, u32[]{:S(2)}, u32[]{:S(2)}) %all-to-all-start.2) | async-done | bytes 16416 | tf_op jit(solution)/shard_map/all_to_all | solution.py:22
  80.7 4.0 %all-to-all-start = ((bf16[8,2,64,128]{3,2,1,0:T(8,128)(2,1)}), bf16[8,2,64,128]{3,2,1,0:T(8,128)(2,1)S(1)}, u32[]{:S(2)}, u32[]{:S(2)}) async-start(bf16[8,2,64,128]{3,2,1,0:T(8,128)(2,1)} %bitcast.4), calls=%async_computation | async-start | bytes 524288 | tf_op jit(solution)/shard_map/all_to_all | solution.py:274
  85.8 39.6 %all-gather = bf16[80,16,256]{2,1,0:T(8,128)(2,1)S(1)} all-gather(bf16[10,16,256]{2,1,0:T(8,128)(2,1)S(1)} %pad_maximum_fusion.2), channel_id=2, replica_groups=mesh['img'=2,'x'=4,'zh'=8,'zl'=4,'col'=2] {'zh'}, dimensions={0}, use_global_device_ids=true | all-gather | bytes 737280 | tf_op jit(solution)/shard_map/all_gather | solution.py:265
  125.4 1.8 conv_one.1
  127.2 8.4 %all-to-all-start.3 = ((bf16[4,128,256]{2,1,0:T(8,128)(2,1)}), bf16[4,128,256]{2,1,0:T(8,128)(2,1)S(1)}, u32[]{:S(2)}, u32[]{:S(2)}) async-start(bf16[4,128,256]{2,1,0:T(8,128)(2,1)} %conv_one.1), calls=%async_computation.3 | async-start | bytes 524288 | tf_op jit(solution)/shard_map/all_to_all | solution.py:309
  137.5 4.1 %collective-permute-start.1 = (bf16[64,512]{1,0:T(8,128)(2,1)S(1)}, bf16[64,512]{1,0:T(8,128)(2,1)S(1)}, u32[]{:S(2)}, u32[]{:S(2)}) collective-permute-start(bf16[64,512]{1,0:T(8,128)(2,1)S(1)} %bitcast.66), channel_id=1, source_target_pairs={{0,2},{2,4},{4,6},{6,8},{8,10},{10,12},{12,14},{14,16},{16,18},{18... | collective-permute-start | bytes 196616 | tf_op jit(solution)/shard_map/ppermute | solution.py:28
  141.6 1.3 collective-permute-start.2
  144.2 4.5 %collective-permute-done.2 = bf16[64,512]{1,0:T(8,128)(2,1)S(1)} collective-permute-done((bf16[64,512]{1,0:T(8,128)(2,1)S(1)}, bf16[64,512]{1,0:T(8,128)(2,1)S(1)}, u32[]{:S(2)}, u32[]{:S(2)}) %collective-permute-start.2) | collective-permute-done | bytes 65568 | tf_op jit(solution)/shard_map/ppermute | solution.py:28
  149.3 9.8 %all-to-all-start.4 = ((f32[32,1,128]{2,1,0:T(1,128)}), f32[32,1,128]{2,1,0:T(1,128)S(1)}, u32[]{:S(2)}, u32[]{:S(2)}) async-start(f32[32,1,128]{2,1,0:T(1,128)} %broadcast_in_dim.58), calls=%async_computation.4 | async-start | bytes 32768 | tf_op jit(solution)/shard_map/all_to_all | solution.py:22
  159.2 2.5 %all_gather.37 = bf16[3,128,512]{2,1,0:T(8,128)(2,1)S(1)} all-gather(bf16[3,64,512]{2,1,0:T(8,128)(2,1)S(1)} %pad_maximum_fusion.1), channel_id=1, replica_groups=mesh['img'=2,'x'=4,'zh'=8,'zl'=4,'col'=2] {'col'}, dimensions={1}, use_global_device_ids=true | all-gather | bytes 589824 | tf_op jit(solution)/shard_map/all_gather | solution.py:326
  162.1 2.0 all-gather.1
  164.8 1.6 all-to-all-done.4
  166.4 1.3 collective-permute-start.3
  167.7 1.3 collective-permute-start.4
  170.4 15.9 %all-to-all-start.5 = ((f32[8,1,128]{2,1,0:T(1,128)}), f32[8,1,128]{2,1,0:T(1,128)S(1)}, u32[]{:S(2)}, u32[]{:S(2)}) async-start(f32[8,1,128]{2,1,0:T(1,128)} %broadcast_in_dim.60), calls=%async_computation.5 | async-start | bytes 8192 | tf_op jit(solution)/shard_map/all_to_all | solution.py:22
  186.3 2.4 %all-gather.2 = bf16[4,2,128,256]{3,2,1,0:T(8,128)(2,1)S(1)} all-gather(bf16[2,2,128,256]{3,2,1,0:T(8,128)(2,1)S(1)} %pad_maximum_fusion), channel_id=4, replica_groups=mesh['img'=2,'x'=4,'zh'=8,'zl'=4,'col'=2] {'col'}, dimensions={0}, use_global_device_ids=true | all-gather | bytes 786432 | tf_op jit(solution)/shard_map/all_gather | solution.py:331
  188.8 18.5 %all-to-all-done.5 = f32[8,1,128]{2,1,0:T(1,128)S(1)} async-done(((f32[8,1,128]{2,1,0:T(1,128)}), f32[8,1,128]{2,1,0:T(1,128)S(1)}, u32[]{:S(2)}, u32[]{:S(2)}) %all-to-all-start.5) | async-done | bytes 4128 | tf_op jit(solution)/shard_map/all_to_all | solution.py:22
  209.2 5.2 %conv_two.1 = bf16[384,256]{1,0:T(8,128)(2,1)} custom-call(s32[1]{0:T(128)} %bitcast.1.at_ref, bf16[2,640,256]{2,1,0:T(8,128)(2,1)} %copy-done, bf16[384,256]{1,0:T(8,128)(2,1)} %dynamic-slice_convert_fusion.res_ref, f32[1,256]{1,0:T(1,128)} %get-tuple-element.34.bias_ref, bf16[32,18,16,256]{3,2,1,0:T(8,128)(2,1)} %all-gather.6.cloned.1.call-done.w_ref), custom_call_target="tpu_custom_call" | custom-call | tf_op jit(solution)/shard_map/conv_two/pallas_call | solution.py:346
  214.4 4.9 %all-gather.3 = bf16[768,256]{1,0:T(8,128)(2,1)} all-gather(bf16[384,256]{1,0:T(8,128)(2,1)} %conv_two.1), channel_id=5, replica_groups=mesh['img'=2,'x'=4,'zh'=8,'zl'=4,'col'=2] {'col'}, dimensions={0}, use_global_device_ids=true | all-gather | bytes 589824 | tf_op jit(solution)/shard_map/all_gather | solution.py:355
  219.3 5.6 %conv_up.1 = (bf16[2,128,256]{2,1,0:T(8,128)(2,1)}, bf16[2,128,256]{2,1,0:T(8,128)(2,1)}) custom-call(s32[1]{0:T(128)} %bitcast.at_ref, bf16[2,384,256]{2,1,0:T(8,128)(2,1)} %bitcast.55, f32[1,256]{1,0:T(1,128)} %get-tuple-element.33.bias_ref, bf16[32,18,16,256]{3,2,1,0:T(8,128)(2,1)} %all-gather.6.cloned.1.call-done.w_ref), custom_call_target="tpu_custom_call" | custom-call | tf_op jit(solution)/shard_map/conv_up/pallas_call | solution.py:359
  224.9 2.1 collective-permute-start.5
  227.0 1.4 collective-permute-done.5.theirs_ref
  (106 shorter events, 17.5 us)
Async XLA Ops:
  6.5 14.0 %copy-start.2 = (bf16[1,64,512]{2,1,0:T(8,128)(2,1)S(1)}, bf16[1,64,512]{2,1,0:T(8,128)(2,1)}, u32[]{:S(2)}) copy-start(bf16[1,64,512]{2,1,0:T(8,128)(2,1)} %param.11) | copy-start | bytes 196612
  6.5 202.6 %all-gather.6.cloned.1.call-start = ((), (), s32[]{:S(2)}) async-start(), calls=%async_computation.6 | async-start | bytes 4866048 | tf_op jit(solution)/shard_map/all_gather | solution.py:250
  20.6 52.3 %collective-permute-start = (bf16[64,512]{1,0:T(8,128)(2,1)S(1)}, bf16[64,512]{1,0:T(8,128)(2,1)S(1)}, u32[]{:S(2)}, u32[]{:S(2)}) collective-permute-start(bf16[64,512]{1,0:T(8,128)(2,1)S(1)} %bitcast.64), channel_id=1, source_target_pairs={{6,8},{14,16},{22,24},{30,32},{38,40},{46,48},{54,56},{62,64},{70,... | collective-permute-start | bytes 196616 | tf_op jit(solution)/shard_map/ppermute | solution.py:269
  22.4 57.6 %all-to-all-start.2 = ((f32[32,1,128]{2,1,0:T(1,128)}), f32[32,1,128]{2,1,0:T(1,128)S(1)}, u32[]{:S(2)}, u32[]{:S(2)}) async-start(f32[32,1,128]{2,1,0:T(1,128)} %broadcast_in_dim.27), calls=%async_computation.2 | async-start | bytes 32768 | tf_op jit(solution)/shard_map/all_to_all | solution.py:22
  72.9 11.8 %copy-start.3 = (f32[512]{0:T(512)S(1)}, f32[512]{0:T(512)}, u32[]{:S(2)}) copy-start(f32[512]{0:T(512)} %param.12) | copy-start | bytes 6148
  72.9 12.1 %copy-start.4 = (f32[512]{0:T(512)S(1)}, f32[512]{0:T(512)}, u32[]{:S(2)}) copy-start(f32[512]{0:T(512)} %param.13) | copy-start | bytes 6148
  73.3 62.3 %copy-start.5 = (f32[512]{0:T(512)S(1)}, f32[512]{0:T(512)}, u32[]{:S(2)}) copy-start(f32[512]{0:T(512)} %param.16) | copy-start | bytes 6148
  73.3 62.5 %copy-start.6 = (f32[512]{0:T(512)S(1)}, f32[512]{0:T(512)}, u32[]{:S(2)}) copy-start(f32[512]{0:T(512)} %param.17) | copy-start | bytes 6148
  73.3 62.6 %copy-start.7 = (f32[512]{0:T(512)S(1)}, f32[512]{0:T(512)}, u32[]{:S(2)}) copy-start(f32[512]{0:T(512)} %param.15) | copy-start | bytes 6148
  73.3 62.7 %copy-start.8 = (f32[512]{0:T(512)S(1)}, f32[512]{0:T(512)}, u32[]{:S(2)}) copy-start(f32[512]{0:T(512)} %param.19) | copy-start | bytes 6148
  73.3 63.5 %copy-start.9 = (f32[512]{0:T(512)S(1)}, f32[512]{0:T(512)}, u32[]{:S(2)}) copy-start(f32[512]{0:T(512)} %param.21) | copy-start | bytes 6148
  80.7 44.7 %all-to-all-start = ((bf16[8,2,64,128]{3,2,1,0:T(8,128)(2,1)}), bf16[8,2,64,128]{3,2,1,0:T(8,128)(2,1)S(1)}, u32[]{:S(2)}, u32[]{:S(2)}) async-start(bf16[8,2,64,128]{3,2,1,0:T(8,128)(2,1)} %bitcast.4), calls=%async_computation | async-start | bytes 524288 | tf_op jit(solution)/shard_map/all_to_all | solution.py:274
  127.2 15.8 %all-to-all-start.3 = ((bf16[4,128,256]{2,1,0:T(8,128)(2,1)}), bf16[4,128,256]{2,1,0:T(8,128)(2,1)S(1)}, u32[]{:S(2)}, u32[]{:S(2)}) async-start(bf16[4,128,256]{2,1,0:T(8,128)(2,1)} %conv_one.1), calls=%async_computation.3 | async-start | bytes 524288 | tf_op jit(solution)/shard_map/all_to_all | solution.py:309
  137.5 6.8 %collective-permute-start.1 = (bf16[64,512]{1,0:T(8,128)(2,1)S(1)}, bf16[64,512]{1,0:T(8,128)(2,1)S(1)}, u32[]{:S(2)}, u32[]{:S(2)}) collective-permute-start(bf16[64,512]{1,0:T(8,128)(2,1)S(1)} %bitcast.66), channel_id=1, source_target_pairs={{0,2},{2,4},{4,6},{6,8},{8,10},{10,12},{12,14},{14,16},{16,18},{18... | collective-permute-start | bytes 196616 | tf_op jit(solution)/shard_map/ppermute | solution.py:28
  141.6 7.1 %collective-permute-start.2 = (bf16[64,512]{1,0:T(8,128)(2,1)S(1)}, bf16[64,512]{1,0:T(8,128)(2,1)S(1)}, u32[]{:S(2)}, u32[]{:S(2)}) collective-permute-start(bf16[64,512]{1,0:T(8,128)(2,1)S(1)} %bitcast.67), channel_id=1, source_target_pairs={{2,0},{4,2},{6,4},{8,6},{10,8},{12,10},{14,12},{16,14},{18,16},{20... | collective-permute-start | bytes 196616 | tf_op jit(solution)/shard_map/ppermute | solution.py:28
  149.3 17.0 %all-to-all-start.4 = ((f32[32,1,128]{2,1,0:T(1,128)}), f32[32,1,128]{2,1,0:T(1,128)S(1)}, u32[]{:S(2)}, u32[]{:S(2)}) async-start(f32[32,1,128]{2,1,0:T(1,128)} %broadcast_in_dim.58), calls=%async_computation.4 | async-start | bytes 32768 | tf_op jit(solution)/shard_map/all_to_all | solution.py:22
  166.4 19.9 %collective-permute-start.3 = (bf16[2,128,256]{2,1,0:T(8,128)(2,1)S(1)}, bf16[2,128,256]{2,1,0:T(8,128)(2,1)S(1)}, u32[]{:S(2)}, u32[]{:S(2)}) collective-permute-start(bf16[2,128,256]{2,1,0:T(8,128)(2,1)S(1)} %bitcast.51), channel_id=1, source_target_pairs={{0,2},{2,4},{4,6},{6,8},{8,10},{10,12},{12,14},{14,16},{16,18},{18... | collective-permute-start | bytes 393224 | tf_op jit(solution)/shard_map/ppermute | solution.py:330
  167.7 18.6 %collective-permute-start.4 = (bf16[2,128,256]{2,1,0:T(8,128)(2,1)S(1)}, bf16[2,128,256]{2,1,0:T(8,128)(2,1)S(1)}, u32[]{:S(2)}, u32[]{:S(2)}) collective-permute-start(bf16[2,128,256]{2,1,0:T(8,128)(2,1)S(1)} %bitcast.52), channel_id=1, source_target_pairs={{0,4},{2,6},{4,8},{6,10},{8,12},{10,14},{12,16},{14,18},{16,20},{1... | collective-permute-start | bytes 393224 | tf_op jit(solution)/shard_map/ppermute | solution.py:330
  170.4 36.9 %all-to-all-start.5 = ((f32[8,1,128]{2,1,0:T(1,128)}), f32[8,1,128]{2,1,0:T(1,128)S(1)}, u32[]{:S(2)}, u32[]{:S(2)}) async-start(f32[8,1,128]{2,1,0:T(1,128)} %broadcast_in_dim.60), calls=%async_computation.5 | async-start | bytes 8192 | tf_op jit(solution)/shard_map/all_to_all | solution.py:22
  208.3 0.9 copy-start
  224.9 3.5 %collective-permute-start.5 = (bf16[2,128,256]{2,1,0:T(8,128)(2,1)}, bf16[2,128,256]{2,1,0:T(8,128)(2,1)S(1)}, u32[]{:S(2)}, u32[]{:S(2)}) collective-permute-start(bf16[2,128,256]{2,1,0:T(8,128)(2,1)} %get-tuple-element.28), channel_id=1, source_target_pairs={{0,1},{1,0},{2,3},{3,2},{4,5},{5,4},{6,7},{7,6},{8,9},{9,8},{10,11... | collective-permute-start | bytes 393224 | tf_op jit(solution)/shard_map/ppermute | solution.py:372
  228.4 0.9 copy-start.1
Sparse Core Ops, SparseCore 0:
  20.7 166.3 all-gather.5

commit v7 on v6

--- a/solution.py
+++ b/solution.py
@@ -31,14 +31,6 @@
 def fetch(count, by):
     above = [(2 * (i - by), 2 * i) for i in range(by, count)]
     return above + [(2 * (i + by) + 1, 2 * i + 1) for i in range(count - by)]
-
-
-def put_shifted(S, row, cols, y, lanes):
-    at = pl.ds(row * cols, cols)
-    column = lax.broadcasted_iota(jnp.int32, y.shape, 0)
-    S[1, at, lanes] = y.astype(BF16)
-    S[0, at, lanes] = jnp.where(column == 0, 0.0, pltpu.roll(y, 1, 0)).astype(BF16)
-    S[2, at, lanes] = jnp.where(column == cols - 1, 0.0, pltpu.roll(y, cols - 1, 0)).astype(BF16)
 
 
 def silu(u):
@@ -113,29 +105,40 @@
 
 
 def fetch_weights(w_ref, base, held, arrived):
+    lines = held.shape[1]
     copies = [
-        pltpu.make_async_copy(w_ref.at[:, base + t], held.at[t], arrived.at[t]) for t in range(9)
+        pltpu.make_async_copy(
+            w_ref.at[pl.ds(h * lines, lines), pl.ds(base, 9)], held.at[h], arrived.at[h]
+        )
+        for h in range(2)
     ]
     for copy in copies:
         copy.start()
     return copies
 
 
-def conv_two_kernel(cols, rows, image_rows, at_ref, x_ref, res_ref, bias_ref, w_ref, out_ref, S, held, arrived):
+def moved_right(y, cols):
+    column = lax.broadcasted_iota(jnp.int32, y.shape, 0) % cols
+    return jnp.where(column == 0, 0.0, pltpu.roll(y, 1, 0))
+
+
+def moved_left(y, cols):
+    column = lax.broadcasted_iota(jnp.int32, y.shape, 0) % cols
+    return jnp.where(column == cols - 1, 0.0, pltpu.roll(y, y.shape[0] - 1, 0))
+
+
+def conv_two_kernel(cols, rows, image_rows, at_ref, x_ref, res_ref, bias_ref, w_ref, out_ref, held, arrived):
     copies = fetch_weights(w_ref, 0, held, arrived)
     outs = out_ref.shape[1]
-    for i in range(rows + 2):
-        for h in range(2):
-            y = x_ref[h, i * cols : (i + 1) * cols, :].astype(F32)
-            put_shifted(S, i, cols, y, slice(h * outs, (h + 1) * outs))
-    total = jnp.broadcast_to(bias_ref[...], out_ref.shape)
-    for r in range(3):
-        for k in range(3):
-            copies[3 * r + k].wait()
-            piece = held[3 * r + k].reshape(-1, outs)
-            total += jnp.dot(
-                S[k, r * cols : (r + rows) * cols, :], piece, preferred_element_type=F32
-            )
+    totals = [jnp.zeros(out_ref.shape, F32) for _ in range(3)]
+    for h in range(2):
+        copies[h].wait()
+        for r in range(3):
+            x = x_ref[h, r * cols : (r + rows) * cols, :]
+            for k in range(3):
+                piece = held[h, :, 3 * r + k].reshape(-1, outs)
+                totals[k] += jnp.dot(x, piece, preferred_element_type=F32)
+    total = totals[1] + moved_right(totals[0], cols) + moved_left(totals[2], cols) + bias_ref[...]
     first = at_ref[0] - rows // 2
     for i in range(rows):
         at = slice(i * cols, (i + 1) * cols)
@@ -144,31 +147,28 @@
         out_ref[at, :] = jnp.where(inside, y, 0.0).astype(BF16)
 
 
-def conv_up_kernel(cols, at_ref, x_ref, bias_ref, w_ref, mine_ref, theirs_ref, S, full, held, arrived):
+def conv_up_kernel(cols, at_ref, x_ref, bias_ref, w_ref, mine_ref, theirs_ref, full, held, arrived):
     copies = fetch_weights(w_ref, 9, held, arrived)
     outs = mine_ref.shape[2]
-    for i in range(3):
-        for h in range(2):
-            y = x_ref[h, i * cols : (i + 1) * cols, :].astype(F32)
-            put_shifted(S, i, cols, y, slice(h * outs, (h + 1) * outs))
-    total = jnp.broadcast_to(bias_ref[...], (4 * cols, outs))
-    for r in range(3):
-        for k in range(3):
-            copies[3 * r + k].wait()
-            piece = held[3 * r + k].reshape(-1, outs)
-            phases = []
-            for p in range(2):
-                start = (r + 1 + p) // 2 * cols
-                phases += [S[(k + 1 + q) // 2, start : start + cols, :] for q in range(2)]
-            total += jnp.dot(jnp.concatenate(phases), piece, preferred_element_type=F32)
+    totals = [jnp.zeros((2 * cols, outs), F32) for _ in range(3)]
+    for h in range(2):
+        copies[h].wait()
+        for r in range(3):
+            starts = [(r + 1 + p) // 2 * cols for p in range(2)]
+            x = jnp.concatenate([x_ref[h, start : start + cols, :] for start in starts])
+            for k in range(3):
+                piece = held[h, :, 3 * r + k].reshape(-1, outs)
+                totals[k] += jnp.dot(x, piece, preferred_element_type=F32)
+    middle = totals[1] + bias_ref[...]
+    even = moved_right(totals[0], cols) + middle + totals[2]
+    odd = totals[0] + middle + moved_left(totals[2], cols)
     mine = pl.multiple_of(at_ref[0] * cols, cols)
     theirs = pl.multiple_of((1 - at_ref[0]) * cols, cols)
     for p in range(2):
         for k in range(2):
             lanes = slice(k * 128, (k + 1) * 128)
-            for q in range(2):
-                phase = (2 * p + q) * cols
-                full[p, k, pl.ds(q, cols, stride=2), :] = total[phase : phase + cols, lanes]
+            for q, y in enumerate((even, odd)):
+                full[p, k, pl.ds(q, cols, stride=2), :] = y[p * cols : (p + 1) * cols, lanes]
             mine_ref[p, :, lanes] = full[p, k, pl.ds(mine, cols), :].astype(BF16)
             theirs_ref[p, :, lanes] = full[p, k, pl.ds(theirs, cols), :].astype(BF16)
 
@@ -322,7 +322,8 @@
 
     both = lax.all_gather(hidden, "col")
     three, _ = lax.optimization_barrier((three, sums_two))
-    stats = jnp.sum(sum_over(sums_two[:1], ("x", "zl", "col")), axis=0, keepdims=True)
+    stats = sum_over(sums_two[:1], ("x", "zl", "col"))
+    stats = jnp.sum(stats, axis=0, keepdims=True)
     three = lax.all_gather(jnp.stack(three), "col", axis=1, tiled=True)
     residual = own_half(moved(three.reshape(3 * cols, channels), move))
     stats, both, residual = lax.optimization_barrier((stats, both, residual))
@@ -340,16 +341,16 @@
 
     rows = 3
     held = [
-        pltpu.VMEM((9, weights.shape[0]) + weights.shape[2:], BF16),
-        pltpu.SemaphoreType.DMA((9,)),
+        pltpu.VMEM((2, nz // 2, 9) + weights.shape[2:], BF16),
+        pltpu.SemaphoreType.DMA((2,)),
     ]
     block = pl.pallas_call(
         functools.partial(conv_two_kernel, cols, rows, image_rows),
         out_shape=jax.ShapeDtypeStruct((rows * cols, half), BF16),
         in_specs=[SM, VM, VM, VM, HB],
         out_specs=VM,
-        scratch_shapes=[pltpu.VMEM((3, (rows + 2) * cols, channels), BF16)] + held,
-        compiler_params=grant(58),
+        scratch_shapes=held,
+        compiler_params=grant(50),
         name="conv_two",
     )(at, normed, residual, bias_two, weights)
     block = lax.all_gather(block, "col")
@@ -361,12 +362,8 @@
         out_shape=(side, side),
         in_specs=[SM, VM, VM, HB],
         out_specs=(VM, VM),
-        scratch_shapes=[
-            pltpu.VMEM((3, 3 * cols, channels), BF16),
-            pltpu.VMEM((2, 2, 2 * cols, 128), F32),
-        ]
-        + held,
-        compiler_params=grant(58),
+        scratch_shapes=[pltpu.VMEM((2, 2, 2 * cols, 128), F32)] + held,
+        compiler_params=grant(50),
         name="conv_up",
     )(core, block, bias_up, weights)
     theirs = lax.ppermute(theirs, "col", [(0, 1), (1, 0)])

time: 238 us -> 227 us (0.954)
  Pallas kernels: 14.6 us -> 8.95 us
  local copies, waits for them, and re-layouts: 11.2 us -> 8.18 us
    pallas_call x1, Pallas kernels: 5.59 us -> 2.4 us  [on_device(): pl.pallas_call(functools.partial(conv_up_kernel, cols), out_shape=(side,...]
    pallas_call x1, Pallas kernels: 5.19 us -> 2.73 us  [on_device(): pl.pallas_call(functools.partial(conv_two_kernel, cols, rows, image_rows)...]
  transfers between devices with their start and end apart: 12 -> 12, of which waited for: 6 -> 7; matrix products, arithmetic and copies ran while one was open for 4% -> 3% of each run, Pallas kernels for 1% -> 1%
where the time goes in v7:
time: 227 us
  starting transfers between devices  100 us (44%)
  blocking collectives  59.4 us (26%)
  waiting for transfers between devices  33.3 us (15%)
  between operations  14 us (6%)
  Pallas kernels  8.95 us (4%)
  local copies, waits for them, and re-layouts  8.18 us (4%)
    all_to_all x3, starting transfers between devices, sum_over(): return lax.all_to_all(sent, axes, 0, 0, tiled=True)  76.8 us
    all_gather x1, blocking collectives, on_device(): weights_one = lax.all_gather(jnp.concatenate([hold_one, terms[None]]), 'zh')  39.6 us
    all_to_all x3, waiting for transfers between devices, sum_over(): return lax.all_to_all(sent, axes, 0, 0, tiled=True)  27.2 us
    all_to_all x1, blocking collectives, on_device(): lax.all_to_all(jnp.broadcast_to(hold, (nx, 27, k_own, half)), 'x', 0, 0,...  10.2 us
    all_to_all x1, starting transfers between devices, on_device(): parts = lax.all_to_all(parts, 'zl', 0, 0, tiled=True)  8.52 us
    ppermute x2, starting transfers between devices, shifted_rows(): return lax.ppermute(values, axis, pairs)  5.44 us
  transfers between devices with their start and end apart: 12, of which 7 were waited for; matrix products, arithmetic and copies ran while one was open for 3% of the time, Pallas kernels for 1%

profile of v7, /device:TPU:33, one launch (start us, length us, event | category | flops | bytes accessed | tf_op | source)
XLA Modules:
  0.0 226.6 jit_solution(18049001001610450729)
XLA Ops:
  9.4 10.2 %all_to_all.35 = bf16[4,27,4,256]{3,2,1,0:T(4,128)(2,1)S(1)} all-to-all(bf16[4,27,4,256]{3,2,1,0:T(4,128)(2,1)S(1)} %broadcast_in_dim.26), channel_id=1, replica_groups=mesh['img'=2,'x'=4,'zh'=8,'zl'=4,'col'=2] {'x'}, dimensions={0} | all-to-all | bytes 442368 | tf_op jit(solution)/shard_map/all_to_all | solution.py:248
  22.4 50.4 %all-to-all-start.2 = ((f32[32,1,128]{2,1,0:T(1,128)}), f32[32,1,128]{2,1,0:T(1,128)S(1)}, u32[]{:S(2)}, u32[]{:S(2)}) async-start(f32[32,1,128]{2,1,0:T(1,128)} %broadcast_in_dim.27), calls=%async_computation.2 | async-start | bytes 32768 | tf_op jit(solution)/shard_map/all_to_all | solution.py:22
  73.4 6.6 %all-to-all-done.2 = f32[32,1,128]{2,1,0:T(1,128)S(1)} async-done(((f32[32,1,128]{2,1,0:T(1,128)}), f32[32,1,128]{2,1,0:T(1,128)S(1)}, u32[]{:S(2)}, u32[]{:S(2)}) %all-to-all-start.2) | async-done | bytes 16416 | tf_op jit(solution)/shard_map/all_to_all | solution.py:22
  80.7 4.0 %all-to-all-start = ((bf16[8,2,64,128]{3,2,1,0:T(8,128)(2,1)}), bf16[8,2,64,128]{3,2,1,0:T(8,128)(2,1)S(1)}, u32[]{:S(2)}, u32[]{:S(2)}) async-start(bf16[8,2,64,128]{3,2,1,0:T(8,128)(2,1)} %bitcast.4), calls=%async_computation | async-start | bytes 524288 | tf_op jit(solution)/shard_map/all_to_all | solution.py:274
  85.8 39.6 %all-gather = bf16[80,16,256]{2,1,0:T(8,128)(2,1)S(1)} all-gather(bf16[10,16,256]{2,1,0:T(8,128)(2,1)S(1)} %pad_maximum_fusion.2), channel_id=2, replica_groups=mesh['img'=2,'x'=4,'zh'=8,'zl'=4,'col'=2] {'zh'}, dimensions={0}, use_global_device_ids=true | all-gather | bytes 737280 | tf_op jit(solution)/shard_map/all_gather | solution.py:265
  125.4 1.8 conv_one.1
  127.1 8.5 %all-to-all-start.3 = ((bf16[4,128,256]{2,1,0:T(8,128)(2,1)}), bf16[4,128,256]{2,1,0:T(8,128)(2,1)S(1)}, u32[]{:S(2)}, u32[]{:S(2)}) async-start(bf16[4,128,256]{2,1,0:T(8,128)(2,1)} %conv_one.1), calls=%async_computation.3 | async-start | bytes 524288 | tf_op jit(solution)/shard_map/all_to_all | solution.py:309
  136.9 4.1 %collective-permute-start.1 = (bf16[64,512]{1,0:T(8,128)(2,1)S(1)}, bf16[64,512]{1,0:T(8,128)(2,1)S(1)}, u32[]{:S(2)}, u32[]{:S(2)}) collective-permute-start(bf16[64,512]{1,0:T(8,128)(2,1)S(1)} %bitcast.66), channel_id=1, source_target_pairs={{0,2},{2,4},{4,6},{6,8},{8,10},{10,12},{12,14},{14,16},{16,18},{18... | collective-permute-start | bytes 196616 | tf_op jit(solution)/shard_map/ppermute | solution.py:28
  141.1 1.3 collective-permute-start.2
  144.1 3.8 %collective-permute-done.2 = bf16[64,512]{1,0:T(8,128)(2,1)S(1)} collective-permute-done((bf16[64,512]{1,0:T(8,128)(2,1)S(1)}, bf16[64,512]{1,0:T(8,128)(2,1)S(1)}, u32[]{:S(2)}, u32[]{:S(2)}) %collective-permute-start.2) | collective-permute-done | bytes 65568 | tf_op jit(solution)/shard_map/ppermute | solution.py:28
  148.4 9.9 %all-to-all-start.4 = ((f32[32,1,128]{2,1,0:T(1,128)}), f32[32,1,128]{2,1,0:T(1,128)S(1)}, u32[]{:S(2)}, u32[]{:S(2)}) async-start(f32[32,1,128]{2,1,0:T(1,128)} %broadcast_in_dim.58), calls=%async_computation.4 | async-start | bytes 32768 | tf_op jit(solution)/shard_map/all_to_all | solution.py:22
  158.4 2.5 %all_gather.37 = bf16[3,128,512]{2,1,0:T(8,128)(2,1)S(1)} all-gather(bf16[3,64,512]{2,1,0:T(8,128)(2,1)S(1)} %pad_maximum_fusion.1), channel_id=1, replica_groups=mesh['img'=2,'x'=4,'zh'=8,'zl'=4,'col'=2] {'col'}, dimensions={1}, use_global_device_ids=true | all-gather | bytes 589824 | tf_op jit(solution)/shard_map/all_gather | solution.py:327
  161.3 2.0 all-gather.1
  163.3 2.2 all-to-all-done.4
  165.5 1.3 collective-permute-start.3
  166.8 1.3 collective-permute-start.4
  169.5 16.4 %all-to-all-start.5 = ((f32[8,1,128]{2,1,0:T(1,128)}), f32[8,1,128]{2,1,0:T(1,128)S(1)}, u32[]{:S(2)}, u32[]{:S(2)}) async-start(f32[8,1,128]{2,1,0:T(1,128)} %broadcast_in_dim.60), calls=%async_computation.5 | async-start | bytes 8192 | tf_op jit(solution)/shard_map/all_to_all | solution.py:22
  185.9 2.4 %all-gather.2 = bf16[4,2,128,256]{3,2,1,0:T(8,128)(2,1)S(1)} all-gather(bf16[2,2,128,256]{3,2,1,0:T(8,128)(2,1)S(1)} %pad_maximum_fusion), channel_id=4, replica_groups=mesh['img'=2,'x'=4,'zh'=8,'zl'=4,'col'=2] {'col'}, dimensions={0}, use_global_device_ids=true | all-gather | bytes 786432 | tf_op jit(solution)/shard_map/all_gather | solution.py:332
  188.3 18.4 %all-to-all-done.5 = f32[8,1,128]{2,1,0:T(1,128)S(1)} async-done(((f32[8,1,128]{2,1,0:T(1,128)}), f32[8,1,128]{2,1,0:T(1,128)S(1)}, u32[]{:S(2)}, u32[]{:S(2)}) %all-to-all-start.5) | async-done | bytes 4128 | tf_op jit(solution)/shard_map/all_to_all | solution.py:22
  206.8 1.1 norm_two.1.x_ref
  207.9 2.7 %conv_two.1 = bf16[384,256]{1,0:T(8,128)(2,1)S(1)} custom-call(s32[1]{0:T(128)} %bitcast.1.at_ref, bf16[2,640,256]{2,1,0:T(8,128)(2,1)S(1)} %norm_two.1.x_ref, bf16[384,256]{1,0:T(8,128)(2,1)S(1)} %dynamic-slice_convert_fusion.res_ref, f32[1,256]{1,0:T(1,128)S(1)} %get-tuple-element.34.bias_ref, bf16[32,18,16,256]{3,2,1,0:T(8,128)(2,1)} %all-gather.6.cloned.1.call-done.w_ref), custom_call_target="tpu_custom_call" | custom-call | tf_op jit(solution)/shard_map/conv_two/pallas_call | solution.py:347
  210.6 2.7 %all-gather.3 = bf16[768,256]{1,0:T(8,128)(2,1)S(1)} all-gather(bf16[384,256]{1,0:T(8,128)(2,1)S(1)} %conv_two.1), channel_id=5, replica_groups=mesh['img'=2,'x'=4,'zh'=8,'zl'=4,'col'=2] {'col'}, dimensions={0}, use_global_device_ids=true | all-gather | bytes 589824 | tf_op jit(solution)/shard_map/all_gather | solution.py:356
  213.4 2.4 %conv_up.1 = (bf16[2,128,256]{2,1,0:T(8,128)(2,1)S(1)}, bf16[2,128,256]{2,1,0:T(8,128)(2,1)S(1)}) custom-call(s32[1]{0:T(128)} %bitcast.at_ref, bf16[2,384,256]{2,1,0:T(8,128)(2,1)S(1)} %bitcast.50, f32[1,256]{1,0:T(1,128)S(1)} %get-tuple-element.33.bias_ref, bf16[32,18,16,256]{3,2,1,0:T(8,128)(2,1)} %all-gather.6.cloned.1.call-done.w_ref), custom_call_target="tpu_custom_call" | custom-call | tf_op jit(solution)/shard_map/conv_up/pallas_call | solution.py:360
  215.8 2.3 %collective-permute-start.5 = (bf16[2,128,256]{2,1,0:T(8,128)(2,1)S(1)}, bf16[2,128,256]{2,1,0:T(8,128)(2,1)S(1)}, u32[]{:S(2)}, u32[]{:S(2)}) collective-permute-start(bf16[2,128,256]{2,1,0:T(8,128)(2,1)S(1)} %get-tuple-element.28), channel_id=1, source_target_pairs={{0,1},{1,0},{2,3},{3,2},{4,5},{5,4},{6,7},{7,6},{8,9},{9,8},{10,11... | collective-permute-start | bytes 393224 | tf_op jit(solution)/shard_map/ppermute | solution.py:369
  (102 shorter events, 14.8 us)
Async XLA Ops:
  6.5 14.0 %copy-start = (bf16[1,64,512]{2,1,0:T(8,128)(2,1)S(1)}, bf16[1,64,512]{2,1,0:T(8,128)(2,1)}, u32[]{:S(2)}) copy-start(bf16[1,64,512]{2,1,0:T(8,128)(2,1)} %param.11) | copy-start | bytes 196612
  6.5 201.3 %all-gather.6.cloned.1.call-start = ((), (), s32[]{:S(2)}) async-start(), calls=%async_computation.6 | async-start | bytes 4866048 | tf_op jit(solution)/shard_map/all_gather | solution.py:250
  20.6 52.3 %collective-permute-start = (bf16[64,512]{1,0:T(8,128)(2,1)S(1)}, bf16[64,512]{1,0:T(8,128)(2,1)S(1)}, u32[]{:S(2)}, u32[]{:S(2)}) collective-permute-start(bf16[64,512]{1,0:T(8,128)(2,1)S(1)} %bitcast.64), channel_id=1, source_target_pairs={{6,8},{14,16},{22,24},{30,32},{38,40},{46,48},{54,56},{62,64},{70,... | collective-permute-start | bytes 196616 | tf_op jit(solution)/shard_map/ppermute | solution.py:269
  22.4 57.6 %all-to-all-start.2 = ((f32[32,1,128]{2,1,0:T(1,128)}), f32[32,1,128]{2,1,0:T(1,128)S(1)}, u32[]{:S(2)}, u32[]{:S(2)}) async-start(f32[32,1,128]{2,1,0:T(1,128)} %broadcast_in_dim.27), calls=%async_computation.2 | async-start | bytes 32768 | tf_op jit(solution)/shard_map/all_to_all | solution.py:22
  72.9 11.8 %copy-start.1 = (f32[512]{0:T(512)S(1)}, f32[512]{0:T(512)}, u32[]{:S(2)}) copy-start(f32[512]{0:T(512)} %param.12) | copy-start | bytes 6148
  72.9 12.1 %copy-start.2 = (f32[512]{0:T(512)S(1)}, f32[512]{0:T(512)}, u32[]{:S(2)}) copy-start(f32[512]{0:T(512)} %param.13) | copy-start | bytes 6148
  73.3 62.4 %copy-start.3 = (f32[512]{0:T(512)S(1)}, f32[512]{0:T(512)}, u32[]{:S(2)}) copy-start(f32[512]{0:T(512)} %param.16) | copy-start | bytes 6148
  73.3 62.5 %copy-start.4 = (f32[512]{0:T(512)S(1)}, f32[512]{0:T(512)}, u32[]{:S(2)}) copy-start(f32[512]{0:T(512)} %param.17) | copy-start | bytes 6148
  73.3 62.7 %copy-start.5 = (f32[512]{0:T(512)S(1)}, f32[512]{0:T(512)}, u32[]{:S(2)}) copy-start(f32[512]{0:T(512)} %param.15) | copy-start | bytes 6148
  73.3 62.8 %copy-start.6 = (f32[512]{0:T(512)S(1)}, f32[512]{0:T(512)}, u32[]{:S(2)}) copy-start(f32[512]{0:T(512)} %param.19) | copy-start | bytes 6148
  73.3 63.5 %copy-start.7 = (f32[512]{0:T(512)S(1)}, f32[512]{0:T(512)}, u32[]{:S(2)}) copy-start(f32[512]{0:T(512)} %param.21) | copy-start | bytes 6148
  80.7 44.6 %all-to-all-start = ((bf16[8,2,64,128]{3,2,1,0:T(8,128)(2,1)}), bf16[8,2,64,128]{3,2,1,0:T(8,128)(2,1)S(1)}, u32[]{:S(2)}, u32[]{:S(2)}) async-start(bf16[8,2,64,128]{3,2,1,0:T(8,128)(2,1)} %bitcast.4), calls=%async_computation | async-start | bytes 524288 | tf_op jit(solution)/shard_map/all_to_all | solution.py:274
  127.1 16.3 %all-to-all-start.3 = ((bf16[4,128,256]{2,1,0:T(8,128)(2,1)}), bf16[4,128,256]{2,1,0:T(8,128)(2,1)S(1)}, u32[]{:S(2)}, u32[]{:S(2)}) async-start(bf16[4,128,256]{2,1,0:T(8,128)(2,1)} %conv_one.1), calls=%async_computation.3 | async-start | bytes 524288 | tf_op jit(solution)/shard_map/all_to_all | solution.py:309
  136.9 7.1 %collective-permute-start.1 = (bf16[64,512]{1,0:T(8,128)(2,1)S(1)}, bf16[64,512]{1,0:T(8,128)(2,1)S(1)}, u32[]{:S(2)}, u32[]{:S(2)}) collective-permute-start(bf16[64,512]{1,0:T(8,128)(2,1)S(1)} %bitcast.66), channel_id=1, source_target_pairs={{0,2},{2,4},{4,6},{6,8},{8,10},{10,12},{12,14},{14,16},{16,18},{18... | collective-permute-start | bytes 196616 | tf_op jit(solution)/shard_map/ppermute | solution.py:28
  141.1 6.7 %collective-permute-start.2 = (bf16[64,512]{1,0:T(8,128)(2,1)S(1)}, bf16[64,512]{1,0:T(8,128)(2,1)S(1)}, u32[]{:S(2)}, u32[]{:S(2)}) collective-permute-start(bf16[64,512]{1,0:T(8,128)(2,1)S(1)} %bitcast.67), channel_id=1, source_target_pairs={{2,0},{4,2},{6,4},{8,6},{10,8},{12,10},{14,12},{16,14},{18,16},{20... | collective-permute-start | bytes 196616 | tf_op jit(solution)/shard_map/ppermute | solution.py:28
  148.4 17.0 %all-to-all-start.4 = ((f32[32,1,128]{2,1,0:T(1,128)}), f32[32,1,128]{2,1,0:T(1,128)S(1)}, u32[]{:S(2)}, u32[]{:S(2)}) async-start(f32[32,1,128]{2,1,0:T(1,128)} %broadcast_in_dim.58), calls=%async_computation.4 | async-start | bytes 32768 | tf_op jit(solution)/shard_map/all_to_all | solution.py:22
  165.5 20.4 %collective-permute-start.3 = (bf16[2,128,256]{2,1,0:T(8,128)(2,1)S(1)}, bf16[2,128,256]{2,1,0:T(8,128)(2,1)S(1)}, u32[]{:S(2)}, u32[]{:S(2)}) collective-permute-start(bf16[2,128,256]{2,1,0:T(8,128)(2,1)S(1)} %bitcast.52), channel_id=1, source_target_pairs={{0,2},{2,4},{4,6},{6,8},{8,10},{10,12},{12,14},{14,16},{16,18},{18... | collective-permute-start | bytes 393224 | tf_op jit(solution)/shard_map/ppermute | solution.py:331
  166.8 19.1 %collective-permute-start.4 = (bf16[2,128,256]{2,1,0:T(8,128)(2,1)S(1)}, bf16[2,128,256]{2,1,0:T(8,128)(2,1)S(1)}, u32[]{:S(2)}, u32[]{:S(2)}) collective-permute-start(bf16[2,128,256]{2,1,0:T(8,128)(2,1)S(1)} %bitcast.53), channel_id=1, source_target_pairs={{0,4},{2,6},{4,8},{6,10},{8,12},{10,14},{12,16},{14,18},{16,20},{1... | collective-permute-start | bytes 393224 | tf_op jit(solution)/shard_map/ppermute | solution.py:331
  169.5 37.3 %all-to-all-start.5 = ((f32[8,1,128]{2,1,0:T(1,128)}), f32[8,1,128]{2,1,0:T(1,128)S(1)}, u32[]{:S(2)}, u32[]{:S(2)}) async-start(f32[8,1,128]{2,1,0:T(1,128)} %broadcast_in_dim.60), calls=%async_computation.5 | async-start | bytes 8192 | tf_op jit(solution)/shard_map/all_to_all | solution.py:22
  215.8 3.3 %collective-permute-start.5 = (bf16[2,128,256]{2,1,0:T(8,128)(2,1)S(1)}, bf16[2,128,256]{2,1,0:T(8,128)(2,1)S(1)}, u32[]{:S(2)}, u32[]{:S(2)}) collective-permute-start(bf16[2,128,256]{2,1,0:T(8,128)(2,1)S(1)} %get-tuple-element.28), channel_id=1, source_target_pairs={{0,1},{1,0},{2,3},{3,2},{4,5},{5,4},{6,7},{7,6},{8,9},{9,8},{10,11... | collective-permute-start | bytes 393224 | tf_op jit(solution)/shard_map/ppermute | solution.py:369
Sparse Core Ops, SparseCore 0:
  20.7 166.0 all-gather.5

commit v8 on v7

--- a/solution.py
+++ b/solution.py
@@ -35,6 +35,22 @@
 
 def silu(u):
     return u / (1.0 + jnp.exp(-u))
+
+
+def prep_kernel(nx, k_own, core_ref, one_ref, two_ref, up_ref, out_ref):
+    taps, _, channels = one_ref.shape
+    half = out_ref.shape[3]
+    place = lax.broadcasted_iota(jnp.int32, (channels, half), 1) + core_ref[0] * half
+    natural = lax.broadcasted_iota(jnp.int32, (channels, half), 0)
+    line, x, k = place // (k_own * nx), place // k_own % nx, place % k_own
+    move = (natural == (x * (channels // (nx * k_own)) + line) * k_own + k).astype(BF16)
+    rows = [ref[t].astype(F32) for ref in (one_ref, two_ref) for t in range(taps)]
+    moved = jnp.dot(jnp.concatenate(rows).astype(BF16), move, preferred_element_type=F32)
+    lanes = pl.ds(pl.multiple_of(core_ref[0] * half, half), half)
+    for d in range(nx):
+        for t in range(2 * taps):
+            out_ref[d, t] = moved[t * k_own : (t + 1) * k_own].astype(BF16)
+        out_ref[d, 2 * taps :] = up_ref[:, :, lanes]
 
 
 def spread_stats(totals, pick, count, gain, shift):
@@ -147,17 +163,16 @@
         out_ref[at, :] = jnp.where(inside, y, 0.0).astype(BF16)
 
 
-def conv_up_kernel(cols, at_ref, x_ref, bias_ref, w_ref, mine_ref, theirs_ref, full, held, arrived):
-    copies = fetch_weights(w_ref, 9, held, arrived)
+def conv_up_kernel(cols, at_ref, x_ref, bias_ref, w_ref, mine_ref, theirs_ref, full):
+    lines = w_ref.shape[0] // 2
     outs = mine_ref.shape[2]
     totals = [jnp.zeros((2 * cols, outs), F32) for _ in range(3)]
     for h in range(2):
-        copies[h].wait()
         for r in range(3):
             starts = [(r + 1 + p) // 2 * cols for p in range(2)]
             x = jnp.concatenate([x_ref[h, start : start + cols, :] for start in starts])
             for k in range(3):
-                piece = held[h, :, 3 * r + k].reshape(-1, outs)
+                piece = w_ref[h * lines : (h + 1) * lines, 9 + 3 * r + k].reshape(-1, outs)
                 totals[k] += jnp.dot(x, piece, preferred_element_type=F32)
     middle = totals[1] + bias_ref[...]
     even = moved_right(totals[0], cols) + middle + totals[2]
@@ -238,14 +253,16 @@
     def own_half(v):
         return lax.dynamic_slice_in_dim(v, c * half, half, v.ndim - 1)
 
-    taps = 9 * k_own
-    hold = moved(
-        jnp.concatenate([first_weight.reshape(taps, channels), second_weight.reshape(taps, channels)]),
-        move,
-    )
-    hold = jnp.concatenate([hold, upsample_weight.reshape(taps, channels)])
-    hold = own_half(hold).reshape(1, 27, k_own, half)
-    hold = lax.all_to_all(jnp.broadcast_to(hold, (nx, 27, k_own, half)), "x", 0, 0, tiled=True)
+    core = c.astype(jnp.int32)[None]
+    hold = pl.pallas_call(
+        functools.partial(prep_kernel, nx, k_own),
+        out_shape=jax.ShapeDtypeStruct((nx, 27, k_own, half), BF16),
+        in_specs=[SM, VM, VM, VM],
+        out_specs=VM,
+        compiler_params=grant(60),
+        name="prep",
+    )(core, *[w.reshape(9, k_own, channels) for w in (first_weight, second_weight, upsample_weight)])
+    hold = lax.all_to_all(hold, "x", 0, 0, tiled=True)
     hold = hold.transpose(1, 0, 2, 3).reshape(27, nx * k_own, half)
     weights = lax.all_gather(hold[9:], ("zh", "zl"))
     hold_one = hold[:9]
@@ -355,15 +372,14 @@
     )(at, normed, residual, bias_two, weights)
     block = lax.all_gather(block, "col")
 
-    core = c.astype(jnp.int32)[None]
     side = jax.ShapeDtypeStruct((2, cols, half), BF16)
     mine, theirs = pl.pallas_call(
         functools.partial(conv_up_kernel, cols),
         out_shape=(side, side),
-        in_specs=[SM, VM, VM, HB],
+        in_specs=[SM, VM, VM, VM],
         out_specs=(VM, VM),
-        scratch_shapes=[pltpu.VMEM((2, 2, 2 * cols, 128), F32)] + held,
-        compiler_params=grant(50),
+        scratch_shapes=[pltpu.VMEM((2, 2, 2 * cols, 128), F32)],
+        compiler_params=grant(16),
         name="conv_up",
     )(core, block, bias_up, weights)
     theirs = lax.ppermute(theirs, "col", [(0, 1), (1, 0)])

time: 227 us -> 229 us (level)
  blocking collectives: 59.4 us -> 65.7 us
  starting transfers between devices: 100 us -> 96.2 us
  local copies, waits for them, and re-layouts: 8.18 us -> 5.78 us
    all_to_all x3, starting transfers between devices: 76.8 us -> 69.8 us  [sum_over(): return lax.all_to_all(sent, axes, 0, 0, tiled=True)]
    all_gather x1, blocking collectives: 39.6 us -> 45.6 us  [on_device(): weights_one = lax.all_gather(jnp.concatenate([hold_one, terms[None]]), 'zh')]
    all_to_all x1, starting transfers between devices: 3.95 us -> 7.84 us  [on_device(): quad = lax.all_to_all(sent, ('zl', 'col'), 0, 0, tiled=True)]
    reshape x3 -> x0, local copies, waits for them, and re-layouts: 2.36 us -> none  [the longest x1 0.79 us: on_device(): first_weight.reshape(taps, channels)]
  transfers between devices with their start and end apart: 12 -> 12, of which waited for: 7 -> 6; matrix products, arithmetic and copies ran while one was open for 3% -> 4% of each run, Pallas kernels for 1% -> 1%
where the time goes in v8:
time: 229 us; the launch traced here: 227 us
  starting transfers between devices  96.2 us (42%)
  blocking collectives  65.7 us (29%)
  waiting for transfers between devices  32.3 us (14%)
  between operations  14 us (6%)
  Pallas kernels  9.28 us (4%)
  local copies, waits for them, and re-layouts  5.78 us (3%)
    all_to_all x3, starting transfers between devices, sum_over(): return lax.all_to_all(sent, axes, 0, 0, tiled=True)  69.8 us
    all_gather x1, blocking collectives, on_device(): weights_one = lax.all_gather(jnp.concatenate([hold_one, terms[None]]), 'zh')  45.6 us
    all_to_all x3, waiting for transfers between devices, sum_over(): return lax.all_to_all(sent, axes, 0, 0, tiled=True)  26.2 us
    all_to_all x1, blocking collectives, on_device(): hold = lax.all_to_all(hold, 'x', 0, 0, tiled=True)  10.4 us
    all_to_all x1, starting transfers between devices, on_device(): quad = lax.all_to_all(sent, ('zl', 'col'), 0, 0, tiled=True)  7.84 us
    all_to_all x1, starting transfers between devices, on_device(): parts = lax.all_to_all(parts, 'zl', 0, 0, tiled=True)  7.52 us
    ppermute x2, starting transfers between devices, shifted_rows(): return lax.ppermute(values, axis, pairs)  5.43 us
  transfers between devices with their start and end apart: 12, of which 6 were waited for; matrix products, arithmetic and copies ran while one was open for 4% of the time, Pallas kernels for 1%

profile of v8, /device:TPU:33, one launch (start us, length us, event | category | flops | bytes accessed | tf_op | source)
XLA Modules:
  0.0 227.2 jit_solution(232734529063017935)
XLA Ops:
  6.6 1.7 prep.1
  8.3 10.4 %all_to_all.35 = bf16[4,27,4,256]{3,2,1,0:T(4,128)(2,1)S(1)} all-to-all(bf16[4,27,4,256]{3,2,1,0:T(4,128)(2,1)} %prep.1), channel_id=1, replica_groups=mesh['img'=2,'x'=4,'zh'=8,'zl'=4,'col'=2] {'x'}, dimensions={0} | all-to-all | bytes 442368 | tf_op jit(solution)/shard_map/all_to_all | solution.py:265
  21.6 44.6 %all-to-all-start.2 = ((f32[32,1,128]{2,1,0:T(1,128)}), f32[32,1,128]{2,1,0:T(1,128)S(1)}, u32[]{:S(2)}, u32[]{:S(2)}) async-start(f32[32,1,128]{2,1,0:T(1,128)} %broadcast_in_dim.21), calls=%async_computation.2 | async-start | bytes 32768 | tf_op jit(solution)/shard_map/all_to_all | solution.py:22
  66.9 1.2 convolution_convert_fusion
  68.3 5.4 %all-to-all-done.2 = f32[32,1,128]{2,1,0:T(1,128)S(1)} async-done(((f32[32,1,128]{2,1,0:T(1,128)}), f32[32,1,128]{2,1,0:T(1,128)S(1)}, u32[]{:S(2)}, u32[]{:S(2)}) %all-to-all-start.2) | async-done | bytes 16416 | tf_op jit(solution)/shard_map/all_to_all | solution.py:22
  74.4 7.8 %all-to-all-start = ((bf16[8,2,64,128]{3,2,1,0:T(8,128)(2,1)}), bf16[8,2,64,128]{3,2,1,0:T(8,128)(2,1)S(1)}, u32[]{:S(2)}, u32[]{:S(2)}) async-start(bf16[8,2,64,128]{3,2,1,0:T(8,128)(2,1)} %bitcast.4), calls=%async_computation | async-start | bytes 524288 | tf_op jit(solution)/shard_map/all_to_all | solution.py:291
  83.4 45.6 %all-gather = bf16[80,16,256]{2,1,0:T(8,128)(2,1)S(1)} all-gather(bf16[10,16,256]{2,1,0:T(8,128)(2,1)S(1)} %pad_maximum_fusion.2), channel_id=2, replica_groups=mesh['img'=2,'x'=4,'zh'=8,'zl'=4,'col'=2] {'zh'}, dimensions={0}, use_global_device_ids=true | all-gather | bytes 737280 | tf_op jit(solution)/shard_map/all_gather | solution.py:282
  128.9 1.8 conv_one.1
  130.7 7.5 %all-to-all-start.3 = ((bf16[4,128,256]{2,1,0:T(8,128)(2,1)}), bf16[4,128,256]{2,1,0:T(8,128)(2,1)S(1)}, u32[]{:S(2)}, u32[]{:S(2)}) async-start(bf16[4,128,256]{2,1,0:T(8,128)(2,1)} %conv_one.1), calls=%async_computation.3 | async-start | bytes 524288 | tf_op jit(solution)/shard_map/all_to_all | solution.py:326
  139.5 4.1 %collective-permute-start.1 = (bf16[64,512]{1,0:T(8,128)(2,1)S(1)}, bf16[64,512]{1,0:T(8,128)(2,1)S(1)}, u32[]{:S(2)}, u32[]{:S(2)}) collective-permute-start(bf16[64,512]{1,0:T(8,128)(2,1)S(1)} %bitcast.69), channel_id=1, source_target_pairs={{0,2},{2,4},{4,6},{6,8},{8,10},{10,12},{12,14},{14,16},{16,18},{18... | collective-permute-start | bytes 196616 | tf_op jit(solution)/shard_map/ppermute | solution.py:28
  143.6 1.3 collective-permute-start.2
  146.1 4.4 %collective-permute-done.2 = bf16[64,512]{1,0:T(8,128)(2,1)S(1)} collective-permute-done((bf16[64,512]{1,0:T(8,128)(2,1)S(1)}, bf16[64,512]{1,0:T(8,128)(2,1)S(1)}, u32[]{:S(2)}, u32[]{:S(2)}) %collective-permute-start.2) | collective-permute-done | bytes 65568 | tf_op jit(solution)/shard_map/ppermute | solution.py:28
  151.1 11.1 %all-to-all-start.4 = ((f32[32,1,128]{2,1,0:T(1,128)}), f32[32,1,128]{2,1,0:T(1,128)S(1)}, u32[]{:S(2)}, u32[]{:S(2)}) async-start(f32[32,1,128]{2,1,0:T(1,128)} %broadcast_in_dim.24), calls=%async_computation.4 | async-start | bytes 32768 | tf_op jit(solution)/shard_map/all_to_all | solution.py:22
  162.2 2.5 %all_gather.37 = bf16[3,128,512]{2,1,0:T(8,128)(2,1)S(1)} all-gather(bf16[3,64,512]{2,1,0:T(8,128)(2,1)S(1)} %pad_maximum_fusion.1), channel_id=1, replica_groups=mesh['img'=2,'x'=4,'zh'=8,'zl'=4,'col'=2] {'col'}, dimensions={1}, use_global_device_ids=true | all-gather | bytes 589824 | tf_op jit(solution)/shard_map/all_gather | solution.py:344
  165.1 2.0 all-gather.1
  167.1 2.2 all-to-all-done.4
  169.3 1.3 collective-permute-start.3
  170.6 1.3 collective-permute-start.4
  173.3 14.2 %all-to-all-start.5 = ((f32[8,1,128]{2,1,0:T(1,128)}), f32[8,1,128]{2,1,0:T(1,128)S(1)}, u32[]{:S(2)}, u32[]{:S(2)}) async-start(f32[8,1,128]{2,1,0:T(1,128)} %broadcast_in_dim.51), calls=%async_computation.5 | async-start | bytes 8192 | tf_op jit(solution)/shard_map/all_to_all | solution.py:22
  187.6 2.2 all-gather.2
  189.8 18.6 %all-to-all-done.5 = f32[8,1,128]{2,1,0:T(1,128)S(1)} async-done(((f32[8,1,128]{2,1,0:T(1,128)}), f32[8,1,128]{2,1,0:T(1,128)S(1)}, u32[]{:S(2)}, u32[]{:S(2)}) %all-to-all-start.5) | async-done | bytes 4128 | tf_op jit(solution)/shard_map/all_to_all | solution.py:22
  209.5 2.9 %conv_two.1 = bf16[384,256]{1,0:T(8,128)(2,1)S(1)} custom-call(s32[1]{0:T(128)} %bitcast.1.at_ref, bf16[2,640,256]{2,1,0:T(8,128)(2,1)S(1)} %norm_two.1.x_ref, bf16[384,256]{1,0:T(8,128)(2,1)S(1)} %dynamic-slice_convert_fusion.res_ref, f32[1,256]{1,0:T(1,128)S(1)} %get-tuple-element.34.bias_ref, bf16[32,18,16,256]{3,2,1,0:T(8,128)(2,1)} %all-gather.6.cloned.1.call-done.w_ref), custom_call_target="tpu_custom_call" | custom-call | tf_op jit(solution)/shard_map/conv_two/pallas_call | solution.py:364
  212.4 3.1 %all-gather.3 = bf16[768,256]{1,0:T(8,128)(2,1)S(1)} all-gather(bf16[384,256]{1,0:T(8,128)(2,1)S(1)} %conv_two.1), channel_id=5, replica_groups=mesh['img'=2,'x'=4,'zh'=8,'zl'=4,'col'=2] {'col'}, dimensions={0}, use_global_device_ids=true | all-gather | bytes 589824 | tf_op jit(solution)/shard_map/all_gather | solution.py:373
  216.3 2.3 %collective-permute-start.5 = (bf16[2,128,256]{2,1,0:T(8,128)(2,1)S(1)}, bf16[2,128,256]{2,1,0:T(8,128)(2,1)S(1)}, u32[]{:S(2)}, u32[]{:S(2)}) collective-permute-start(bf16[2,128,256]{2,1,0:T(8,128)(2,1)S(1)} %get-tuple-element.28), channel_id=1, source_target_pairs={{0,1},{1,0},{2,3},{3,2},{4,5},{5,4},{6,7},{7,6},{8,9},{9,8},{10,11... | collective-permute-start | bytes 393224 | tf_op jit(solution)/shard_map/ppermute | solution.py:385
  (98 shorter events, 13.8 us)
Async XLA Ops:
  6.5 203.0 %all-gather.6.cloned.1.call-start = ((), (), s32[]{:S(2)}) async-start(), calls=%async_computation.6 | async-start | bytes 4866048 | tf_op jit(solution)/shard_map/all_gather | solution.py:267
  21.6 52.0 %all-to-all-start.2 = ((f32[32,1,128]{2,1,0:T(1,128)}), f32[32,1,128]{2,1,0:T(1,128)S(1)}, u32[]{:S(2)}, u32[]{:S(2)}) async-start(f32[32,1,128]{2,1,0:T(1,128)} %broadcast_in_dim.21), calls=%async_computation.2 | async-start | bytes 32768 | tf_op jit(solution)/shard_map/all_to_all | solution.py:22
  66.2 0.7 collective-permute-start
  66.9 15.3 %copy-start.2 = (f32[512]{0:T(512)S(1)}, f32[512]{0:T(512)}, u32[]{:S(2)}) copy-start(f32[512]{0:T(512)} %param.12) | copy-start | bytes 6148
  66.9 15.6 %copy-start.3 = (f32[512]{0:T(512)S(1)}, f32[512]{0:T(512)}, u32[]{:S(2)}) copy-start(f32[512]{0:T(512)} %param.13) | copy-start | bytes 6148
  68.1 70.0 %copy-start.4 = (f32[512]{0:T(512)S(1)}, f32[512]{0:T(512)}, u32[]{:S(2)}) copy-start(f32[512]{0:T(512)} %param.16) | copy-start | bytes 6148
  68.2 70.2 %copy-start.5 = (f32[512]{0:T(512)S(1)}, f32[512]{0:T(512)}, u32[]{:S(2)}) copy-start(f32[512]{0:T(512)} %param.17) | copy-start | bytes 6148
  68.2 70.3 %copy-start.6 = (f32[512]{0:T(512)S(1)}, f32[512]{0:T(512)}, u32[]{:S(2)}) copy-start(f32[512]{0:T(512)} %param.15) | copy-start | bytes 6148
  68.2 70.4 %copy-start.7 = (f32[512]{0:T(512)S(1)}, f32[512]{0:T(512)}, u32[]{:S(2)}) copy-start(f32[512]{0:T(512)} %param.19) | copy-start | bytes 6148
  68.2 71.2 %copy-start.8 = (f32[512]{0:T(512)S(1)}, f32[512]{0:T(512)}, u32[]{:S(2)}) copy-start(f32[512]{0:T(512)} %param.21) | copy-start | bytes 6148
  68.2 71.3 %copy-start.1 = (bf16[1,64,512]{2,1,0:T(8,128)(2,1)S(1)}, bf16[1,64,512]{2,1,0:T(8,128)(2,1)}, u32[]{:S(2)}) copy-start(bf16[1,64,512]{2,1,0:T(8,128)(2,1)} %param.11) | copy-start | bytes 196612
  74.4 54.5 %all-to-all-start = ((bf16[8,2,64,128]{3,2,1,0:T(8,128)(2,1)}), bf16[8,2,64,128]{3,2,1,0:T(8,128)(2,1)S(1)}, u32[]{:S(2)}, u32[]{:S(2)}) async-start(bf16[8,2,64,128]{3,2,1,0:T(8,128)(2,1)} %bitcast.4), calls=%async_computation | async-start | bytes 524288 | tf_op jit(solution)/shard_map/all_to_all | solution.py:291
  130.7 15.1 %all-to-all-start.3 = ((bf16[4,128,256]{2,1,0:T(8,128)(2,1)}), bf16[4,128,256]{2,1,0:T(8,128)(2,1)S(1)}, u32[]{:S(2)}, u32[]{:S(2)}) async-start(bf16[4,128,256]{2,1,0:T(8,128)(2,1)} %conv_one.1), calls=%async_computation.3 | async-start | bytes 524288 | tf_op jit(solution)/shard_map/all_to_all | solution.py:326
  139.5 6.6 %collective-permute-start.1 = (bf16[64,512]{1,0:T(8,128)(2,1)S(1)}, bf16[64,512]{1,0:T(8,128)(2,1)S(1)}, u32[]{:S(2)}, u32[]{:S(2)}) collective-permute-start(bf16[64,512]{1,0:T(8,128)(2,1)S(1)} %bitcast.69), channel_id=1, source_target_pairs={{0,2},{2,4},{4,6},{6,8},{8,10},{10,12},{12,14},{14,16},{16,18},{18... | collective-permute-start | bytes 196616 | tf_op jit(solution)/shard_map/ppermute | solution.py:28
  143.6 6.8 %collective-permute-start.2 = (bf16[64,512]{1,0:T(8,128)(2,1)S(1)}, bf16[64,512]{1,0:T(8,128)(2,1)S(1)}, u32[]{:S(2)}, u32[]{:S(2)}) collective-permute-start(bf16[64,512]{1,0:T(8,128)(2,1)S(1)} %bitcast.70), channel_id=1, source_target_pairs={{2,0},{4,2},{6,4},{8,6},{10,8},{12,10},{14,12},{16,14},{18,16},{20... | collective-permute-start | bytes 196616 | tf_op jit(solution)/shard_map/ppermute | solution.py:28
  151.1 18.2 %all-to-all-start.4 = ((f32[32,1,128]{2,1,0:T(1,128)}), f32[32,1,128]{2,1,0:T(1,128)S(1)}, u32[]{:S(2)}, u32[]{:S(2)}) async-start(f32[32,1,128]{2,1,0:T(1,128)} %broadcast_in_dim.24), calls=%async_computation.4 | async-start | bytes 32768 | tf_op jit(solution)/shard_map/all_to_all | solution.py:22
  169.3 18.2 %collective-permute-start.3 = (bf16[2,128,256]{2,1,0:T(8,128)(2,1)S(1)}, bf16[2,128,256]{2,1,0:T(8,128)(2,1)S(1)}, u32[]{:S(2)}, u32[]{:S(2)}) collective-permute-start(bf16[2,128,256]{2,1,0:T(8,128)(2,1)S(1)} %bitcast.55), channel_id=1, source_target_pairs={{0,2},{2,4},{4,6},{6,8},{8,10},{10,12},{12,14},{14,16},{16,18},{18... | collective-permute-start | bytes 393224 | tf_op jit(solution)/shard_map/ppermute | solution.py:348
  170.6 16.9 %collective-permute-start.4 = (bf16[2,128,256]{2,1,0:T(8,128)(2,1)S(1)}, bf16[2,128,256]{2,1,0:T(8,128)(2,1)S(1)}, u32[]{:S(2)}, u32[]{:S(2)}) collective-permute-start(bf16[2,128,256]{2,1,0:T(8,128)(2,1)S(1)} %bitcast.56), channel_id=1, source_target_pairs={{0,4},{2,6},{4,8},{6,10},{8,12},{10,14},{12,16},{14,18},{16,20},{1... | collective-permute-start | bytes 393224 | tf_op jit(solution)/shard_map/ppermute | solution.py:348
  173.3 35.1 %all-to-all-start.5 = ((f32[8,1,128]{2,1,0:T(1,128)}), f32[8,1,128]{2,1,0:T(1,128)S(1)}, u32[]{:S(2)}, u32[]{:S(2)}) async-start(f32[8,1,128]{2,1,0:T(1,128)} %broadcast_in_dim.51), calls=%async_computation.5 | async-start | bytes 8192 | tf_op jit(solution)/shard_map/all_to_all | solution.py:22
  209.5 6.0 %copy-start = (bf16[32,18,16,256]{3,2,1,0:T(8,128)(2,1)S(1)}, bf16[32,18,16,256]{3,2,1,0:T(8,128)(2,1)}, u32[]{:S(2)}) copy-start(bf16[32,18,16,256]{3,2,1,0:T(8,128)(2,1)} %all-gather.6.cloned.1.call-done.w_ref) | copy-start | bytes 14155780
  216.3 3.3 %collective-permute-start.5 = (bf16[2,128,256]{2,1,0:T(8,128)(2,1)S(1)}, bf16[2,128,256]{2,1,0:T(8,128)(2,1)S(1)}, u32[]{:S(2)}, u32[]{:S(2)}) collective-permute-start(bf16[2,128,256]{2,1,0:T(8,128)(2,1)S(1)} %get-tuple-element.28), channel_id=1, source_target_pairs={{0,1},{1,0},{2,3},{3,2},{4,5},{5,4},{6,7},{7,6},{8,9},{9,8},{10,11... | collective-permute-start | bytes 393224 | tf_op jit(solution)/shard_map/ppermute | solution.py:385
Sparse Core Ops, SparseCore 0:
  19.7 167.2 all-gather.5

commit v9 on v7

--- a/solution.py
+++ b/solution.py
@@ -104,16 +104,20 @@
             out_ref[h, (d + 2) * cols : (d + 3) * cols, :] = jnp.where(inside, y, 0.0).astype(BF16)
 
 
-def fetch_weights(w_ref, base, held, arrived):
-    lines = held.shape[1]
+def fetch_weights(w_ref, held, arrived):
+    lines = held.shape[2]
     copies = [
-        pltpu.make_async_copy(
-            w_ref.at[pl.ds(h * lines, lines), pl.ds(base, 9)], held.at[h], arrived.at[h]
-        )
+        [
+            pltpu.make_async_copy(
+                w_ref.at[pl.ds(h * lines, lines), pl.ds(3 * r, 3)], held.at[h, r], arrived.at[h, r]
+            )
+            for r in range(3)
+        ]
         for h in range(2)
     ]
-    for copy in copies:
-        copy.start()
+    for half in copies:
+        for copy in half:
+            copy.start()
     return copies
 
 
@@ -128,15 +132,15 @@
 
 
 def conv_two_kernel(cols, rows, image_rows, at_ref, x_ref, res_ref, bias_ref, w_ref, out_ref, held, arrived):
-    copies = fetch_weights(w_ref, 0, held, arrived)
+    copies = fetch_weights(w_ref, held, arrived)
     outs = out_ref.shape[1]
     totals = [jnp.zeros(out_ref.shape, F32) for _ in range(3)]
     for h in range(2):
-        copies[h].wait()
         for r in range(3):
+            copies[h][r].wait()
             x = x_ref[h, r * cols : (r + rows) * cols, :]
             for k in range(3):
-                piece = held[h, :, 3 * r + k].reshape(-1, outs)
+                piece = held[h, r, :, k].reshape(-1, outs)
                 totals[k] += jnp.dot(x, piece, preferred_element_type=F32)
     total = totals[1] + moved_right(totals[0], cols) + moved_left(totals[2], cols) + bias_ref[...]
     first = at_ref[0] - rows // 2
@@ -147,17 +151,16 @@
         out_ref[at, :] = jnp.where(inside, y, 0.0).astype(BF16)
 
 
-def conv_up_kernel(cols, at_ref, x_ref, bias_ref, w_ref, mine_ref, theirs_ref, full, held, arrived):
-    copies = fetch_weights(w_ref, 9, held, arrived)
+def conv_up_kernel(cols, at_ref, x_ref, bias_ref, w_ref, mine_ref, theirs_ref, full):
+    lines = w_ref.shape[0] // 2
     outs = mine_ref.shape[2]
     totals = [jnp.zeros((2 * cols, outs), F32) for _ in range(3)]
     for h in range(2):
-        copies[h].wait()
         for r in range(3):
             starts = [(r + 1 + p) // 2 * cols for p in range(2)]
             x = jnp.concatenate([x_ref[h, start : start + cols, :] for start in starts])
             for k in range(3):
-                piece = held[h, :, 3 * r + k].reshape(-1, outs)
+                piece = w_ref[h * lines : (h + 1) * lines, 9 + 3 * r + k].reshape(-1, outs)
                 totals[k] += jnp.dot(x, piece, preferred_element_type=F32)
     middle = totals[1] + bias_ref[...]
     even = moved_right(totals[0], cols) + middle + totals[2]
@@ -341,8 +344,8 @@
 
     rows = 3
     held = [
-        pltpu.VMEM((2, nz // 2, 9) + weights.shape[2:], BF16),
-        pltpu.SemaphoreType.DMA((2,)),
+        pltpu.VMEM((2, 3, nz // 2, 3) + weights.shape[2:], BF16),
+        pltpu.SemaphoreType.DMA((2, 3)),
     ]
     block = pl.pallas_call(
         functools.partial(conv_two_kernel, cols, rows, image_rows),
@@ -360,10 +363,10 @@
     mine, theirs = pl.pallas_call(
         functools.partial(conv_up_kernel, cols),
         out_shape=(side, side),
-        in_specs=[SM, VM, VM, HB],
+        in_specs=[SM, VM, VM, VM],
         out_specs=(VM, VM),
-        scratch_shapes=[pltpu.VMEM((2, 2, 2 * cols, 128), F32)] + held,
-        compiler_params=grant(50),
+        scratch_shapes=[pltpu.VMEM((2, 2, 2 * cols, 128), F32)],
+        compiler_params=grant(16),
         name="conv_up",
     )(core, block, bias_up, weights)
     theirs = lax.ppermute(theirs, "col", [(0, 1), (1, 0)])

time: 227 us -> 226 us (level)
  no operation moved by 1% of the time
where the time goes in v9:
time: 226 us
  starting transfers between devices  100 us (44%)
  blocking collectives  59.5 us (26%)
  waiting for transfers between devices  33.3 us (15%)
  between operations  14 us (6%)
  local copies, waits for them, and re-layouts  8.2 us (4%)
  Pallas kernels  7.75 us (3%)
    all_to_all x3, starting transfers between devices, sum_over(): return lax.all_to_all(sent, axes, 0, 0, tiled=True)  76.7 us
    all_gather x1, blocking collectives, on_device(): weights_one = lax.all_gather(jnp.concatenate([hold_one, terms[None]]), 'zh')  39.6 us
    all_to_all x3, waiting for transfers between devices, sum_over(): return lax.all_to_all(sent, axes, 0, 0, tiled=True)  27.2 us
    all_to_all x1, blocking collectives, on_device(): lax.all_to_all(jnp.broadcast_to(hold, (nx, 27, k_own, half)), 'x', 0, 0,...  10.2 us
    all_to_all x1, starting transfers between devices, on_device(): parts = lax.all_to_all(parts, 'zl', 0, 0, tiled=True)  8.52 us
    ppermute x2, starting transfers between devices, shifted_rows(): return lax.ppermute(values, axis, pairs)  5.44 us
  transfers between devices with their start and end apart: 12, of which 7 were waited for; matrix products, arithmetic and copies ran while one was open for 3% of the time, Pallas kernels for 1%

profile of v9, /device:TPU:33, one launch (start us, length us, event | category | flops | bytes accessed | tf_op | source)
XLA Modules:
  0.0 225.5 jit_solution(1094404695329920524)
XLA Ops:
  9.4 10.2 %all_to_all.35 = bf16[4,27,4,256]{3,2,1,0:T(4,128)(2,1)S(1)} all-to-all(bf16[4,27,4,256]{3,2,1,0:T(4,128)(2,1)S(1)} %broadcast_in_dim.26), channel_id=1, replica_groups=mesh['img'=2,'x'=4,'zh'=8,'zl'=4,'col'=2] {'x'}, dimensions={0} | all-to-all | bytes 442368 | tf_op jit(solution)/shard_map/all_to_all | solution.py:251
  22.4 50.4 %all-to-all-start.2 = ((f32[32,1,128]{2,1,0:T(1,128)}), f32[32,1,128]{2,1,0:T(1,128)S(1)}, u32[]{:S(2)}, u32[]{:S(2)}) async-start(f32[32,1,128]{2,1,0:T(1,128)} %broadcast_in_dim.27), calls=%async_computation.2 | async-start | bytes 32768 | tf_op jit(solution)/shard_map/all_to_all | solution.py:22
  73.4 6.6 %all-to-all-done.2 = f32[32,1,128]{2,1,0:T(1,128)S(1)} async-done(((f32[32,1,128]{2,1,0:T(1,128)}), f32[32,1,128]{2,1,0:T(1,128)S(1)}, u32[]{:S(2)}, u32[]{:S(2)}) %all-to-all-start.2) | async-done | bytes 16416 | tf_op jit(solution)/shard_map/all_to_all | solution.py:22
  80.7 4.0 %all-to-all-start = ((bf16[8,2,64,128]{3,2,1,0:T(8,128)(2,1)}), bf16[8,2,64,128]{3,2,1,0:T(8,128)(2,1)S(1)}, u32[]{:S(2)}, u32[]{:S(2)}) async-start(bf16[8,2,64,128]{3,2,1,0:T(8,128)(2,1)} %bitcast.4), calls=%async_computation | async-start | bytes 524288 | tf_op jit(solution)/shard_map/all_to_all | solution.py:277
  85.8 39.6 %all-gather = bf16[80,16,256]{2,1,0:T(8,128)(2,1)S(1)} all-gather(bf16[10,16,256]{2,1,0:T(8,128)(2,1)S(1)} %pad_maximum_fusion.2), channel_id=2, replica_groups=mesh['img'=2,'x'=4,'zh'=8,'zl'=4,'col'=2] {'zh'}, dimensions={0}, use_global_device_ids=true | all-gather | bytes 737280 | tf_op jit(solution)/shard_map/all_gather | solution.py:268
  125.4 1.8 conv_one.1
  127.1 8.5 %all-to-all-start.3 = ((bf16[4,128,256]{2,1,0:T(8,128)(2,1)}), bf16[4,128,256]{2,1,0:T(8,128)(2,1)S(1)}, u32[]{:S(2)}, u32[]{:S(2)}) async-start(bf16[4,128,256]{2,1,0:T(8,128)(2,1)} %conv_one.1), calls=%async_computation.3 | async-start | bytes 524288 | tf_op jit(solution)/shard_map/all_to_all | solution.py:312
  137.0 4.1 %collective-permute-start.1 = (bf16[64,512]{1,0:T(8,128)(2,1)S(1)}, bf16[64,512]{1,0:T(8,128)(2,1)S(1)}, u32[]{:S(2)}, u32[]{:S(2)}) collective-permute-start(bf16[64,512]{1,0:T(8,128)(2,1)S(1)} %bitcast.66), channel_id=1, source_target_pairs={{0,2},{2,4},{4,6},{6,8},{8,10},{10,12},{12,14},{14,16},{16,18},{18... | collective-permute-start | bytes 196616 | tf_op jit(solution)/shard_map/ppermute | solution.py:28
  141.1 1.3 collective-permute-start.2
  142.5 1.0 all-to-all-done.3.x_ref
  144.1 3.8 %collective-permute-done.2 = bf16[64,512]{1,0:T(8,128)(2,1)S(1)} collective-permute-done((bf16[64,512]{1,0:T(8,128)(2,1)S(1)}, bf16[64,512]{1,0:T(8,128)(2,1)S(1)}, u32[]{:S(2)}, u32[]{:S(2)}) %collective-permute-start.2) | collective-permute-done | bytes 65568 | tf_op jit(solution)/shard_map/ppermute | solution.py:28
  148.4 9.9 %all-to-all-start.4 = ((f32[32,1,128]{2,1,0:T(1,128)}), f32[32,1,128]{2,1,0:T(1,128)S(1)}, u32[]{:S(2)}, u32[]{:S(2)}) async-start(f32[32,1,128]{2,1,0:T(1,128)} %broadcast_in_dim.58), calls=%async_computation.4 | async-start | bytes 32768 | tf_op jit(solution)/shard_map/all_to_all | solution.py:22
  158.4 2.5 %all_gather.37 = bf16[3,128,512]{2,1,0:T(8,128)(2,1)S(1)} all-gather(bf16[3,64,512]{2,1,0:T(8,128)(2,1)S(1)} %pad_maximum_fusion.1), channel_id=1, replica_groups=mesh['img'=2,'x'=4,'zh'=8,'zl'=4,'col'=2] {'col'}, dimensions={1}, use_global_device_ids=true | all-gather | bytes 589824 | tf_op jit(solution)/shard_map/all_gather | solution.py:330
  161.3 2.0 all-gather.1
  163.3 2.2 all-to-all-done.4
  165.5 1.3 collective-permute-start.3
  166.8 1.3 collective-permute-start.4
  169.5 16.4 %all-to-all-start.5 = ((f32[8,1,128]{2,1,0:T(1,128)}), f32[8,1,128]{2,1,0:T(1,128)S(1)}, u32[]{:S(2)}, u32[]{:S(2)}) async-start(f32[8,1,128]{2,1,0:T(1,128)} %broadcast_in_dim.60), calls=%async_computation.5 | async-start | bytes 8192 | tf_op jit(solution)/shard_map/all_to_all | solution.py:22
  185.9 2.4 %all-gather.2 = bf16[4,2,128,256]{3,2,1,0:T(8,128)(2,1)S(1)} all-gather(bf16[2,2,128,256]{3,2,1,0:T(8,128)(2,1)S(1)} %pad_maximum_fusion), channel_id=4, replica_groups=mesh['img'=2,'x'=4,'zh'=8,'zl'=4,'col'=2] {'col'}, dimensions={0}, use_global_device_ids=true | all-gather | bytes 786432 | tf_op jit(solution)/shard_map/all_gather | solution.py:335
  188.4 18.4 %all-to-all-done.5 = f32[8,1,128]{2,1,0:T(1,128)S(1)} async-done(((f32[8,1,128]{2,1,0:T(1,128)}), f32[8,1,128]{2,1,0:T(1,128)S(1)}, u32[]{:S(2)}, u32[]{:S(2)}) %all-to-all-start.5) | async-done | bytes 4128 | tf_op jit(solution)/shard_map/all_to_all | solution.py:22
  206.8 1.1 norm_two.1.x_ref
  207.9 3.1 %conv_two.1 = bf16[384,256]{1,0:T(8,128)(2,1)S(1)} custom-call(s32[1]{0:T(128)} %bitcast.1.at_ref, bf16[2,640,256]{2,1,0:T(8,128)(2,1)S(1)} %norm_two.1.x_ref, bf16[384,256]{1,0:T(8,128)(2,1)S(1)} %dynamic-slice_convert_fusion.res_ref, f32[1,256]{1,0:T(1,128)S(1)} %get-tuple-element.34.bias_ref, bf16[32,18,16,256]{3,2,1,0:T(8,128)(2,1)} %all-gather.6.cloned.1.call-done.w_ref), custom_call_target="tpu_custom_call" | custom-call | tf_op jit(solution)/shard_map/conv_two/pallas_call | solution.py:350
  211.0 2.8 %all-gather.3 = bf16[768,256]{1,0:T(8,128)(2,1)S(1)} all-gather(bf16[384,256]{1,0:T(8,128)(2,1)S(1)} %conv_two.1), channel_id=5, replica_groups=mesh['img'=2,'x'=4,'zh'=8,'zl'=4,'col'=2] {'col'}, dimensions={0}, use_global_device_ids=true | all-gather | bytes 589824 | tf_op jit(solution)/shard_map/all_gather | solution.py:359
  214.7 2.3 %collective-permute-start.5 = (bf16[2,128,256]{2,1,0:T(8,128)(2,1)S(1)}, bf16[2,128,256]{2,1,0:T(8,128)(2,1)S(1)}, u32[]{:S(2)}, u32[]{:S(2)}) collective-permute-start(bf16[2,128,256]{2,1,0:T(8,128)(2,1)S(1)} %get-tuple-element.28), channel_id=1, source_target_pairs={{0,1},{1,0},{2,3},{3,2},{4,5},{5,4},{6,7},{7,6},{8,9},{9,8},{10,11... | collective-permute-start | bytes 393224 | tf_op jit(solution)/shard_map/ppermute | solution.py:372
  (104 shorter events, 14.7 us)
Async XLA Ops:
  6.5 14.0 %copy-start.1 = (bf16[1,64,512]{2,1,0:T(8,128)(2,1)S(1)}, bf16[1,64,512]{2,1,0:T(8,128)(2,1)}, u32[]{:S(2)}) copy-start(bf16[1,64,512]{2,1,0:T(8,128)(2,1)} %param.11) | copy-start | bytes 196612
  6.5 201.3 %all-gather.6.cloned.1.call-start = ((), (), s32[]{:S(2)}) async-start(), calls=%async_computation.6 | async-start | bytes 4866048 | tf_op jit(solution)/shard_map/all_gather | solution.py:253
  20.6 52.3 %collective-permute-start = (bf16[64,512]{1,0:T(8,128)(2,1)S(1)}, bf16[64,512]{1,0:T(8,128)(2,1)S(1)}, u32[]{:S(2)}, u32[]{:S(2)}) collective-permute-start(bf16[64,512]{1,0:T(8,128)(2,1)S(1)} %bitcast.64), channel_id=1, source_target_pairs={{6,8},{14,16},{22,24},{30,32},{38,40},{46,48},{54,56},{62,64},{70,... | collective-permute-start | bytes 196616 | tf_op jit(solution)/shard_map/ppermute | solution.py:272
  22.4 57.6 %all-to-all-start.2 = ((f32[32,1,128]{2,1,0:T(1,128)}), f32[32,1,128]{2,1,0:T(1,128)S(1)}, u32[]{:S(2)}, u32[]{:S(2)}) async-start(f32[32,1,128]{2,1,0:T(1,128)} %broadcast_in_dim.27), calls=%async_computation.2 | async-start | bytes 32768 | tf_op jit(solution)/shard_map/all_to_all | solution.py:22
  72.9 11.8 %copy-start.2 = (f32[512]{0:T(512)S(1)}, f32[512]{0:T(512)}, u32[]{:S(2)}) copy-start(f32[512]{0:T(512)} %param.12) | copy-start | bytes 6148
  72.9 12.1 %copy-start.3 = (f32[512]{0:T(512)S(1)}, f32[512]{0:T(512)}, u32[]{:S(2)}) copy-start(f32[512]{0:T(512)} %param.13) | copy-start | bytes 6148
  73.3 62.4 %copy-start.4 = (f32[512]{0:T(512)S(1)}, f32[512]{0:T(512)}, u32[]{:S(2)}) copy-start(f32[512]{0:T(512)} %param.16) | copy-start | bytes 6148
  73.3 62.5 %copy-start.5 = (f32[512]{0:T(512)S(1)}, f32[512]{0:T(512)}, u32[]{:S(2)}) copy-start(f32[512]{0:T(512)} %param.17) | copy-start | bytes 6148
  73.3 62.7 %copy-start.6 = (f32[512]{0:T(512)S(1)}, f32[512]{0:T(512)}, u32[]{:S(2)}) copy-start(f32[512]{0:T(512)} %param.15) | copy-start | bytes 6148
  73.3 62.8 %copy-start.7 = (f32[512]{0:T(512)S(1)}, f32[512]{0:T(512)}, u32[]{:S(2)}) copy-start(f32[512]{0:T(512)} %param.19) | copy-start | bytes 6148
  73.3 63.5 %copy-start.8 = (f32[512]{0:T(512)S(1)}, f32[512]{0:T(512)}, u32[]{:S(2)}) copy-start(f32[512]{0:T(512)} %param.21) | copy-start | bytes 6148
  80.7 44.6 %all-to-all-start = ((bf16[8,2,64,128]{3,2,1,0:T(8,128)(2,1)}), bf16[8,2,64,128]{3,2,1,0:T(8,128)(2,1)S(1)}, u32[]{:S(2)}, u32[]{:S(2)}) async-start(bf16[8,2,64,128]{3,2,1,0:T(8,128)(2,1)} %bitcast.4), calls=%async_computation | async-start | bytes 524288 | tf_op jit(solution)/shard_map/all_to_all | solution.py:277
  127.1 16.3 %all-to-all-start.3 = ((bf16[4,128,256]{2,1,0:T(8,128)(2,1)}), bf16[4,128,256]{2,1,0:T(8,128)(2,1)S(1)}, u32[]{:S(2)}, u32[]{:S(2)}) async-start(bf16[4,128,256]{2,1,0:T(8,128)(2,1)} %conv_one.1), calls=%async_computation.3 | async-start | bytes 524288 | tf_op jit(solution)/shard_map/all_to_all | solution.py:312
  137.0 7.1 %collective-permute-start.1 = (bf16[64,512]{1,0:T(8,128)(2,1)S(1)}, bf16[64,512]{1,0:T(8,128)(2,1)S(1)}, u32[]{:S(2)}, u32[]{:S(2)}) collective-permute-start(bf16[64,512]{1,0:T(8,128)(2,1)S(1)} %bitcast.66), channel_id=1, source_target_pairs={{0,2},{2,4},{4,6},{6,8},{8,10},{10,12},{12,14},{14,16},{16,18},{18... | collective-permute-start | bytes 196616 | tf_op jit(solution)/shard_map/ppermute | solution.py:28
  141.1 6.7 %collective-permute-start.2 = (bf16[64,512]{1,0:T(8,128)(2,1)S(1)}, bf16[64,512]{1,0:T(8,128)(2,1)S(1)}, u32[]{:S(2)}, u32[]{:S(2)}) collective-permute-start(bf16[64,512]{1,0:T(8,128)(2,1)S(1)} %bitcast.67), channel_id=1, source_target_pairs={{2,0},{4,2},{6,4},{8,6},{10,8},{12,10},{14,12},{16,14},{18,16},{20... | collective-permute-start | bytes 196616 | tf_op jit(solution)/shard_map/ppermute | solution.py:28
  148.4 17.0 %all-to-all-start.4 = ((f32[32,1,128]{2,1,0:T(1,128)}), f32[32,1,128]{2,1,0:T(1,128)S(1)}, u32[]{:S(2)}, u32[]{:S(2)}) async-start(f32[32,1,128]{2,1,0:T(1,128)} %broadcast_in_dim.58), calls=%async_computation.4 | async-start | bytes 32768 | tf_op jit(solution)/shard_map/all_to_all | solution.py:22
  165.5 20.4 %collective-permute-start.3 = (bf16[2,128,256]{2,1,0:T(8,128)(2,1)S(1)}, bf16[2,128,256]{2,1,0:T(8,128)(2,1)S(1)}, u32[]{:S(2)}, u32[]{:S(2)}) collective-permute-start(bf16[2,128,256]{2,1,0:T(8,128)(2,1)S(1)} %bitcast.52), channel_id=1, source_target_pairs={{0,2},{2,4},{4,6},{6,8},{8,10},{10,12},{12,14},{14,16},{16,18},{18... | collective-permute-start | bytes 393224 | tf_op jit(solution)/shard_map/ppermute | solution.py:334
  166.8 19.1 %collective-permute-start.4 = (bf16[2,128,256]{2,1,0:T(8,128)(2,1)S(1)}, bf16[2,128,256]{2,1,0:T(8,128)(2,1)S(1)}, u32[]{:S(2)}, u32[]{:S(2)}) collective-permute-start(bf16[2,128,256]{2,1,0:T(8,128)(2,1)S(1)} %bitcast.53), channel_id=1, source_target_pairs={{0,4},{2,6},{4,8},{6,10},{8,12},{10,14},{12,16},{14,18},{16,20},{1... | collective-permute-start | bytes 393224 | tf_op jit(solution)/shard_map/ppermute | solution.py:334
  169.5 37.3 %all-to-all-start.5 = ((f32[8,1,128]{2,1,0:T(1,128)}), f32[8,1,128]{2,1,0:T(1,128)S(1)}, u32[]{:S(2)}, u32[]{:S(2)}) async-start(f32[8,1,128]{2,1,0:T(1,128)} %broadcast_in_dim.60), calls=%async_computation.5 | async-start | bytes 8192 | tf_op jit(solution)/shard_map/all_to_all | solution.py:22
  207.9 5.9 %copy-start = (bf16[32,18,16,256]{3,2,1,0:T(8,128)(2,1)S(1)}, bf16[32,18,16,256]{3,2,1,0:T(8,128)(2,1)}, u32[]{:S(2)}) copy-start(bf16[32,18,16,256]{3,2,1,0:T(8,128)(2,1)} %all-gather.6.cloned.1.call-done.w_ref) | copy-start | bytes 14155780
  214.7 3.3 %collective-permute-start.5 = (bf16[2,128,256]{2,1,0:T(8,128)(2,1)S(1)}, bf16[2,128,256]{2,1,0:T(8,128)(2,1)S(1)}, u32[]{:S(2)}, u32[]{:S(2)}) collective-permute-start(bf16[2,128,256]{2,1,0:T(8,128)(2,1)S(1)} %get-tuple-element.28), channel_id=1, source_target_pairs={{0,1},{1,0},{2,3},{3,2},{4,5},{5,4},{6,7},{7,6},{8,9},{9,8},{10,11... | collective-permute-start | bytes 393224 | tf_op jit(solution)/shard_map/ppermute | solution.py:372
Sparse Core Ops, SparseCore 0:
  20.7 166.3 all-gather.5
